TPU v7x, 32 devices: a whole 2x2x4 slice. The times are simulated.
32 devices in a mesh: rep: 16 (over z, y, x), grp: 2 (over core).
Axes of the slice: x: 2, y: 2, z: 4, core: 2. Of those that a mesh axis runs over, the one named last changes fastest.
Arguments:
- tokens: bfloat16 [16384, 1600], P(('rep', 'grp')), may hold values from -6 to 6
- first_gain: bfloat16 [1600], P('grp'), may hold values from 0.099609375 to 1.8984375
- first_shift: bfloat16 [1600], P('grp'), may hold values from -3 to 3
- w_heads: bfloat16 [1600, 4800], P('grp'), may hold values from -1 to 1
- query_bias: bfloat16 [1600], P('grp'), may hold values from -3 to 3
- value_bias: bfloat16 [1600], P('grp'), may hold values from -3 to 3
- w_project: bfloat16 [1600, 1600], P('grp'), may hold values from -0.4375 to 0.4375
- project_bias: bfloat16 [1600], P('grp'), may hold values from -3 to 3
- second_gain: bfloat16 [1600], P('grp'), may hold values from 0.099609375 to 1.8984375
- second_shift: bfloat16 [1600], P('grp'), may hold values from -3 to 3
- w_expand: bfloat16 [1600, 6400], P('grp'), may hold values from -0.15625 to 0.15625
- expand_bias: bfloat16 [6400], P('grp'), may hold values from -3 to 3
- w_contract: bfloat16 [6400, 1600], P('grp'), may hold values from -0.078125 to 0.078125
- contract_bias: bfloat16 [1600], P('grp'), may hold values from -3 to 3
- cotangent: bfloat16 [16384, 1600], P(('rep', 'grp')), may hold values from -6 to 6
Outputs:
- block_out: bfloat16 [16384, 1600], P(('rep', 'grp'))
- grad_tokens: bfloat16 [16384, 1600], P(('rep', 'grp'))
- grad_first_gain: float32 [1600], P('grp')
- grad_first_shift: float32 [1600], P('grp')
- grad_w_heads: float32 [1600, 4800], P('grp', 'rep')
- grad_query_bias: float32 [1600], P('grp')
- grad_value_bias: float32 [1600], P('grp')
- grad_w_project: float32 [1600, 1600], P('grp', 'rep')
- grad_project_bias: float32 [1600], P('grp')
- grad_second_gain: float32 [1600], P('grp')
- grad_second_shift: float32 [1600], P('grp')
- grad_w_expand: float32 [1600, 6400], P('grp', 'rep')
- grad_expand_bias: float32 [6400], P('grp')
- grad_w_contract: float32 [6400, 1600], P('grp', 'rep')
- grad_contract_bias: float32 [1600], P('grp')
All inputs are finite; a program needn't handle non-finite values.
Results may differ from a plain program's by a relative error of at most 0.013.
Values may be sent and summed in bfloat16 or wider, within the bound.
A program may use at most 576 MiB of HBM per device.

v0:
```python
import functools
import types

import jax
import jax.numpy as jnp
from jax import lax
from jax.experimental import pallas as pl
from jax.experimental.pallas import tpu as pltpu
from jax.sharding import PartitionSpec as P


HD = 64
LEN = 512
QB = 256
EPS = 1e-05
TANH_COEF = 0.7978845608028654
CUBIC = 0.044715
F32 = jnp.float32
BF16 = jnp.bfloat16
NT = (((1,), (1,)), ((), ()))
VMEM_LIMIT = 60 * 1024 * 1024


def shape_of(shape, dtype):
    return jax.ShapeDtypeStruct(shape, dtype)


def params():
    return pltpu.CompilerParams(vmem_limit_bytes=VMEM_LIMIT)


def cost(flops, moved):
    return pl.CostEstimate(flops=int(flops), bytes_accessed=int(moved), transcendentals=0)


def round_up(n, k):
    return -(-n // k) * k


def swap_group(x):
    return lax.ppermute(x, "grp", [(0, 1), (1, 0)])


def exchange(x, mask, count):
    return lax.ppermute(x, "rep", [(i, i ^ mask) for i in range(count)])


def row_sums(x):
    ones = jnp.ones((8, x.shape[1]), BF16)
    return lax.dot_general(ones, x, NT, preferred_element_type=F32)


def joined_dot(left_one, left_two, right_one, right_two):
    missing = left_one.shape[1] - right_one.shape[0]
    rights = [right_one, right_two]
    if missing:
        fill = jnp.zeros((missing, right_one.shape[1]), right_one.dtype)
        rights = [right_one, fill, right_two, fill]
    left = jnp.concatenate([left_one, left_two], axis=1)
    return jnp.dot(left, jnp.concatenate(rights, axis=0), preferred_element_type=F32)


def stream(step, steps, sources, buffers, sem):
    @pl.when(step == 0)
    def _():
        for i in range(steps):
            for j, (source, buffer) in enumerate(zip(sources, buffers)):
                pltpu.make_async_copy(source(i), buffer.at[i], sem.at[j, i]).start()

    for j, (source, buffer) in enumerate(zip(sources, buffers)):
        pltpu.make_async_copy(source(0), buffer.at[step], sem.at[j, step]).wait()


ANYWHERE = pl.BlockSpec(memory_space=pl.ANY)


def store_pair(side, value, own_ref, away_ref):
    half = value.shape[1] // 2
    fill = jnp.zeros((value.shape[0], own_ref.shape[1] - half), value.dtype)
    low = jnp.concatenate([value[:, :half], fill], axis=1)
    high = jnp.concatenate([value[:, half:], fill], axis=1)

    @pl.when(side == 0)
    def _():
        own_ref[...] = low
        away_ref[...] = high

    @pl.when(side == 1)
    def _():
        own_ref[...] = high
        away_ref[...] = low


def gather_kernel(*refs):
    out = refs[-1]
    out[...] = jnp.zeros_like(out)
    for i, ref in enumerate(refs[:-1]):
        out[i : i + 1, : ref.shape[0]] = ref[...].astype(F32).reshape(1, ref.shape[0])


def gather_smalls(smalls):
    widest = max(x.shape[0] for x in smalls)
    return pl.pallas_call(gather_kernel, out_shape=shape_of((16, widest), F32), name="gather")(*smalls)


def unpack_kernel(side_ref, own_ref, away_ref, rows_ref, cols_ref, packed_ref):
    half = rows_ref.shape[1] // 2
    first = side_ref[0] == 0
    own, away = own_ref[0:8, :half], away_ref[0:8, :half]
    low = jnp.where(first, own, away)
    high = jnp.where(first, away, own)
    rows = jnp.concatenate([low, high], axis=1)
    rows_ref[...] = rows
    cols_ref[...] = jnp.concatenate([rows, jnp.zeros((120, 2 * half), F32)], axis=0).T
    packed_ref[...] = jnp.concatenate([rows[2:3], jnp.zeros((1, 2 * half), F32), rows[3:4]], axis=1)


def unpack_smalls(side, own, away, width):
    vmem = pl.BlockSpec(memory_space=pltpu.VMEM)
    return pl.pallas_call(
        unpack_kernel,
        in_specs=[pl.BlockSpec(memory_space=pltpu.SMEM), vmem, vmem],
        out_shape=[shape_of((8, width), F32), shape_of((width, 128), F32), shape_of((1, 3 * width), F32)],
        name="unpack",
    )(side, own, away)


def collect_kernel(side_ref, pack_ref, eb_ref, *refs):
    rows, (mine_ref, theirs_ref) = refs[:-2], refs[-2:]
    width = rows[0].shape[1]
    half = width // 2
    first = side_ref[0] == 0
    pack = pack_ref[0:1, :]
    full = [r[0:1, :] for r in rows[:2]] + [pack[:, :width], pack[:, 2 * width :]]
    full += [r[0:1, :] for r in rows[2:]]
    full = jnp.concatenate(full, axis=0)
    low, high = full[:, :half], full[:, half:]
    mine_ref[...] = jnp.zeros_like(mine_ref)
    theirs_ref[...] = jnp.zeros_like(theirs_ref)
    mine_ref[0:8, :half] = jnp.where(first, low, high)
    theirs_ref[0:8, :half] = jnp.where(first, high, low)
    units = mine_ref.shape[1]
    low, high = eb_ref[0:1, :units], eb_ref[0:1, units:]
    mine_ref[8:9, :] = jnp.where(first, low, high)
    theirs_ref[8:9, :] = jnp.where(first, high, low)


def collect(side, pack, eb, rows):
    vmem = pl.BlockSpec(memory_space=pltpu.VMEM)
    out = shape_of((16, eb.shape[1] // 2), F32)
    return pl.pallas_call(
        collect_kernel,
        in_specs=[pl.BlockSpec(memory_space=pltpu.SMEM)] + [vmem] * (2 + len(rows)),
        out_shape=[out, out],
        name="collect",
    )(side, pack, eb, *rows)


def add_kernel(a_ref, b_ref, out_ref):
    out_ref[...] = a_ref[...] + b_ref[...]


def add(a, b):
    return pl.pallas_call(add_kernel, out_shape=shape_of(a.shape, a.dtype), name="add")(a, b)


def divide_kernel(a_ref, b_ref, *outs):
    total = a_ref[...] + b_ref[...]
    for i, out in enumerate(outs):
        out[...] = total[i : i + 1, : out.shape[0]].reshape(out.shape[0])


def divide(a, b, sizes):
    return pl.pallas_call(
        divide_kernel, out_shape=[shape_of((n,), F32) for n in sizes], name="divide"
    )(a, b)


def prep_kernel(side_ref, x_ref, c_ref, cols_ref, own_ref, away_ref, cot_ref, sum_ref, act_ref):
    x = x_ref[...].astype(F32)
    half = x.shape[0] // 2
    side = side_ref[0]
    centred = x - jnp.mean(x, axis=0, keepdims=True)
    inverse = lax.rsqrt(jnp.mean(centred * centred, axis=0, keepdims=True) + EPS)
    act_ref[...] = (centred * inverse * cols_ref[:, 0:1] + cols_ref[:, 1:2]).astype(BF16)
    for ref, which in ((own_ref, side), (away_ref, 1 - side)):
        ref[:, :half] = act_ref[pl.ds(pl.multiple_of(which * half, 16), half), :].T
        ref[:, half:] = jnp.zeros((ref.shape[0], ref.shape[1] - half), BF16)
    cot = c_ref[...].T
    cot_ref[...] = cot
    part = jnp.sum(cot.astype(F32), axis=0, keepdims=True)
    part = jnp.broadcast_to(part, sum_ref.shape)

    @pl.when(pl.program_id(0) == 0)
    def _():
        sum_ref[...] = part

    @pl.when(pl.program_id(0) > 0)
    def _():
        sum_ref[...] += part


def prep(side, tok_t, cot_t, cols):
    width, rows = tok_t.shape
    block = min(256, rows)
    half = round_up(width // 2, 128)
    nat = pl.BlockSpec((block, width), lambda i, *_: (i, 0))
    turned = pl.BlockSpec((width, block), lambda i, *_: (0, i))
    pair = pl.BlockSpec((block, half), lambda i, *_: (i, 0))
    return pl.pallas_call(
        prep_kernel,
        grid_spec=pltpu.PrefetchScalarGridSpec(
            num_scalar_prefetch=1,
            grid=(rows // block,),
            in_specs=[turned, turned, pl.BlockSpec((width, 128), lambda i, *_: (0, 0))],
            out_specs=[pair, pair, nat, pl.BlockSpec((8, width), lambda i, *_: (0, 0))],
            scratch_shapes=[pltpu.VMEM((width, block), BF16)],
        ),
        out_shape=[
            shape_of((rows, half), BF16),
            shape_of((rows, half), BF16),
            shape_of((rows, width), BF16),
            shape_of((8, width), F32),
        ],
        compiler_params=params(),
        cost_estimate=cost(0, 8 * rows * width),
        name="prep",
    )(side, tok_t, cot_t, cols)


def heads_kernel(own_ref, away_ref, wo_ref, wa_ref, bias_ref, out_ref):
    total = joined_dot(own_ref[...], away_ref[...], wo_ref[...], wa_ref[...])
    out_ref[...] = (total + bias_ref[...]).astype(BF16)


def heads_project(own, away, w_own, w_away, bias):
    rows, wide = own.shape
    half, columns = w_own.shape
    tile = 1280
    left = pl.BlockSpec((rows, wide), lambda i: (0, 0))
    right = pl.BlockSpec((half, tile), lambda i: (0, i))
    return pl.pallas_call(
        heads_kernel,
        grid=(pl.cdiv(columns, tile),),
        in_specs=[left, left, right, right, pl.BlockSpec((1, tile), lambda i: (0, i))],
        out_specs=pl.BlockSpec((rows, tile), lambda i: (0, i)),
        out_shape=shape_of((rows, columns), BF16),
        compiler_params=params(),
        cost_estimate=cost(4 * rows * half * columns, 4 * half * columns + 2 * rows * columns),
        name="heads",
    )(own, away, w_own, w_away, bias)


def lane_ids(shape):
    return lax.broadcasted_iota(jnp.int32, shape, len(shape) - 1)


def pair_of(left, right):
    return jnp.concatenate([left[:, HD:], right[:, :HD]], axis=1)


def causal_fill(scores, fill):
    rows, cols = scores.shape
    shift = cols - rows
    keep = lax.broadcasted_iota(jnp.int32, (rows, rows), 0) >= lax.broadcasted_iota(
        jnp.int32, (rows, rows), 1
    )
    diag = jnp.where(keep, scores[:, shift:], fill)
    return diag if shift == 0 else jnp.concatenate([scores[:, :shift], diag], axis=1)


def attend_kernel(q_ref, ka_ref, kb_ref, v_ref, o_ref, lse_ref):
    p = pl.program_id(1)
    lanes = lane_ids((LEN, 2 * HD))
    q = q_ref[...] * BF16(HD**-0.5)
    k = pair_of(ka_ref[...], kb_ref[...])
    v = jnp.concatenate([v_ref[...], jnp.ones((LEN, 2 * HD), BF16)], axis=1)
    for at in range(0, LEN, QB):
        end = at + QB
        low = lanes[at:end] < HD
        parts = []
        for h in range(2):
            qh = jnp.where(low == (h == 0), q[at:end], BF16(0))
            s = lax.dot_general(qh, k[:end], NT, preferred_element_type=F32)
            s = causal_fill(s, -jnp.inf)
            m = jnp.max(s, axis=1, keepdims=True)
            e = jnp.exp(s - m)
            both = jnp.dot(e.astype(BF16), v[:end], preferred_element_type=F32)
            parts.append((m, both[:, : 2 * HD], both[:, 2 * HD :]))
        out = jnp.where(low, parts[0][1], parts[1][1])
        sums = jnp.where(low, parts[0][2], parts[1][2])
        o_ref[at:end, :] = (out / sums).astype(BF16)
        ln = lanes[at:end]
        for h in range(2):
            value = parts[h][0] + jnp.log(parts[h][2])
            lse_ref[at:end, :] = jnp.where(ln == 2 * p + h, value, lse_ref[at:end, :])


def attend(packed):
    rows = packed.shape[0]
    width = packed.shape[1] // 3
    seqs = rows // LEN
    pairs = pl.cdiv(width, 2 * HD)
    kb, vb = width // (2 * HD), 2 * width // (2 * HD)

    def blk(f):
        return pl.BlockSpec((LEN, 2 * HD), f)

    return pl.pallas_call(
        attend_kernel,
        grid=(seqs, pairs),
        in_specs=[
            blk(lambda s, p: (s, p)),
            blk(lambda s, p: (s, p + kb)),
            blk(lambda s, p: (s, p + kb + 1)),
            blk(lambda s, p: (s, p + vb)),
        ],
        out_specs=[blk(lambda s, p: (s, p)), blk(lambda s, p: (s, 0))],
        out_shape=[shape_of((rows, width), BF16), shape_of((rows, 2 * HD), F32)],
        cost_estimate=cost(rows * LEN * width * 12, 8 * rows * width),
        name="attend",
    )(packed, packed, packed, packed)


def attend_back_kernel(width, q_ref, ka_ref, kb_ref, v_ref, do_ref, o_ref, lse_ref, out_ref, dq_ref):
    p = pl.program_id(1)
    lanes = lane_ids((LEN, 2 * HD))
    low = lanes < HD
    q = q_ref[...] * BF16(HD**-0.5)
    k = pair_of(ka_ref[...], kb_ref[...])
    real = lanes + 2 * HD * p < width
    v = jnp.where(real, v_ref[...], BF16(0))
    dot_t = do_ref[...]
    do = jnp.where(real, dot_t.T, BF16(0))
    o = jnp.where(real, o_ref[...], BF16(0))
    prod = do.astype(F32) * o.astype(F32)
    lse = lse_ref[...]
    q_t = q.T
    for h in range(2):
        mine = low if h == 0 else jnp.logical_not(low)
        qh = jnp.where(mine, q, BF16(0))
        doh = jnp.where(mine, do, BF16(0))
        delta = jnp.sum(jnp.where(mine, prod, 0.0), axis=1, keepdims=True)
        norm = jnp.sum(jnp.where(lanes == 2 * p + h, lse, 0.0), axis=1, keepdims=True)
        rows = slice(h * HD, (h + 1) * HD)
        dk = None
        for at in range(LEN - QB, -1, -QB):
            end = at + QB
            s = lax.dot_general(qh[at:end], k[:end], NT, preferred_element_type=F32)
            w = causal_fill(jnp.exp(s - norm[at:end]), 0.0)
            wb = w.astype(BF16)
            dp = lax.dot_general(doh[at:end], v[:end], NT, preferred_element_type=F32)
            ds = (w * (dp - delta[at:end])).astype(BF16)
            dq = jnp.dot(ds, k[:end], preferred_element_type=F32) * HD**-0.5
            if h == 0:
                dq_ref[at:end, :] = dq.astype(BF16)
            else:
                dq_ref[at:end, :] = jnp.where(low[at:end], dq_ref[at:end, :], dq.astype(BF16))
            dk_part = jnp.dot(q_t[rows, at:end], ds, preferred_element_type=F32)
            dv_part = jnp.dot(dot_t[rows, at:end], wb, preferred_element_type=F32)
            if dk is None:
                dk, dv = dk_part, dv_part
            else:
                dk = jnp.concatenate([dk[:, :end] + dk_part, dk[:, end:]], axis=1)
                dv = jnp.concatenate([dv[:, :end] + dv_part, dv[:, end:]], axis=1)
        out_ref[1, rows, :] = dk.astype(BF16)
        out_ref[2, rows, :] = dv.astype(BF16)
    out_ref[0, :, :] = dq_ref[...].T


def attend_back(packed, grad_t, attended, lse):
    rows = packed.shape[0]
    width = packed.shape[1] // 3
    seqs = rows // LEN
    pairs = pl.cdiv(width, 2 * HD)
    kb, vb = width // (2 * HD), 2 * width // (2 * HD)

    def blk(f):
        return pl.BlockSpec((LEN, 2 * HD), f)

    out = pl.pallas_call(
        functools.partial(attend_back_kernel, width),
        grid=(seqs, pairs),
        in_specs=[
            blk(lambda s, p: (s, p)),
            blk(lambda s, p: (s, p + kb)),
            blk(lambda s, p: (s, p + kb + 1)),
            blk(lambda s, p: (s, p + vb)),
            pl.BlockSpec((2 * HD, LEN), lambda s, p: (p, s)),
            blk(lambda s, p: (s, p)),
            blk(lambda s, p: (s, 0)),
        ],
        out_specs=pl.BlockSpec((3, 2 * HD, LEN), lambda s, p: (0, p, s)),
        out_shape=shape_of((3, width, rows), BF16),
        scratch_shapes=[pltpu.VMEM((LEN, 2 * HD), BF16)],
        cost_estimate=cost(rows * LEN * width * 12, 14 * rows * width),
        name="aback",
    )(packed, packed, packed, packed, grad_t, attended, lse)
    return out.reshape(3 * width, rows)


def project_kernel(
    side_ref, att_ref, x_ref, wo_ref, wa_ref, rows_ref,
    ao_ref, aa_ref, mid_ref, so_ref, sa_ref, n_ref, inv_ref,
):
    side = side_ref[0]
    store_pair(side, att_ref[...], ao_ref, aa_ref)
    mid = joined_dot(ao_ref[...], aa_ref[...], wo_ref[...], wa_ref[...])
    mid += x_ref[...].T.astype(F32) + rows_ref[4:5, :]
    mid_ref[...] = mid.T
    centred = mid - jnp.mean(mid, axis=1, keepdims=True)
    inverse = lax.rsqrt(jnp.mean(centred * centred, axis=1, keepdims=True) + EPS)
    normed = centred * inverse
    act = (normed * rows_ref[5:6, :] + rows_ref[6:7, :]).astype(BF16)
    store_pair(side, act, so_ref, sa_ref)
    n_ref[...] = normed.astype(BF16).T
    inv_ref[...] = jnp.broadcast_to(inverse, (inverse.shape[0], 128)).T[:8]


def project(side, attended, tok_t, w_own, w_away, small_rows):
    width, rows = tok_t.shape
    half = width // 2
    wide = round_up(half, 128)
    block = min(256, rows)
    nat = pl.BlockSpec((block, width), lambda i, *_: (i, 0))
    pair = pl.BlockSpec((block, wide), lambda i, *_: (i, 0))
    whole = pl.BlockSpec((half, width), lambda i, *_: (0, 0))
    turned = pl.BlockSpec((width, block), lambda i, *_: (0, i))
    return pl.pallas_call(
        project_kernel,
        grid_spec=pltpu.PrefetchScalarGridSpec(
            num_scalar_prefetch=1,
            grid=(rows // block,),
            in_specs=[nat, turned, whole, whole, pl.BlockSpec((8, width), lambda i, *_: (0, 0))],
            out_specs=[
                pair, pair, turned, pair, pair, turned,
                pl.BlockSpec((8, block), lambda i, *_: (0, i)),
            ],
        ),
        out_shape=[
            shape_of((rows, wide), BF16),
            shape_of((rows, wide), BF16),
            shape_of((width, rows), F32),
            shape_of((rows, wide), BF16),
            shape_of((rows, wide), BF16),
            shape_of((width, rows), BF16),
            shape_of((8, rows), F32),
        ],
        compiler_params=params(),
        cost_estimate=cost(4 * rows * half * width, 4 * half * width + 14 * rows * width),
        name="project",
    )(side, attended, tok_t, w_own, w_away, small_rows)


def hidden_kernel(start_ref, so_ref, sa_ref, wo_ref, wa_ref, bias_ref, act_ref, slope_ref):
    rows = so_ref.shape[0] // 2
    wo, wa = wo_ref[...], wa_ref[...]
    for at in range(0, so_ref.shape[0], rows):
        part = slice(at, at + rows)
        v = joined_dot(so_ref[part, :], sa_ref[part, :], wo, wa)
        v += bias_ref[8:9, :]
        square = v * v
        t = jnp.tanh(TANH_COEF * v * (1.0 + CUBIC * square))
        grown = 0.5 * (1.0 + t)
        act_ref[part, :] = (v * grown).astype(BF16)
        slope = grown * (1.0 + v * (1.0 - t) * (TANH_COEF + 3.0 * TANH_COEF * CUBIC * square))
        slope_ref[part, :] = slope.astype(BF16)


def hidden(start, own, away, w_own, w_away, bias, units):
    rows, wide = own.shape
    half = w_own.shape[0]
    tile = 640
    resident = pl.BlockSpec((rows, wide), lambda i, s: (0, 0))
    right = pl.BlockSpec((half, tile), lambda i, s: (0, s[0] + i))
    out = pl.BlockSpec((rows, tile), lambda i, s: (0, i))
    return pl.pallas_call(
        hidden_kernel,
        grid_spec=pltpu.PrefetchScalarGridSpec(
            num_scalar_prefetch=1,
            grid=(units // tile,),
            in_specs=[resident, resident, right, right, pl.BlockSpec((16, tile), lambda i, s: (0, i))],
            out_specs=[out, out],
        ),
        out_shape=[shape_of((rows, units), BF16)] * 2,
        compiler_params=params(),
        cost_estimate=cost(4 * rows * units * half, 4 * units * half + 4 * rows * units),
        name="hidden",
    )(start, own, away, w_own, w_away, bias)


def hidden_back_kernel(meta_ref, cot_ref, w1_ref, w2_ref, s1_ref, s2_ref, ge_ref, sum_ref):
    def part(w_ref, slope_ref):
        ge = jnp.dot(cot_ref[...], w_ref[...], preferred_element_type=F32) * slope_ref[...].astype(F32)
        ge_ref[...] = ge.astype(BF16).T
        sum_ref[...] = jnp.broadcast_to(jnp.sum(ge, axis=0, keepdims=True), sum_ref.shape)

    first = pl.program_id(0) < pl.num_programs(0) // 2
    pl.when(first)(lambda: part(w1_ref, s1_ref))
    pl.when(jnp.logical_not(first))(lambda: part(w2_ref, s2_ref))


def hidden_back(meta, cot, w_first_t, w_second_t, slope_first, slope_second):
    width, units = w_first_t.shape
    rows = cot.shape[0]
    tile = 640
    steps = units // tile
    first = lambda i: jnp.minimum(i, steps - 1)
    second = lambda i: jnp.maximum(i - steps, 0)
    place = lambda i, m: jnp.where(i < steps, (1 - m[0]) * steps + i, m[0] * steps + i - steps)
    return pl.pallas_call(
        hidden_back_kernel,
        grid_spec=pltpu.PrefetchScalarGridSpec(
            num_scalar_prefetch=1,
            grid=(2 * steps,),
            in_specs=[
                pl.BlockSpec((rows, width), lambda i, m: (0, 0)),
                pl.BlockSpec((width, tile), lambda i, m: (0, first(i))),
                pl.BlockSpec((width, tile), lambda i, m: (0, second(i))),
                pl.BlockSpec((rows, tile), lambda i, m: (0, first(i))),
                pl.BlockSpec((rows, tile), lambda i, m: (0, second(i))),
            ],
            out_specs=[
                pl.BlockSpec((tile, rows), lambda i, m: (place(i, m), 0)),
                pl.BlockSpec((8, tile), lambda i, m: (0, place(i, m))),
            ],
        ),
        out_shape=[shape_of((2 * units, rows), BF16), shape_of((8, 2 * units), F32)],
        compiler_params=params(),
        cost_estimate=cost(4 * rows * units * width, 4 * units * width + 8 * rows * units),
        name="hback",
    )(meta, cot, w_first_t, w_second_t, slope_first, slope_second)


ROWS = 160


def middle_kernel(
    meta_ref, g_ref, wo_hbm, wa_hbm, n_hbm, inv_ref, gain_ref, cot_hbm, po_hbm, pa_hbm,
    gm_ref, gmb_ref, ga_ref, s_gain_ref, s_shift_ref, s_bias_ref,
    acc_ref, prod_ref, wo_buf, wa_buf, n_ref, cot_ref, po_ref, pa_ref, sem, sem_late,
):
    side = meta_ref[0]
    width = acc_ref.shape[0]
    half = width // 2
    i = pl.program_id(0)
    steps, tile, _ = wo_buf.shape
    rows = lambda ref: lambda i: ref.at[pl.ds(i * tile, tile), :]
    stream(i, steps, (rows(wo_hbm), rows(wa_hbm)), (wo_buf, wa_buf), sem)
    late = [
        pltpu.make_async_copy(src, dst, sem_late.at[j])
        for j, (src, dst) in enumerate(
            ((n_hbm, n_ref), (cot_hbm, cot_ref), (po_hbm, po_ref), (pa_hbm, pa_ref))
        )
    ]

    @pl.when(i == 0)
    def _():
        for c in late:
            c.start()

    left = jnp.concatenate([wo_buf[i], wa_buf[i]], axis=0)
    total = jnp.dot(left, g_ref[...], preferred_element_type=F32)
    acc_ref[pl.ds(pl.multiple_of(side * half + i * tile, 8), tile), :] = total[:tile]
    acc_ref[pl.ds(pl.multiple_of((1 - side) * half + i * tile, 8), tile), :] = total[tile:]

    @pl.when(i == steps - 1)
    def _():
        for c in late:
            c.wait()
        tokens = acc_ref.shape[1]
        inverse = inv_ref[0:1, :]

        def first(j, sums):
            at = pl.ds(j * ROWS, ROWS)
            e, n = acc_ref[at, :], n_ref[at, :].astype(F32)
            w = e * gain_ref[at, 5:6]
            gmb_ref[at, :] = e.astype(BF16)
            prod_ref[at, :] = (e * n).astype(BF16)
            return (
                sums[0] + jnp.sum(w, axis=0, keepdims=True),
                sums[1] + jnp.sum(w * n, axis=0, keepdims=True),
            )

        zero = jnp.zeros((1, tokens), F32)
        one, two = lax.fori_loop(0, width // ROWS, first, (zero, zero))
        one, two = one / width, two / width
        s_gain_ref[...] = row_sums(prod_ref[...])
        s_shift_ref[...] = row_sums(gmb_ref[...])

        def second(j, _):
            at = pl.ds(j * ROWS, ROWS)
            n = n_ref[at, :].astype(F32)
            back = inverse * (acc_ref[at, :] * gain_ref[at, 5:6] - one - n * two)
            g = cot_ref[at, :].astype(F32) + back
            gm_ref[at, :] = g
            gmb_ref[at, :] = g.astype(BF16)
            return 0

        lax.fori_loop(0, width // ROWS, second, 0)
        g = gmb_ref[...]
        s_bias_ref[...] = row_sums(g)
        for which, p_ref in ((side, po_ref), (1 - side, pa_ref)):
            ga_ref[pl.ds(pl.multiple_of(which * half, 16), half), :] = jnp.dot(
                p_ref[...], g, preferred_element_type=F32
            ).astype(BF16)


def middle_back(meta, ge, w_own, w_away, normed_t, inv_t, cols, cot_t, p_own, p_away):
    units, rows = ge.shape
    half = w_own.shape[0]
    width = 2 * half
    tile = 200
    steps = half // tile
    once = pl.Buffered(1)
    const = lambda shape: pl.BlockSpec(shape, lambda i, m: (0, 0), pipeline_mode=once)
    out = lambda shape: pl.BlockSpec(shape, lambda i, m: (0, 0))
    small = shape_of((8, width), F32)
    return pl.pallas_call(
        middle_kernel,
        grid_spec=pltpu.PrefetchScalarGridSpec(
            num_scalar_prefetch=1,
            grid=(steps,),
            in_specs=[
                const((units, rows)), ANYWHERE, ANYWHERE, ANYWHERE,
                const((8, rows)), const((width, 128)), ANYWHERE, ANYWHERE, ANYWHERE,
            ],
            out_specs=[out((width, rows))] * 3 + [out((8, width))] * 3,
            scratch_shapes=[
                pltpu.VMEM((width, rows), F32),
                pltpu.VMEM((width, rows), BF16),
                pltpu.VMEM((steps, tile, units), BF16),
                pltpu.VMEM((steps, tile, units), BF16),
                pltpu.VMEM((width, rows), BF16),
                pltpu.VMEM((width, rows), BF16),
                pltpu.VMEM((half, width), BF16),
                pltpu.VMEM((half, width), BF16),
                pltpu.SemaphoreType.DMA((2, steps)),
                pltpu.SemaphoreType.DMA((4,)),
            ],
        ),
        out_shape=[
            shape_of((width, rows), F32),
            shape_of((width, rows), BF16),
            shape_of((width, rows), BF16),
            small, small, small,
        ],
        compiler_params=params(),
        cost_estimate=cost(
            2 * rows * units * width + 2 * rows * width * width, 2 * units * width + 12 * rows * width
        ),
        name="middle",
    )(meta, ge, w_own, w_away, normed_t, inv_t, cols, cot_t, p_own, p_away)


def first_kernel(
    meta_ref, gp_ref, wo_hbm, wa_hbm, tok_hbm, gain_ref, gm_hbm,
    out_ref, s_gain_ref, s_shift_ref, s_pack_ref,
    acc_ref, prod_ref, e_ref, wo_buf, wa_buf, tok_ref, gm_ref, sem, sem_late,
):
    side = meta_ref[0]
    width = acc_ref.shape[0]
    half = width // 2
    i = pl.program_id(0)
    steps, tile, _ = wo_buf.shape
    rows = lambda ref: lambda i: ref.at[pl.ds(i * tile, tile), :]
    stream(i, steps, (rows(wo_hbm), rows(wa_hbm)), (wo_buf, wa_buf), sem)
    late = [
        pltpu.make_async_copy(src, dst, sem_late.at[j])
        for j, (src, dst) in enumerate(((tok_hbm, tok_ref), (gm_hbm, gm_ref)))
    ]

    @pl.when(i == 0)
    def _():
        for c in late:
            c.start()

    g = gp_ref[...]
    total = jnp.dot(
        jnp.concatenate([wo_buf[i], wa_buf[i]], axis=0), g, preferred_element_type=F32
    )
    acc_ref[pl.ds(pl.multiple_of(side * half + i * tile, 8), tile), :] = total[:tile]
    acc_ref[pl.ds(pl.multiple_of((1 - side) * half + i * tile, 8), tile), :] = total[tile:]

    @pl.when(i == 0)
    def _():
        s_pack_ref[...] = row_sums(g)

    @pl.when(i == pl.num_programs(0) - 1)
    def _():
        for c in late:
            c.wait()
        tokens = acc_ref.shape[1]
        zero = jnp.zeros((1, tokens), F32)
        loops = width // ROWS

        def total(j, s):
            return s + jnp.sum(tok_ref[pl.ds(j * ROWS, ROWS), :].astype(F32), axis=0, keepdims=True)

        mean = lax.fori_loop(0, loops, total, zero) / width

        def spread_of(j, s):
            c = tok_ref[pl.ds(j * ROWS, ROWS), :].astype(F32) - mean
            return s + jnp.sum(c * c, axis=0, keepdims=True)

        inverse = lax.rsqrt(lax.fori_loop(0, loops, spread_of, zero) / width + EPS)

        def first(j, sums):
            at = pl.ds(j * ROWS, ROWS)
            e = acc_ref[at, :]
            n = (tok_ref[at, :].astype(F32) - mean) * inverse
            w = e * gain_ref[at, 0:1]
            e_ref[at, :] = e.astype(BF16)
            prod_ref[at, :] = (e * n).astype(BF16)
            return (
                sums[0] + jnp.sum(w, axis=0, keepdims=True),
                sums[1] + jnp.sum(w * n, axis=0, keepdims=True),
            )

        one, two = lax.fori_loop(0, loops, first, (zero, zero))
        one, two = one / width, two / width
        s_gain_ref[...] = row_sums(prod_ref[...])
        s_shift_ref[...] = row_sums(e_ref[...])

        def second(j, _):
            at = pl.ds(j * ROWS, ROWS)
            n = (tok_ref[at, :].astype(F32) - mean) * inverse
            back = inverse * (acc_ref[at, :] * gain_ref[at, 0:1] - one - n * two)
            out_ref[at, :] = (gm_ref[at, :] + back).astype(BF16)
            return 0

        lax.fori_loop(0, loops, second, 0)


def first_back(meta, gp_t, w_own, w_away, tok_t, cols, gm_t):
    columns, rows = gp_t.shape
    half = w_own.shape[0]
    width = 2 * half
    tile = 200
    steps = half // tile
    const = lambda shape: pl.BlockSpec(shape, lambda i, m: (0, 0))
    return pl.pallas_call(
        first_kernel,
        grid_spec=pltpu.PrefetchScalarGridSpec(
            num_scalar_prefetch=1,
            grid=(steps,),
            in_specs=[
                const((columns, rows)), ANYWHERE, ANYWHERE, ANYWHERE, const((width, 128)), ANYWHERE,
            ],
            out_specs=[const((width, rows)), const((8, width)), const((8, width)), const((8, columns))],
            scratch_shapes=[
                pltpu.VMEM((width, rows), F32),
                pltpu.VMEM((width, rows), BF16),
                pltpu.VMEM((width, rows), BF16),
                pltpu.VMEM((steps, tile, columns), BF16),
                pltpu.VMEM((steps, tile, columns), BF16),
                pltpu.VMEM((width, rows), BF16),
                pltpu.VMEM((width, rows), F32),
                pltpu.SemaphoreType.DMA((2, steps)),
                pltpu.SemaphoreType.DMA((2,)),
            ],
        ),
        out_shape=[
            shape_of((width, rows), BF16),
            shape_of((8, width), F32),
            shape_of((8, width), F32),
            shape_of((8, columns), F32),
        ],
        compiler_params=params(),
        cost_estimate=cost(4 * rows * half * columns, 4 * half * columns + 2 * rows * columns + 10 * rows * width),
        name="first",
    )(meta, gp_t, w_own, w_away, tok_t, cols, gm_t)


def output_kernel(a1_ref, a2_ref, w1_hbm, w2_hbm, mid_ref, cols_ref, out_ref, w1_buf, w2_buf, sem):
    i = pl.program_id(0)
    steps, tile, _ = w1_buf.shape
    rows = lambda ref: lambda i: ref.at[pl.ds(i * tile, tile), :]
    stream(i, steps, (rows(w1_hbm), rows(w2_hbm)), (w1_buf, w2_buf), sem)
    weights = jnp.concatenate([w1_buf[i], w2_buf[i]], axis=1)
    acts = jnp.concatenate([a1_ref[...], a2_ref[...]], axis=1)
    total = lax.dot_general(weights, acts, NT, preferred_element_type=F32)
    out_ref[...] = (total + mid_ref[...] + cols_ref[:, 7:8]).astype(BF16)


def block_output(act_first, act_second, w_away_t, w_own_t, middle_t, cols):
    rows, units = act_first.shape
    width = w_own_t.shape[0]
    tile = 400
    left = pl.BlockSpec((rows, units), lambda i: (0, 0))
    steps = width // tile
    part = pl.BlockSpec((tile, rows), lambda i: (i, 0))
    return pl.pallas_call(
        output_kernel,
        grid=(width // tile,),
        in_specs=[left, left, ANYWHERE, ANYWHERE, part, pl.BlockSpec((tile, 128), lambda i: (i, 0))],
        out_specs=part,
        scratch_shapes=[pltpu.VMEM((steps, tile, units), BF16)] * 2 + [pltpu.SemaphoreType.DMA((2, steps))],
        out_shape=shape_of((width, rows), BF16),
        compiler_params=params(),
        cost_estimate=cost(4 * rows * units * width, 4 * units * width + 4 * rows * units + 6 * rows * width),
        name="output",
    )(act_first, act_second, w_away_t, w_own_t, middle_t, cols)


class Group:
    def __init__(self, count, lanes, chunks, plan):
        self.count, self.lanes, self.chunks = count, lanes, chunks
        shares, orders = plan
        bits = count.bit_length() - 1
        self.orders = [list(order) + list(range(len(order), bits)) for order in orders]
        tiles = lanes // 128
        one, two = (round(tiles * share) for share in shares)
        self.cuts = [0, one * 128, (one + two) * 128, tiles * 128]
        self.widths = [self.cuts[k + 1] - self.cuts[k] for k in range(3)]
        self.left_over = lanes % 128
        self.pieces = self.widths[2] // self.left_over if self.left_over else 0

    def padded(self, which):
        return round_up(self.chunks[which], 16)

    def each(self, which):
        return pl.cdiv(self.chunks[which], self.pieces)

    def packed(self, which):
        return round_up(self.each(which), 16) if self.left_over else 0

    def rows(self, k, which):
        return self.padded(which) + (self.packed(which) if k == 2 else 0)

    def base(self, k, which):
        return sum(self.rows(k, w) for w in range(which))

    def total_rows(self, k):
        return self.base(k, len(self.chunks))


SLOTS = 4


def spread_kernel(spec, meta_ref, lo_ref, la_ref, ro_ref, ra_ref, *refs):
    group, which, batch, n_into = spec
    refs = refs[n_into:]
    keeps, sends, stages, sem = refs[:3], refs[3:6], refs[6:9], refs[9]
    count, chunk = group.count, group.chunks[which]
    step, steps = pl.program_id(0), pl.num_programs(0)
    rank, first = meta_ref[0], meta_ref[1]
    padded = group.padded(which)
    half = count // 2

    def rows_of(k):
        return pl.ds(group.base(k, which), group.rows(k, which))

    def wait_slot(slot):
        for k in range(3):
            pltpu.make_async_copy(
                stages[k].at[slot], keeps[k].at[0, rows_of(k), :], sem.at[k, slot]
            ).wait()

    lanes = group.lanes
    total = joined_dot(lo_ref[...], la_ref[...], ro_ref[:, :lanes], ra_ref[:, :lanes])
    for s in range(batch):
        index = step * batch + s
        slot = s % SLOTS if batch % SLOTS == 0 else lax.rem(index, SLOTS)
        if s >= SLOTS:
            wait_slot(slot)
        else:
            pl.when(index >= SLOTS)(lambda slot=slot: wait_slot(slot))
        mixed = jnp.bitwise_xor(first + index, rank)
        part = total[s * chunk : (s + 1) * chunk]
        for k in range(3):
            low, width = group.cuts[k], group.widths[k]
            stages[k][slot, :chunk, :] = part[:, low : low + width].astype(BF16)
            if k == 2 and group.left_over:
                each, pieces = group.each(which), group.pieces
                extra = part[:, low + width :]
                if pieces * each > chunk:
                    extra = jnp.concatenate(
                        [extra, jnp.zeros((pieces * each - chunk, group.left_over), F32)], axis=0
                    )
                extra = jnp.concatenate([extra[j * each : (j + 1) * each] for j in range(pieces)], axis=1)
                stages[k][slot, padded : padded + each, :] = extra.astype(BF16)
            place = jnp.int32(0)
            order = group.orders[k]
            for depth, bit in enumerate(order):
                place += ((mixed >> bit) & 1) << (len(order) - 1 - depth)

            @pl.when(place < half)
            def _(k=k, slot=slot, place=place):
                pltpu.make_async_copy(
                    stages[k].at[slot], keeps[k].at[place, rows_of(k), :], sem.at[k, slot]
                ).start()

            @pl.when(place >= half)
            def _(k=k, slot=slot, place=place):
                pltpu.make_async_copy(
                    stages[k].at[slot], sends[k].at[place - half, rows_of(k), :], sem.at[k, slot]
                ).start()

    @pl.when(step == steps - 1)
    def _():
        for slot in range(SLOTS):
            wait_slot(slot)


def spread(group, which, meta, lefts, rights, into=None):
    left_own, left_away = lefts
    columns, tokens = left_own.shape
    count, chunk = group.count, group.chunks[which]
    batch = 1
    while batch * chunk % 16:
        batch *= 2
    outs = [shape_of((count // 2, group.total_rows(k), group.widths[k]), BF16) for k in range(3)] * 2
    extra = list(into) if into is not None else []
    spec = (group, which, batch, len(extra))
    anywhere = pl.BlockSpec(memory_space=pl.ANY)
    left = pl.BlockSpec((batch * chunk, tokens), lambda i, *_: (i, 0))
    whole = pl.BlockSpec(rights[0].shape, lambda i, *_: (0, 0))
    return pl.pallas_call(
        functools.partial(spread_kernel, spec),
        grid_spec=pltpu.PrefetchScalarGridSpec(
            num_scalar_prefetch=1,
            grid=(columns // (batch * chunk),),
            in_specs=[left, left, whole, whole] + [anywhere] * len(extra),
            out_specs=[anywhere] * len(outs),
            scratch_shapes=[
                pltpu.VMEM((SLOTS, group.rows(k, which), group.widths[k]), BF16) for k in range(3)
            ]
            + [pltpu.SemaphoreType.DMA((3, SLOTS))],
        ),
        out_shape=outs,
        input_output_aliases={5 + i: i for i in range(len(extra))},
        compiler_params=params(),
        cost_estimate=cost(
            4 * columns * tokens * group.lanes, 4 * columns * tokens + 2 * columns * group.lanes
        ),
        name="spread",
    )(meta, left_own, left_away, *rights, *extra)


def merge_kernel(*refs):
    for k in range(3):
        keep_low, came_low, keep_high, came_high = refs[4 * k : 4 * k + 4]
        keep, send = refs[12 + k], refs[15 + k]
        keep[...] = (keep_low[...].astype(F32) + came_low[...].astype(F32)).astype(BF16)
        send[...] = (keep_high[...].astype(F32) + came_high[...].astype(F32)).astype(BF16)


def merge(keeps, arrived):
    half = keeps[0].shape[0] // 2
    ins, specs, outs, out_specs = [], [], [], []
    moved = 0
    for keep, came in zip(keeps, arrived):
        shape = (1,) + keep.shape[1:]
        low = pl.BlockSpec(shape, lambda i: (i, 0, 0))
        high = pl.BlockSpec(shape, lambda i: (i + half, 0, 0))
        ins += [keep, came, keep, came]
        specs += [low, low, high, high]
        outs.append(shape_of((half,) + keep.shape[1:], BF16))
        out_specs.append(low)
        moved += 6 * keep.size
    return pl.pallas_call(
        merge_kernel,
        grid=(half,),
        in_specs=specs,
        out_specs=out_specs * 2,
        out_shape=outs * 2,
        compiler_params=params(),
        cost_estimate=cost(0, moved),
        name="merge",
    )(*ins)


def finish_kernel(group, *refs):
    outs = refs[6:]
    totals = [refs[2 * k][0].astype(F32) + refs[2 * k + 1][0].astype(F32) for k in range(3)]
    for which, chunk in enumerate(group.chunks):
        out = outs[which]
        for k in range(3):
            base = group.base(k, which)
            out[:, group.cuts[k] : group.cuts[k + 1]] = totals[k][base : base + chunk]
        width = group.left_over
        if width:
            base = group.base(2, which) + group.padded(which)
            rest = totals[2][base : base + group.each(which)]
            rest = jnp.concatenate([rest[:, j * width : (j + 1) * width] for j in range(group.pieces)], axis=0)
            out[:, group.cuts[3] :] = rest[:chunk]


def finish(group, keeps, arrived):
    ins = []
    for keep, came in zip(keeps, arrived):
        ins += [keep, came]
    res = pl.pallas_call(
        functools.partial(finish_kernel, group),
        out_shape=[shape_of((chunk, group.lanes), F32) for chunk in group.chunks],
        compiler_params=params(),
        cost_estimate=cost(0, 8 * sum(group.chunks) * group.lanes),
        name="finish",
    )(*ins)
    return [x.T for x in res]


ORDER = (
    "sc", "hb", "mid", "mc", "e", "p", "ab", "mc", "sh", "me", "mc", "first", "s", "mh", "s", "me",
    "mh", "s", "me", "out", "s", "mc", "s", "mh", "s", "me", "mh",
)

PLANS = (
    ((0.36, 0.36), ((0, 2, 1, 3), (1, 0, 2, 3), (2, 1, 0, 3))),
    ((0.33, 0.33), ((0, 1, 2, 3), (1, 2, 0, 3), (2, 0, 1, 3))),
    ((0.5, 0.33), ((0, 1, 2, 3), (1, 0, 2, 3), (2, 1, 0, 3))),
)


def all_steps(bits):
    steps = list(ORDER)
    for name in ("mc", "me", "mh"):
        steps += [name] * (bits - steps.count(name))
    return steps + ["s"] * (bits + 2 - steps.count("s"))


def solution(mesh):
    count = mesh.shape["rep"]
    assert mesh.shape["grp"] == 2
    bits = count.bit_length() - 1
    assert 1 << bits == count and bits >= 4

    def per_device(
        tokens,
        first_gain,
        first_shift,
        w_heads,
        query_bias,
        value_bias,
        w_project,
        project_bias,
        second_gain,
        second_shift,
        w_expand,
        expand_bias,
        w_contract,
        contract_bias,
        cotangent,
    ):
        width = tokens.shape[1]
        units = w_contract.shape[0]
        side = lax.axis_index("grp")
        rank = lax.axis_index("rep")
        sides = jnp.reshape(side, (1,))

        smalls = (
            first_gain,
            first_shift,
            query_bias,
            value_bias,
            project_bias,
            second_gain,
            second_shift,
            contract_bias,
            expand_bias,
        )
        tok_t, cot_t, contract_own = tokens.T, cotangent.T, w_contract.T
        own_small = gather_smalls(smalls)
        away_small = swap_group(own_small)
        heads_in, _ = lax.optimization_barrier((w_heads, away_small))
        heads_away = swap_group(heads_in)
        small_rows, cols, packed_row = unpack_smalls(sides, own_small, away_small, width)
        first_own, first_out, cot, cot_sum = prep(sides, tok_t, cot_t, cols)
        w_project_in, _ = lax.optimization_barrier((w_project, first_own))
        project_away = swap_group(w_project_in)
        packed = heads_project(first_own, first_out, w_heads, heads_away, packed_row)

        latest = [packed]


        def hold(x):
            return lax.optimization_barrier((x, latest[0]))[0]

        def held(out):
            latest[0] = jax.tree.leaves(out)[0]
            return out

        w_expand_in, _ = lax.optimization_barrier((hold(w_expand), project_away))
        expand_away = swap_group(w_expand_in)
        contract_away = swap_group(hold(contract_own))
        cot_away_t = swap_group(hold(cot_t))
        first_away = swap_group(hold(first_out))

        tiles = units // 640
        start_first = jnp.reshape((1 - side) * tiles, (1,)).astype(jnp.int32)
        start_second = jnp.reshape(side * tiles, (1,)).astype(jnp.int32)

        def do_hidden(start, bias):
            return held(hidden(hold(start), second_own, second_out, w_expand, expand_away, bias, units))

        attended, lse = held(attend(packed))
        att_own, att_out, middle_t, second_own, second_out, normed_t, inv_t = held(project(
            sides, attended, tok_t, w_project, project_away, small_rows
        ))
        act_first, slope_first = do_hidden(start_first, away_small)
        act_away = swap_group(act_first)
        act_second, slope_second = do_hidden(start_second, own_small)

        chunk_d = width // count
        chunk_f = 2 * units // count
        chunk_h = w_heads.shape[1] // count
        groups = {
            "c": Group(count, units, [chunk_d], PLANS[0]),
            "e": Group(count, width // 2, [chunk_f, chunk_d], PLANS[1]),
            "h": Group(count, width // 2, [chunk_h], PLANS[2]),
        }
        meta_all = jnp.stack([rank, jnp.int32(0)]).astype(jnp.int32)
        state, results = {}, {}
        r = types.SimpleNamespace()

        def send(name, buffers):
            group = groups[name]
            state[name] = [list(buffers[:3]), 0, [
                exchange(buffers[3 + k], 1 << group.orders[k][0], count) for k in range(3)
            ]]

        def advance(name):
            group = groups[name]
            keeps, depth, arrived = state[name]
            keeps = [hold(keeps[0])] + keeps[1:]
            if depth == bits - 1:
                results[name] = held(finish(group, keeps, arrived))
                return
            buffers = held(merge(keeps, arrived))
            state[name] = [list(buffers[:3]), depth + 1, [
                exchange(buffers[3 + k], 1 << group.orders[k][depth + 1], count) for k in range(3)
            ]]

        def do_contract():
            send("c", held(spread(
                groups["c"], 0, hold(meta_all), (cot_t, cot_away_t), (act_second, act_away)
            )))

        def do_hidden_back():
            r.ge, r.eb = held(hidden_back(
                hold(sides), cot, contract_away, contract_own, slope_first, slope_second
            ))
            r.ge_away = swap_group(r.ge)
            r.second_away = swap_group(second_out)
            r.att_away = swap_group(att_out)

        def do_middle():
            r.gm_t, r.gmb_t, r.ga_t, r.s_gain2, r.s_shift2, r.s_pb = held(middle_back(
                hold(sides), r.ge, w_expand, expand_away, normed_t, inv_t,
                cols, cot_t, w_project, project_away,
            ))
            r.gmb_away = swap_group(r.gmb_t)

        def do_expand():
            r.buffers = held(spread(
                groups["e"], 0, hold(meta_all), (r.ge, r.ge_away), (second_own, r.second_away)
            ))

        def do_project():
            send("e", held(spread(
                groups["e"], 1, hold(meta_all), (r.gmb_t, r.gmb_away),
                (att_own, r.att_away), r.buffers,
            )))

        def do_attend_back():
            r.gp_t = held(attend_back(hold(packed), r.ga_t, attended, lse))
            r.gp_away = swap_group(r.gp_t)

        def do_heads():
            send("h", held(spread(
                groups["h"], 0, hold(meta_all), (r.gp_t, r.gp_away), (first_own, first_away)
            )))

        def do_first():
            r.grad_tokens_t, r.s_gain1, r.s_shift1, r.s_pack = held(first_back(
                hold(sides), r.gp_t, w_heads, heads_away, tok_t, cols, r.gm_t
            ))

        def do_output():
            r.block_out_t = held(
                block_output(hold(act_first), act_second, contract_away, contract_own, middle_t, cols)
            )

        small = []

        def do_small():
            if not small:
                mine, theirs = held(collect(
                    hold(sides), r.s_pack, r.eb,
                    [r.s_gain1, r.s_shift1, r.s_pb, r.s_gain2, r.s_shift2, cot_sum],
                ))
                small.extend([mine, swap_group(theirs), 0])
                return
            vector, arrived, bit = small
            if bit == bits:
                small[0] = held(divide(hold(vector), arrived, [width // 2] * 8 + [units]))
                return
            vector = held(add(hold(vector), arrived))
            small[:] = [vector, exchange(vector, 1 << (bits - 1 - bit), count), bit + 1]

        steps = {
            "sc": do_contract, "hb": do_hidden_back, "mid": do_middle,
            "e": do_expand, "p": do_project, "ab": do_attend_back,
            "sh": do_heads, "first": do_first, "out": do_output, "s": do_small,
            "mc": lambda: advance("c"), "me": lambda: advance("e"),
            "mh": lambda: advance("h"),
        }
        for name in all_steps(bits):
            steps[name]()
        finals = small[0]
        (out_w_contract,) = results["c"]
        out_w_expand, out_w_project = results["e"]
        (out_w_heads,) = results["h"]
        grad_tokens_t, block_out_t = r.grad_tokens_t, r.block_out_t

        return (
            block_out_t.T,
            grad_tokens_t.T,
            finals[0],
            finals[1],
            out_w_heads,
            finals[2],
            finals[3],
            out_w_project,
            finals[4],
            finals[5],
            finals[6],
            out_w_expand,
            finals[8],
            out_w_contract,
            finals[7],
        )

    placed = (
        P(("rep", "grp"), None),
        P("grp"),
        P("grp"),
        P("grp", None),
        P("grp"),
        P("grp"),
        P("grp", None),
        P("grp"),
        P("grp"),
        P("grp"),
        P("grp", None),
        P("grp"),
        P("grp", None),
        P("grp"),
        P(("rep", "grp"), None),
    )
    return jax.shard_map(
        per_device,
        mesh=mesh,
        in_specs=placed,
        out_specs=(
            P(("rep", "grp"), None),
            P(("rep", "grp"), None),
            P("grp"),
            P("grp"),
            P("grp", "rep"),
            P("grp"),
            P("grp"),
            P("grp", "rep"),
            P("grp"),
            P("grp"),
            P("grp"),
            P("grp", "rep"),
            P("grp"),
            P("grp", "rep"),
            P("grp"),
        ),
        check_vma=False,
    )
```

profile of v0, /device:TPU:0, one launch (start us, length us, event | category | flops | bytes accessed | tf_op | source)
XLA Modules:
  0.0 529.6 jit_solution(10007682770779076864)
XLA Ops:
  4.7 2.2 unpack.1
  6.9 6.0 %prep.1 = (bf16[512,896]{1,0:T(8,128)(2,1)}, bf16[512,896]{1,0:T(8,128)(2,1)}, bf16[512,1600]{1,0:T(8,128)(2,1)}, f32[8,1600]{1,0:T(8,128)}) custom-call(s32[1]{0:T(128)} %bitcast.1.side_ref.meta_ref, bf16[1600,512]{1,0:T(8,128)(2,1)} %bitcast.21, bf16[1600,512]{1,0:T(8,128)(2,1)} %bitcast.17, f32[1600,128]{1,0:T(8,128)} %get-tuple-element.174.cols_ref.gain_ref), custom_call_target="tpu_custom_call" | custom-call | bytes 6553600 | tf_op jit(solution)/shard_map/prep/pallas_call | solution.py:210
  13.4 3.2 collective-permute-done.1.wa_ref.wa_hbm
  16.6 14.1 %heads.1.q_ref.ka_ref.kb_ref.v_ref = bf16[512,4800]{1,0:T(8,128)(2,1)} custom-call(bf16[512,896]{1,0:T(8,128)(2,1)} %get-tuple-element.175.own_ref.ro_ref, bf16[512,896]{1,0:T(8,128)(2,1)} %get-tuple-element.233.away_ref, bf16[800,4800]{1,0:T(8,128)(2,1)} %wo_hbm.3, bf16[800,4800]{1,0:T(8,128)(2,1)} %collective-permute-done.1.wa_ref.wa_hbm, ...), custom_call_target="tpu_custom_call" | custom-call | flops 7864320000 | bytes 20275200 | tf_op jit(solution)/shard_map/heads/pallas_call | solution.py:242
  31.3 16.4 %attend.1 = (bf16[512,1600]{1,0:T(8,128)(2,1)}, f32[512,128]{1,0:T(8,128)}) custom-call(bf16[512,4800]{1,0:T(8,128)(2,1)} %heads.1.q_ref.ka_ref.kb_ref.v_ref, bf16[512,4800]{1,0:T(8,128)(2,1)} %heads.1.q_ref.ka_ref.kb_ref.v_ref, bf16[512,4800]{1,0:T(8,128)(2,1)} %heads.1.q_ref.ka_ref.kb_ref.v_ref, bf16[512,4800]{1,0:T(8,128)(2,1)} %heads.1.q_ref.ka_ref.kb_ref.v_ref), custom_call_target="tpu_custom_call" | custom-call | flops 5033164800 | bytes 6553600 | tf_op jit(solution)/shard_map/attend/pallas_call | solution.py:309
  47.7 10.9 %project.1 = (bf16[512,896]{1,0:T(8,128)(2,1)}, bf16[512,896]{1,0:T(8,128)(2,1)}, f32[1600,512]{1,0:T(8,128)}, bf16[512,896]{1,0:T(8,128)(2,1)}, bf16[512,896]{1...) custom-call(s32[1]{0:T(128)} %bitcast.1.side_ref.meta_ref, ...), custom_call_target="tpu_custom_call" | custom-call | flops 2621440000 | bytes 16588800 | tf_op jit(solution)/shard_map/project/pallas_call | solution.py:429
  58.6 13.8 %hidden.2 = (bf16[512,3200]{1,0:T(8,128)(2,1)}, bf16[512,3200]{1,0:T(8,128)(2,1)}) custom-call(s32[1]{0:T(128)} %bitcast.start_ref, bf16[512,896]{1,0:T(8,128)(2,1)} %get-tuple-element.184.so_ref.ro_ref, bf16[512,896]{1,0:T(8,128)(2,1)} %get-tuple-element.185.sa_ref, bf16[800,6400]{1,0:T(8,128)(2,1)} %wo_hbm.2, ...), custom_call_target="tpu_custom_call" | custom-call | flops 5242880000 | bytes 16793600 | tf_op jit(solution)/shard_map/hidden/pallas_call | solution.py:477
  73.5 13.5 %hidden.3 = (bf16[512,3200]{1,0:T(8,128)(2,1)}, bf16[512,3200]{1,0:T(8,128)(2,1)}) custom-call(s32[1]{0:T(128)} %bitcast.5.start_ref, bf16[512,896]{1,0:T(8,128)(2,1)} %get-tuple-element.184.so_ref.ro_ref, bf16[512,896]{1,0:T(8,128)(2,1)} %get-tuple-element.185.sa_ref, bf16[800,6400]{1,0:T(8,128)(2,1)} %wo_hbm.2, ...), custom_call_target="tpu_custom_call" | custom-call | flops 5242880000 | bytes 16793600 | tf_op jit(solution)/shard_map/hidden/pallas_call | solution.py:477
  88.2 19.0 %spread.4 = (bf16[8,112,1152]{2,1,0:T(8,128)(2,1)}, bf16[8,112,1152]{2,1,0:T(8,128)(2,1)}, bf16[8,112,896]{2,1,0:T(8,128)(2,1)}, bf16[8,112,1152]{2,1,0:T(8,128)...) custom-call(s32[2]{0:T(128)} %pad_add_fusion.meta_ref, bf16[1600,512]{1,0:T(8,128)(2,1)} %bitcast.18, ...), custom_call_target="tpu_custom_call" | custom-call | flops 10485760000 | bytes 13516800 | tf_op jit(solution)/shard_map/spread/pallas_call | solution.py:919
  107.2 21.9 %hback.1 = (bf16[6400,512]{1,0:T(8,128)(2,1)}, f32[8,6400]{1,0:T(8,128)}) custom-call(s32[1]{0:T(128)} %bitcast.1.side_ref.meta_ref, bf16[512,1600]{1,0:T(8,128)(2,1)} %get-tuple-element.195.cot_ref, bf16[1600,3200]{1,0:T(8,128)(2,1)} %collective-permute-done.6.w1_ref.w1_hbm, bf16[1600,3200]{1,0:T(8,128)(2,1)} %bitcast.27, ...), custom_call_target="tpu_custom_call" | custom-call | flops 10485760000 | bytes 33587200 | tf_op jit(solution)/shard_map/hback/pallas_call | solution.py:511
  129.5 2.7 collective-permute-start.9
  135.2 27.0 %middle.1 = (f32[1600,512]{1,0:T(8,128)}, bf16[1600,512]{1,0:T(8,128)(2,1)}, bf16[1600,512]{1,0:T(8,128)(2,1)}, f32[8,1600]{1,0:T(8,128)}, f32[8,1600]{1,0:T(8,128)}, /*index=5*/f32[8,1600]{1,0:T(8,128)}) custom-call(s32[1]{0:T(128)} %bitcast.1.side_ref.meta_ref, bf16[6400,512]{1,0:T(8,128)(2,1)} %get-tuple-element.199.g_ref.lo_ref, ...), custom_call_target="tpu_custom_call" | custom-call | flops 13107200000 | bytes 30310400 | tf_op jit(solution)/shard_map/middle/pallas_call | solution.py:619
  162.2 6.0 %collective-permute-done.9.refs_9_.refs_11_ = bf16[8,112,896]{2,1,0:T(8,128)(2,1)} collective-permute-done((bf16[8,112,896]{2,1,0:T(8,128)(2,1)}, bf16[8,112,896]{2,1,0:T(8,128)(2,1)}, u32[]{:S(2)}, u32[]{:S(2)}) %collective-permute-start.9) | collective-permute-done | bytes 1605664 | tf_op jit(solution)/shard_map/ppermute | solution.py:45
  168.1 11.2 %collective-permute-done.7.refs_1_.refs_3_ = bf16[8,112,1152]{2,1,0:T(8,128)(2,1)S(1)} collective-permute-done((bf16[8,112,1152]{2,1,0:T(8,128)(2,1)}, bf16[8,112,1152]{2,1,0:T(8,128)(2,1)S(1)}, u32[]{:S(2)}, u32[]{:S(2)}) %collective-permute-start.7) | collective-permute-done | bytes 2064416 | tf_op jit(solution)/shard_map/ppermute | solution.py:45
  181.9 7.2 %merge.9 = (bf16[4,112,1152]{2,1,0:T(8,128)(2,1)}, bf16[4,112,1152]{2,1,0:T(8,128)(2,1)}, bf16[4,112,896]{2,1,0:T(8,128)(2,1)}, bf16[4,112,1152]{2,1,0:T(8,128)(...) custom-call(bf16[8,112,1152]{2,1,0:T(8,128)(2,1)} %get-tuple-element.204.refs_0_.refs_2_, ...), custom_call_target="tpu_custom_call" | custom-call | bytes 17203200 | tf_op jit(solution)/shard_map/merge/pallas_call | solution.py:962
  189.1 22.7 %spread.5 = (bf16[8,512,256]{2,1,0:T(8,128)(2,1)}, bf16[8,512,256]{2,1,0:T(8,128)(2,1)}, bf16[8,592,256]{2,1,0:T(8,128)(2,1)}, bf16[8,512,256]{2,1,0:T(8,128)(2,...) custom-call(s32[2]{0:T(128)} %pad_add_fusion.meta_ref, ...), custom_call_target="tpu_custom_call" | custom-call | flops 10485760000 | bytes 23347200 | tf_op jit(solution)/shard_map/spread/pallas_call | solution.py:919
  211.8 8.5 %spread.6 = (bf16[8,512,256]{2,1,0:T(8,128)(2,1)}, bf16[8,512,256]{2,1,0:T(8,128)(2,1)}, bf16[8,592,256]{2,1,0:T(8,128)(2,1)}, bf16[8,512,256]{2,1,0:T(8,128)(2,...) custom-call(s32[2]{0:T(128)} %pad_add_fusion.meta_ref, ...), custom_call_target="tpu_custom_call", output_to_operand_aliasing={{0}: (5, {}), {1}: (6, {}), {2}: (7, {}), {3}: (8, {}), {4}... | custom-call | flops 2621440000 | bytes 5836800 | tf_op jit(solution)/shard_map/spread/pallas_call | solution.py:919
  220.4 22.8 %aback.1 = bf16[3,1600,512]{2,1,0:T(8,128)(2,1)} custom-call(bf16[512,4800]{1,0:T(8,128)(2,1)} %heads.1.q_ref.ka_ref.kb_ref.v_ref, bf16[512,4800]{1,0:T(8,128)(2,1)} %heads.1.q_ref.ka_ref.kb_ref.v_ref, bf16[512,4800]{1,0:T(8,128)(2,1)} %heads.1.q_ref.ka_ref.kb_ref.v_ref, bf16[512,4800]{1,0:T(8,128)(2,1)} %heads.1.q_ref.ka_ref.kb_ref.v_ref, ...), custom_call_target="tpu_custom_call" | custom-call | flops 5033164800 | bytes 11468800 | tf_op jit(solution)/shard_map/aback/pallas_call | solution.py:381
  247.7 16.7 %collective-permute-done.16.refs_9_.refs_11_ = bf16[4,112,896]{2,1,0:T(8,128)(2,1)S(1)} collective-permute-done((bf16[4,112,896]{2,1,0:T(8,128)(2,1)}, bf16[4,112,896]{2,1,0:T(8,128)(2,1)S(1)}, u32[]{:S(2)}, u32[]{:S(2)}) %collective-permute-start.16) | collective-permute-done | bytes 802848 | tf_op jit(solution)/shard_map/ppermute | solution.py:45
  264.4 4.7 collective-permute-done.14.refs_1_.refs_3_
  271.6 4.1 merge.10
  276.8 16.6 %spread.7 = (bf16[8,304,384]{2,1,0:T(8,128)(2,1)}, bf16[8,304,256]{2,1,0:T(8,128)(2,1)}, bf16[8,384,128]{2,1,0:T(8,128)(2,1)}, bf16[8,304,384]{2,1,0:T(8,128)(2,...) custom-call(s32[2]{0:T(128)} %pad_add_fusion.meta_ref, bf16[4800,512]{1,0:T(8,128)(2,1)} %bitcast.15, ...), custom_call_target="tpu_custom_call" | custom-call | flops 7864320000 | bytes 17510400 | tf_op jit(solution)/shard_map/spread/pallas_call | solution.py:919
  294.5 32.0 %collective-permute-done.24.refs_9_.refs_11_ = bf16[2,112,896]{2,1,0:T(8,128)(2,1)S(1)} collective-permute-done((bf16[2,112,896]{2,1,0:T(8,128)(2,1)}, bf16[2,112,896]{2,1,0:T(8,128)(2,1)S(1)}, u32[]{:S(2)}, u32[]{:S(2)}) %collective-permute-start.24) | collective-permute-done | bytes 401440 | tf_op jit(solution)/shard_map/ppermute | solution.py:45
  331.4 7.8 %merge.11 = (bf16[4,512,256]{2,1,0:T(8,128)(2,1)}, bf16[4,512,256]{2,1,0:T(8,128)(2,1)}, bf16[4,592,256]{2,1,0:T(8,128)(2,1)}, bf16[4,512,256]{2,1,0:T(8,128)(2,...) custom-call(bf16[8,512,256]{2,1,0:T(8,128)(2,1)} %get-tuple-element.235.refs_0_.refs_2_, ...), custom_call_target="tpu_custom_call" | custom-call | bytes 19857408 | tf_op jit(solution)/shard_map/merge/pallas_call | solution.py:962
  339.2 2.6 collective-permute-done.22.refs_1_.refs_3_
  341.8 12.0 %collective-permute-done.23.refs_5_.refs_7_ = bf16[2,112,1152]{2,1,0:T(8,128)(2,1)} collective-permute-done((bf16[2,112,1152]{2,1,0:T(8,128)(2,1)}, bf16[2,112,1152]{2,1,0:T(8,128)(2,1)}, u32[]{:S(2)}, u32[]{:S(2)}) %collective-permute-start.23) | collective-permute-done | bytes 516128 | tf_op jit(solution)/shard_map/ppermute | solution.py:45
  353.8 3.1 merge.12
  359.7 20.7 %first.1 = (bf16[1600,512]{1,0:T(8,128)(2,1)}, f32[8,1600]{1,0:T(8,128)}, f32[8,1600]{1,0:T(8,128)}, f32[8,4800]{1,0:T(8,128)}) custom-call(s32[1]{0:T(128)} %bitcast.1.side_ref.meta_ref, bf16[4800,512]{1,0:T(8,128)(2,1)} %bitcast.16, bf16[800,4800]{1,0:T(8,128)(2,1)} %wo_hbm.3, bf16[800,4800]{1,0:T(8,128)(2,1)} %collective-permute-done.1.wa_ref.wa_hbm, ...), custom_call_target="tpu_custom_call" | custom-call | flops 7864320000 | bytes 28467200 | tf_op jit(solution)/shard_map/first/pallas_call | solution.py:742
  383.5 5.7 %merge.13 = (bf16[4,304,384]{2,1,0:T(8,128)(2,1)}, bf16[4,304,256]{2,1,0:T(8,128)(2,1)}, bf16[4,384,128]{2,1,0:T(8,128)(2,1)}, bf16[4,304,384]{2,1,0:T(8,128)(2,...) custom-call(bf16[8,304,384]{2,1,0:T(8,128)(2,1)} %get-tuple-element.261.refs_0_.refs_2_, ...), custom_call_target="tpu_custom_call" | custom-call | bytes 11698176 | tf_op jit(solution)/shard_map/merge/pallas_call | solution.py:962
  395.1 4.4 merge.14
  401.7 19.8 %collective-permute-done.34.refs_9_.refs_11_ = bf16[4,384,128]{2,1,0:T(8,128)(2,1)S(1)} collective-permute-done((bf16[4,384,128]{2,1,0:T(8,128)(2,1)}, bf16[4,384,128]{2,1,0:T(8,128)(2,1)S(1)}, u32[]{:S(2)}, u32[]{:S(2)}) %collective-permute-start.34) | collective-permute-done | bytes 393248 | tf_op jit(solution)/shard_map/ppermute | solution.py:45
  423.3 2.7 collective-permute-start.35
  426.9 3.3 merge.15
  430.2 2.6 collective-permute-done.35.b_ref
  435.0 3.5 collective-permute-start.42
  438.6 2.9 collective-permute-start.41
  442.3 3.1 merge.16
  447.5 18.3 %output.1 = bf16[1600,512]{1,0:T(8,128)(2,1)} custom-call(bf16[512,3200]{1,0:T(8,128)(2,1)} %get-tuple-element.292.a1_ref, bf16[512,3200]{1,0:T(8,128)(2,1)} %get-tuple-element.190.ro_ref.a2_ref, bf16[1600,3200]{1,0:T(8,128)(2,1)} %collective-permute-done.6.w1_ref.w1_hbm, bf16[1600,3200]{1,0:T(8,128)(2,1)} %bitcast.28, ...), custom_call_target="tpu_custom_call" | custom-call | flops 10485760000 | bytes 31948800 | tf_op jit(solution)/shard_map/output/pallas_call | solution.py:793
  469.5 4.2 collective-permute-done.43.b_ref
  473.8 2.6 finish.3
  479.2 2.8 collective-permute-start.49
  482.7 2.7 merge.17
  485.6 15.3 %collective-permute-done.48.refs_1_ = bf16[1,512,256]{2,1,0:T(8,128)(2,1)S(1)} collective-permute-done((bf16[1,512,256]{2,1,0:T(8,128)(2,1)S(1)}, bf16[1,512,256]{2,1,0:T(8,128)(2,1)S(1)}, u32[]{:S(2)}, u32[]{:S(2)}) %collective-permute-start.48) | collective-permute-done | bytes 262176 | tf_op jit(solution)/shard_map/ppermute | solution.py:45
  500.9 2.9 collective-permute-start.53
  505.5 12.9 %collective-permute-done.49.refs_3_ = bf16[1,512,256]{2,1,0:T(8,128)(2,1)S(1)} collective-permute-done((bf16[1,512,256]{2,1,0:T(8,128)(2,1)S(1)}, bf16[1,512,256]{2,1,0:T(8,128)(2,1)S(1)}, u32[]{:S(2)}, u32[]{:S(2)}) %collective-permute-start.49) | collective-permute-done | bytes 262176 | tf_op jit(solution)/shard_map/ppermute | solution.py:45
  519.2 2.8 finish.4
  522.1 4.1 collective-permute-done.53.refs_5_
  527.0 2.4 finish.5
  (174 shorter events, 60.0 us)
Async XLA Ops:
  4.0 12.6 %collective-permute-start.1 = (bf16[800,4800]{1,0:T(8,128)(2,1)}, bf16[800,4800]{1,0:T(8,128)(2,1)}, u32[]{:S(2)}, u32[]{:S(2)}) collective-permute-start(bf16[800,4800]{1,0:T(8,128)(2,1)} %wo_hbm.3), channel_id=1, source_target_pairs={{0,1},{1,0},{2,3},{3,2},{4,5},{5,4},{6,7},{7,6},{8,9},{9,8},{10,11... | collective-permute-start | bytes 23040008 | tf_op jit(solution)/shard_map/ppermute | solution.py:41
  12.9 17.8 %collective-permute-start.2 = (bf16[800,1600]{1,0:T(8,128)(2,1)S(1)}, bf16[800,1600]{1,0:T(8,128)(2,1)}, u32[]{:S(2)}, u32[]{:S(2)}) collective-permute-start(bf16[800,1600]{1,0:T(8,128)(2,1)S(1)} %copy-done.33), channel_id=1, source_target_pairs={{0,1},{1,0},{2,3},{3,2},{4,5},{5,4},{6,7},{7,6},{8,9},{9,8},{10,11... | collective-permute-start | bytes 7680008 | tf_op jit(solution)/shard_map/ppermute | solution.py:41
  30.8 27.9 %collective-permute-start.3 = (bf16[800,6400]{1,0:T(8,128)(2,1)}, bf16[800,6400]{1,0:T(8,128)(2,1)}, u32[]{:S(2)}, u32[]{:S(2)}) collective-permute-start(bf16[800,6400]{1,0:T(8,128)(2,1)} %wo_hbm.2), channel_id=1, source_target_pairs={{0,1},{1,0},{2,3},{3,2},{4,5},{5,4},{6,7},{7,6},{8,9},{9,8},{10,11... | collective-permute-start | bytes 30720008 | tf_op jit(solution)/shard_map/ppermute | solution.py:41
  31.1 76.0 %collective-permute-start.6 = (bf16[1600,3200]{1,0:T(8,128)(2,1)}, bf16[1600,3200]{1,0:T(8,128)(2,1)}, u32[]{:S(2)}, u32[]{:S(2)}) collective-permute-start(bf16[1600,3200]{1,0:T(8,128)(2,1)} %bitcast.26), channel_id=1, source_target_pairs={{0,1},{1,0},{2,3},{3,2},{4,5},{5,4},{6,7},{7,6},{8,9},{9,8},{10,11... | collective-permute-start | bytes 30720008 | tf_op jit(solution)/shard_map/ppermute | solution.py:41
  72.4 14.6 %collective-permute-start.5 = (bf16[512,3200]{1,0:T(8,128)(2,1)}, bf16[512,3200]{1,0:T(8,128)(2,1)}, u32[]{:S(2)}, u32[]{:S(2)}) collective-permute-start(bf16[512,3200]{1,0:T(8,128)(2,1)} %get-tuple-element.292.a1_ref), channel_id=1, source_target_pairs={{0,1},{1,0},{2,3},{3,2},{4,5},{5,4},{6,7},{7,6},{8,9},{9,8},{10,11... | collective-permute-start | bytes 9830408 | tf_op jit(solution)/shard_map/ppermute | solution.py:41
  72.8 14.2 %collective-permute-start.4 = (bf16[1600,512]{1,0:T(8,128)(2,1)S(1)}, bf16[1600,512]{1,0:T(8,128)(2,1)S(1)}, u32[]{:S(2)}, u32[]{:S(2)}) collective-permute-start(bf16[1600,512]{1,0:T(8,128)(2,1)S(1)} %bitcast.20), channel_id=1, source_target_pairs={{0,1},{1,0},{2,3},{3,2},{4,5},{5,4},{6,7},{7,6},{8,9},{9,8},{10,11... | collective-permute-start | bytes 4915208 | tf_op jit(solution)/shard_map/ppermute | solution.py:41
  129.1 60.0 %collective-permute-start.10 = (bf16[6400,512]{1,0:T(8,128)(2,1)}, bf16[6400,512]{1,0:T(8,128)(2,1)}, u32[]{:S(2)}, u32[]{:S(2)}) collective-permute-start(bf16[6400,512]{1,0:T(8,128)(2,1)} %get-tuple-element.199.g_ref.lo_ref), channel_id=1, source_target_pairs={{0,1},{1,0},{2,3},{3,2},{4,5},{5,4},{6,7},{7,6},{8,9},{9,8},{10,11... | collective-permute-start | bytes 19660808 | tf_op jit(solution)/shard_map/ppermute | solution.py:41
  129.5 38.6 %collective-permute-start.9 = (bf16[8,112,896]{2,1,0:T(8,128)(2,1)}, bf16[8,112,896]{2,1,0:T(8,128)(2,1)}, u32[]{:S(2)}, u32[]{:S(2)}) collective-permute-start(bf16[8,112,896]{2,1,0:T(8,128)(2,1)} %get-tuple-element.209), channel_id=1, source_target_pairs={{0,8},{2,10},{4,12},{6,14},{8,0},{10,2},{12,4},{14,6},{16,24},{18,... | collective-permute-start | bytes 4816904 | tf_op jit(solution)/shard_map/ppermute | solution.py:45
  132.2 47.1 %collective-permute-start.7 = (bf16[8,112,1152]{2,1,0:T(8,128)(2,1)}, bf16[8,112,1152]{2,1,0:T(8,128)(2,1)S(1)}, u32[]{:S(2)}, u32[]{:S(2)}) collective-permute-start(bf16[8,112,1152]{2,1,0:T(8,128)(2,1)} %get-tuple-element.205), channel_id=1, source_target_pairs={{0,2},{2,0},{4,6},{6,4},{8,10},{10,8},{12,14},{14,12},{16,18},{18,... | collective-permute-start | bytes 6193160 | tf_op jit(solution)/shard_map/ppermute | solution.py:45
  133.7 46.9 %collective-permute-start.8 = (bf16[8,112,1152]{2,1,0:T(8,128)(2,1)}, bf16[8,112,1152]{2,1,0:T(8,128)(2,1)S(1)}, u32[]{:S(2)}, u32[]{:S(2)}) collective-permute-start(bf16[8,112,1152]{2,1,0:T(8,128)(2,1)} %get-tuple-element.207), channel_id=1, source_target_pairs={{0,4},{2,6},{4,0},{6,2},{8,12},{10,14},{12,8},{14,10},{16,20},{18,... | collective-permute-start | bytes 6193160 | tf_op jit(solution)/shard_map/ppermute | solution.py:45
  135.2 53.9 %collective-permute-start.11 = (bf16[512,896]{1,0:T(8,128)(2,1)}, bf16[512,896]{1,0:T(8,128)(2,1)}, u32[]{:S(2)}, u32[]{:S(2)}) collective-permute-start(bf16[512,896]{1,0:T(8,128)(2,1)} %get-tuple-element.185.sa_ref), channel_id=1, source_target_pairs={{0,1},{1,0},{2,3},{3,2},{4,5},{5,4},{6,7},{7,6},{8,9},{9,8},{10,11... | collective-permute-start | bytes 2752520 | tf_op jit(solution)/shard_map/ppermute | solution.py:41
  168.1 43.7 %collective-permute-start.12 = (bf16[1600,512]{1,0:T(8,128)(2,1)}, bf16[1600,512]{1,0:T(8,128)(2,1)}, u32[]{:S(2)}, u32[]{:S(2)}) collective-permute-start(bf16[1600,512]{1,0:T(8,128)(2,1)} %get-tuple-element.214.lo_ref), channel_id=1, source_target_pairs={{0,1},{1,0},{2,3},{3,2},{4,5},{5,4},{6,7},{7,6},{8,9},{9,8},{10,11... | collective-permute-start | bytes 4915208 | tf_op jit(solution)/shard_map/ppermute | solution.py:41
  179.3 32.5 %collective-permute-start.13 = (bf16[512,896]{1,0:T(8,128)(2,1)}, bf16[512,896]{1,0:T(8,128)(2,1)}, u32[]{:S(2)}, u32[]{:S(2)}) collective-permute-start(bf16[512,896]{1,0:T(8,128)(2,1)} %get-tuple-element.215), channel_id=1, source_target_pairs={{0,1},{1,0},{2,3},{3,2},{4,5},{5,4},{6,7},{7,6},{8,9},{9,8},{10,11... | collective-permute-start | bytes 2752520 | tf_op jit(solution)/shard_map/ppermute | solution.py:41
  243.2 33.6 %collective-permute-start.17 = (bf16[4800,512]{1,0:T(8,128)(2,1)}, bf16[4800,512]{1,0:T(8,128)(2,1)}, u32[]{:S(2)}, u32[]{:S(2)}) collective-permute-start(bf16[4800,512]{1,0:T(8,128)(2,1)} %bitcast.14), channel_id=1, source_target_pairs={{0,1},{1,0},{2,3},{3,2},{4,5},{5,4},{6,7},{7,6},{8,9},{9,8},{10,11... | collective-permute-start | bytes 14745608 | tf_op jit(solution)/shard_map/ppermute | solution.py:41
  243.2 26.0 %collective-permute-start.14 = (bf16[4,112,1152]{2,1,0:T(8,128)(2,1)}, bf16[4,112,1152]{2,1,0:T(8,128)(2,1)S(1)}, u32[]{:S(2)}, u32[]{:S(2)}) collective-permute-start(bf16[4,112,1152]{2,1,0:T(8,128)(2,1)} %get-tuple-element.226), channel_id=1, source_target_pairs={{0,8},{2,10},{4,12},{6,14},{8,0},{10,2},{12,4},{14,6},{16,24},{18,... | collective-permute-start | bytes 3096584 | tf_op jit(solution)/shard_map/ppermute | solution.py:45
  243.6 26.4 %collective-permute-start.15 = (bf16[4,112,1152]{2,1,0:T(8,128)(2,1)}, bf16[4,112,1152]{2,1,0:T(8,128)(2,1)}, u32[]{:S(2)}, u32[]{:S(2)}) collective-permute-start(bf16[4,112,1152]{2,1,0:T(8,128)(2,1)} %get-tuple-element.228), channel_id=1, source_target_pairs={{0,2},{2,0},{4,6},{6,4},{8,10},{10,8},{12,14},{14,12},{16,18},{18,... | collective-permute-start | bytes 3096584 | tf_op jit(solution)/shard_map/ppermute | solution.py:45
  244.5 19.9 %collective-permute-start.16 = (bf16[4,112,896]{2,1,0:T(8,128)(2,1)}, bf16[4,112,896]{2,1,0:T(8,128)(2,1)S(1)}, u32[]{:S(2)}, u32[]{:S(2)}) collective-permute-start(bf16[4,112,896]{2,1,0:T(8,128)(2,1)} %get-tuple-element.230), channel_id=1, source_target_pairs={{0,4},{2,6},{4,0},{6,2},{8,12},{10,14},{12,8},{14,10},{16,20},{18,... | collective-permute-start | bytes 2408456 | tf_op jit(solution)/shard_map/ppermute | solution.py:45
  246.1 83.8 %collective-permute-start.21 = (bf16[8,592,256]{2,1,0:T(8,128)(2,1)}, bf16[8,592,256]{2,1,0:T(8,128)(2,1)S(1)}, u32[]{:S(2)}, u32[]{:S(2)}) collective-permute-start(bf16[8,592,256]{2,1,0:T(8,128)(2,1)} %get-tuple-element.240), channel_id=1, source_target_pairs={{0,8},{2,10},{4,12},{6,14},{8,0},{10,2},{12,4},{14,6},{16,24},{18,... | collective-permute-start | bytes 7274504 | tf_op jit(solution)/shard_map/ppermute | solution.py:45
  264.4 11.2 %collective-permute-start.18 = (bf16[512,896]{1,0:T(8,128)(2,1)}, bf16[512,896]{1,0:T(8,128)(2,1)}, u32[]{:S(2)}, u32[]{:S(2)}) collective-permute-start(bf16[512,896]{1,0:T(8,128)(2,1)} %get-tuple-element.233.away_ref), channel_id=1, source_target_pairs={{0,1},{1,0},{2,3},{3,2},{4,5},{5,4},{6,7},{7,6},{8,9},{9,8},{10,11... | collective-permute-start | bytes 2752520 | tf_op jit(solution)/shard_map/ppermute | solution.py:41
  269.1 57.7 %collective-permute-start.19 = (bf16[8,512,256]{2,1,0:T(8,128)(2,1)}, bf16[8,512,256]{2,1,0:T(8,128)(2,1)}, u32[]{:S(2)}, u32[]{:S(2)}) collective-permute-start(bf16[8,512,256]{2,1,0:T(8,128)(2,1)} %get-tuple-element.236), channel_id=1, source_target_pairs={{0,2},{2,0},{4,6},{6,4},{8,10},{10,8},{12,14},{14,12},{16,18},{18,... | collective-permute-start | bytes 6291464 | tf_op jit(solution)/shard_map/ppermute | solution.py:45
  270.0 58.4 %collective-permute-start.20 = (bf16[8,512,256]{2,1,0:T(8,128)(2,1)}, bf16[8,512,256]{2,1,0:T(8,128)(2,1)}, u32[]{:S(2)}, u32[]{:S(2)}) collective-permute-start(bf16[8,512,256]{2,1,0:T(8,128)(2,1)} %get-tuple-element.238), channel_id=1, source_target_pairs={{0,4},{2,6},{4,0},{6,2},{8,12},{10,14},{12,8},{14,10},{16,20},{18,... | collective-permute-start | bytes 6291464 | tf_op jit(solution)/shard_map/ppermute | solution.py:45
  275.7 50.8 %collective-permute-start.24 = (bf16[2,112,896]{2,1,0:T(8,128)(2,1)}, bf16[2,112,896]{2,1,0:T(8,128)(2,1)S(1)}, u32[]{:S(2)}, u32[]{:S(2)}) collective-permute-start(bf16[2,112,896]{2,1,0:T(8,128)(2,1)} %get-tuple-element.247), channel_id=1, source_target_pairs={{0,2},{2,0},{4,6},{6,4},{8,10},{10,8},{12,14},{14,12},{16,18},{18,... | collective-permute-start | bytes 1204232 | tf_op jit(solution)/shard_map/ppermute | solution.py:45
  293.4 89.1 %collective-permute-start.25 = (bf16[8,304,384]{2,1,0:T(8,128)(2,1)}, bf16[8,304,384]{2,1,0:T(8,128)(2,1)}, u32[]{:S(2)}, u32[]{:S(2)}) collective-permute-start(bf16[8,304,384]{2,1,0:T(8,128)(2,1)} %get-tuple-element.262), channel_id=1, source_target_pairs={{0,2},{2,0},{4,6},{6,4},{8,10},{10,8},{12,14},{14,12},{16,18},{18,... | collective-permute-start | bytes 5603336 | tf_op jit(solution)/shard_map/ppermute | solution.py:45
  326.4 32.4 %collective-permute-start.27 = (bf16[8,384,128]{2,1,0:T(8,128)(2,1)}, bf16[8,384,128]{2,1,0:T(8,128)(2,1)}, u32[]{:S(2)}, u32[]{:S(2)}) collective-permute-start(bf16[8,384,128]{2,1,0:T(8,128)(2,1)} %get-tuple-element.266), channel_id=1, source_target_pairs={{0,8},{2,10},{4,12},{6,14},{8,0},{10,2},{12,4},{14,6},{16,24},{18,... | collective-permute-start | bytes 2359304 | tf_op jit(solution)/shard_map/ppermute | solution.py:45
  326.9 14.9 %collective-permute-start.22 = (bf16[2,112,1152]{2,1,0:T(8,128)(2,1)}, bf16[2,112,1152]{2,1,0:T(8,128)(2,1)}, u32[]{:S(2)}, u32[]{:S(2)}) collective-permute-start(bf16[2,112,1152]{2,1,0:T(8,128)(2,1)} %get-tuple-element.243), channel_id=1, source_target_pairs={{0,4},{2,6},{4,0},{6,2},{8,12},{10,14},{12,8},{14,10},{16,20},{18,... | collective-permute-start | bytes 1548296 | tf_op jit(solution)/shard_map/ppermute | solution.py:45
  328.4 25.3 %collective-permute-start.23 = (bf16[2,112,1152]{2,1,0:T(8,128)(2,1)}, bf16[2,112,1152]{2,1,0:T(8,128)(2,1)}, u32[]{:S(2)}, u32[]{:S(2)}) collective-permute-start(bf16[2,112,1152]{2,1,0:T(8,128)(2,1)} %get-tuple-element.245), channel_id=1, source_target_pairs={{0,8},{2,10},{4,12},{6,14},{8,0},{10,2},{12,4},{14,6},{16,24},{18,... | collective-permute-start | bytes 1548296 | tf_op jit(solution)/shard_map/ppermute | solution.py:45
  329.9 52.5 %collective-permute-start.26 = (bf16[8,304,256]{2,1,0:T(8,128)(2,1)}, bf16[8,304,256]{2,1,0:T(8,128)(2,1)S(1)}, u32[]{:S(2)}, u32[]{:S(2)}) collective-permute-start(bf16[8,304,256]{2,1,0:T(8,128)(2,1)} %get-tuple-element.264), channel_id=1, source_target_pairs={{0,4},{2,6},{4,0},{6,2},{8,12},{10,14},{12,8},{14,10},{16,20},{18,... | collective-permute-start | bytes 3735560 | tf_op jit(solution)/shard_map/ppermute | solution.py:45
  356.8 34.0 %collective-permute-start.29 = (bf16[4,512,256]{2,1,0:T(8,128)(2,1)}, bf16[4,512,256]{2,1,0:T(8,128)(2,1)}, u32[]{:S(2)}, u32[]{:S(2)}) collective-permute-start(bf16[4,512,256]{2,1,0:T(8,128)(2,1)} %get-tuple-element.271), channel_id=1, source_target_pairs={{0,4},{2,6},{4,0},{6,2},{8,12},{10,14},{12,8},{14,10},{16,20},{18,... | collective-permute-start | bytes 3145736 | tf_op jit(solution)/shard_map/ppermute | solution.py:45
  358.3 35.8 %collective-permute-start.30 = (bf16[4,512,256]{2,1,0:T(8,128)(2,1)}, bf16[4,512,256]{2,1,0:T(8,128)(2,1)}, u32[]{:S(2)}, u32[]{:S(2)}) collective-permute-start(bf16[4,512,256]{2,1,0:T(8,128)(2,1)} %get-tuple-element.273), channel_id=1, source_target_pairs={{0,8},{2,10},{4,12},{6,14},{8,0},{10,2},{12,4},{14,6},{16,24},{18,... | collective-permute-start | bytes 3145736 | tf_op jit(solution)/shard_map/ppermute | solution.py:45
  358.8 35.3 %collective-permute-start.31 = (bf16[4,592,256]{2,1,0:T(8,128)(2,1)}, bf16[4,592,256]{2,1,0:T(8,128)(2,1)S(1)}, u32[]{:S(2)}, u32[]{:S(2)}) collective-permute-start(bf16[4,592,256]{2,1,0:T(8,128)(2,1)} %get-tuple-element.275), channel_id=1, source_target_pairs={{0,2},{2,0},{4,6},{6,4},{8,10},{10,8},{12,14},{14,12},{16,18},{18,... | collective-permute-start | bytes 3637256 | tf_op jit(solution)/shard_map/ppermute | solution.py:45
  389.2 36.8 %collective-permute-start.32 = (bf16[4,304,384]{2,1,0:T(8,128)(2,1)}, bf16[4,304,384]{2,1,0:T(8,128)(2,1)S(1)}, u32[]{:S(2)}, u32[]{:S(2)}) collective-permute-start(bf16[4,304,384]{2,1,0:T(8,128)(2,1)} %get-tuple-element.278), channel_id=1, source_target_pairs={{0,4},{2,6},{4,0},{6,2},{8,12},{10,14},{12,8},{14,10},{16,20},{18,... | collective-permute-start | bytes 2801672 | tf_op jit(solution)/shard_map/ppermute | solution.py:45
  389.7 33.6 %collective-permute-start.33 = (bf16[4,304,256]{2,1,0:T(8,128)(2,1)}, bf16[4,304,256]{2,1,0:T(8,128)(2,1)S(1)}, u32[]{:S(2)}, u32[]{:S(2)}) collective-permute-start(bf16[4,304,256]{2,1,0:T(8,128)(2,1)} %get-tuple-element.280), channel_id=1, source_target_pairs={{0,2},{2,0},{4,6},{6,4},{8,10},{10,8},{12,14},{14,12},{16,18},{18,... | collective-permute-start | bytes 1867784 | tf_op jit(solution)/shard_map/ppermute | solution.py:45
  390.8 30.6 %collective-permute-start.34 = (bf16[4,384,128]{2,1,0:T(8,128)(2,1)}, bf16[4,384,128]{2,1,0:T(8,128)(2,1)S(1)}, u32[]{:S(2)}, u32[]{:S(2)}) collective-permute-start(bf16[4,384,128]{2,1,0:T(8,128)(2,1)} %get-tuple-element.282), channel_id=1, source_target_pairs={{0,4},{2,6},{4,0},{6,2},{8,12},{10,14},{12,8},{14,10},{16,20},{18,... | collective-permute-start | bytes 1179656 | tf_op jit(solution)/shard_map/ppermute | solution.py:45
  399.5 41.9 %collective-permute-start.38 = (bf16[2,592,256]{2,1,0:T(8,128)(2,1)}, bf16[2,592,256]{2,1,0:T(8,128)(2,1)S(1)}, u32[]{:S(2)}, u32[]{:S(2)}) collective-permute-start(bf16[2,592,256]{2,1,0:T(8,128)(2,1)} %get-tuple-element.290), channel_id=1, source_target_pairs={{0,4},{2,6},{4,0},{6,2},{8,12},{10,14},{12,8},{14,10},{16,20},{18,... | collective-permute-start | bytes 1818632 | tf_op jit(solution)/shard_map/ppermute | solution.py:45
  400.1 38.5 %collective-permute-start.36 = (bf16[2,512,256]{2,1,0:T(8,128)(2,1)}, bf16[2,512,256]{2,1,0:T(8,128)(2,1)S(1)}, u32[]{:S(2)}, u32[]{:S(2)}) collective-permute-start(bf16[2,512,256]{2,1,0:T(8,128)(2,1)} %get-tuple-element.286), channel_id=1, source_target_pairs={{0,8},{2,10},{4,12},{6,14},{8,0},{10,2},{12,4},{14,6},{16,24},{18,... | collective-permute-start | bytes 1572872 | tf_op jit(solution)/shard_map/ppermute | solution.py:45
  422.2 16.4 %collective-permute-start.37 = (bf16[2,512,256]{2,1,0:T(8,128)(2,1)}, bf16[2,512,256]{2,1,0:T(8,128)(2,1)S(1)}, u32[]{:S(2)}, u32[]{:S(2)}) collective-permute-start(bf16[2,512,256]{2,1,0:T(8,128)(2,1)} %get-tuple-element.288), channel_id=1, source_target_pairs={{0,2},{2,0},{4,6},{6,4},{8,10},{10,8},{12,14},{14,12},{16,18},{18,... | collective-permute-start | bytes 1572872 | tf_op jit(solution)/shard_map/ppermute | solution.py:45
  435.0 32.6 %collective-permute-start.42 = (bf16[1,112,896]{2,1,0:T(8,128)(2,1)}, bf16[1,112,896]{2,1,0:T(8,128)(2,1)S(1)}, u32[]{:S(2)}, u32[]{:S(2)}) collective-permute-start(bf16[1,112,896]{2,1,0:T(8,128)(2,1)} %get-tuple-element.300), channel_id=1, source_target_pairs={{0,16},{2,18},{4,20},{6,22},{8,24},{10,26},{12,28},{14,30},{16,0},... | collective-permute-start | bytes 602120 | tf_op jit(solution)/shard_map/ppermute | solution.py:45
  438.5 29.6 %collective-permute-start.40 = (bf16[1,112,1152]{2,1,0:T(8,128)(2,1)}, bf16[1,112,1152]{2,1,0:T(8,128)(2,1)S(1)}, u32[]{:S(2)}, u32[]{:S(2)}) collective-permute-start(bf16[1,112,1152]{2,1,0:T(8,128)(2,1)} %get-tuple-element.296), channel_id=1, source_target_pairs={{0,16},{2,18},{4,20},{6,22},{8,24},{10,26},{12,28},{14,30},{16,0},... | collective-permute-start | bytes 774152 | tf_op jit(solution)/shard_map/ppermute | solution.py:45
  438.6 30.5 %collective-permute-start.41 = (bf16[1,112,1152]{2,1,0:T(8,128)(2,1)}, bf16[1,112,1152]{2,1,0:T(8,128)(2,1)S(1)}, u32[]{:S(2)}, u32[]{:S(2)}) collective-permute-start(bf16[1,112,1152]{2,1,0:T(8,128)(2,1)} %get-tuple-element.298), channel_id=1, source_target_pairs={{0,16},{2,18},{4,20},{6,22},{8,24},{10,26},{12,28},{14,30},{16,0},... | collective-permute-start | bytes 774152 | tf_op jit(solution)/shard_map/ppermute | solution.py:45
  445.4 33.8 %collective-permute-start.45 = (bf16[2,304,256]{2,1,0:T(8,128)(2,1)}, bf16[2,304,256]{2,1,0:T(8,128)(2,1)S(1)}, u32[]{:S(2)}, u32[]{:S(2)}) collective-permute-start(bf16[2,304,256]{2,1,0:T(8,128)(2,1)} %get-tuple-element.305), channel_id=1, source_target_pairs={{0,8},{2,10},{4,12},{6,14},{8,0},{10,2},{12,4},{14,6},{16,24},{18,... | collective-permute-start | bytes 933896 | tf_op jit(solution)/shard_map/ppermute | solution.py:45
  445.4 36.5 %collective-permute-start.44 = (bf16[2,304,384]{2,1,0:T(8,128)(2,1)}, bf16[2,304,384]{2,1,0:T(8,128)(2,1)S(1)}, u32[]{:S(2)}, u32[]{:S(2)}) collective-permute-start(bf16[2,304,384]{2,1,0:T(8,128)(2,1)} %get-tuple-element.303), channel_id=1, source_target_pairs={{0,8},{2,10},{4,12},{6,14},{8,0},{10,2},{12,4},{14,6},{16,24},{18,... | collective-permute-start | bytes 1400840 | tf_op jit(solution)/shard_map/ppermute | solution.py:45
  469.1 31.7 %collective-permute-start.48 = (bf16[1,512,256]{2,1,0:T(8,128)(2,1)S(1)}, bf16[1,512,256]{2,1,0:T(8,128)(2,1)S(1)}, u32[]{:S(2)}, u32[]{:S(2)}) collective-permute-start(bf16[1,512,256]{2,1,0:T(8,128)(2,1)S(1)} %copy-done.37), channel_id=1, source_target_pairs={{0,16},{2,18},{4,20},{6,22},{8,24},{10,26},{12,28},{14,30},{16,0},... | collective-permute-start | bytes 786440 | tf_op jit(solution)/shard_map/ppermute | solution.py:45
  473.6 44.8 %collective-permute-start.50 = (bf16[1,592,256]{2,1,0:T(8,128)(2,1)S(1)}, bf16[1,592,256]{2,1,0:T(8,128)(2,1)S(1)}, u32[]{:S(2)}, u32[]{:S(2)}) collective-permute-start(bf16[1,592,256]{2,1,0:T(8,128)(2,1)S(1)} %copy-done.35), channel_id=1, source_target_pairs={{0,16},{2,18},{4,20},{6,22},{8,24},{10,26},{12,28},{14,30},{16,0},... | collective-permute-start | bytes 909320 | tf_op jit(solution)/shard_map/ppermute | solution.py:45
  478.2 22.7 %collective-permute-start.47 = (f32[16,3200]{1,0:T(8,128)}, f32[16,3200]{1,0:T(8,128)S(1)}, u32[]{:S(2)}, u32[]{:S(2)}) collective-permute-start(f32[16,3200]{1,0:T(8,128)} %add.9.a_ref), channel_id=1, source_target_pairs={{0,2},{2,0},{4,6},{6,4},{8,10},{10,8},{12,14},{14,12},{16,18},{18,... | collective-permute-start | bytes 614408 | tf_op jit(solution)/shard_map/ppermute | solution.py:45
  479.2 39.3 %collective-permute-start.49 = (bf16[1,512,256]{2,1,0:T(8,128)(2,1)S(1)}, bf16[1,512,256]{2,1,0:T(8,128)(2,1)S(1)}, u32[]{:S(2)}, u32[]{:S(2)}) collective-permute-start(bf16[1,512,256]{2,1,0:T(8,128)(2,1)S(1)} %copy-done.36), channel_id=1, source_target_pairs={{0,16},{2,18},{4,20},{6,22},{8,24},{10,26},{12,28},{14,30},{16,0},... | collective-permute-start | bytes 786440 | tf_op jit(solution)/shard_map/ppermute | solution.py:45
  485.4 40.9 %collective-permute-start.51 = (bf16[1,304,384]{2,1,0:T(8,128)(2,1)}, bf16[1,304,384]{2,1,0:T(8,128)(2,1)S(1)}, u32[]{:S(2)}, u32[]{:S(2)}) collective-permute-start(bf16[1,304,384]{2,1,0:T(8,128)(2,1)} %get-tuple-element.320), channel_id=1, source_target_pairs={{0,16},{2,18},{4,20},{6,22},{8,24},{10,26},{12,28},{14,30},{16,0},... | collective-permute-start | bytes 700424 | tf_op jit(solution)/shard_map/ppermute | solution.py:45
  500.9 25.3 %collective-permute-start.52 = (bf16[1,304,256]{2,1,0:T(8,128)(2,1)}, bf16[1,304,256]{2,1,0:T(8,128)(2,1)S(1)}, u32[]{:S(2)}, u32[]{:S(2)}) collective-permute-start(bf16[1,304,256]{2,1,0:T(8,128)(2,1)} %get-tuple-element.322), channel_id=1, source_target_pairs={{0,16},{2,18},{4,20},{6,22},{8,24},{10,26},{12,28},{14,30},{16,0},... | collective-permute-start | bytes 466952 | tf_op jit(solution)/shard_map/ppermute | solution.py:45
  500.9 25.3 %collective-permute-start.53 = (bf16[1,384,128]{2,1,0:T(8,128)(2,1)}, bf16[1,384,128]{2,1,0:T(8,128)(2,1)S(1)}, u32[]{:S(2)}, u32[]{:S(2)}) collective-permute-start(bf16[1,384,128]{2,1,0:T(8,128)(2,1)} %get-tuple-element.324), channel_id=1, source_target_pairs={{0,16},{2,18},{4,20},{6,22},{8,24},{10,26},{12,28},{14,30},{16,0},... | collective-permute-start | bytes 294920 | tf_op jit(solution)/shard_map/ppermute | solution.py:45
  (45 other events, 288.6 us)
where the time goes:
time: 540 us; the launch traced here: 530 us
  Pallas kernels  316 us (59%)
  waiting for transfers between devices  150 us (28%)
  starting transfers between devices  51.5 us (10%)
  local copies, waits for them, and re-layouts  10.6 us (2%)
    ppermute x40, waiting for transfers between devices, exchange(): return lax.ppermute(x, 'rep', [(i, i ^ mask) for i in range(count)])  145 us
    pallas_call x4, Pallas kernels, spread(): pl.pallas_call(functools.partial(spread_kernel, spec), grid_spec=pltpu.Pr...  66.8 us
    ppermute x40, starting transfers between devices, exchange(): return lax.ppermute(x, 'rep', [(i, i ^ mask) for i in range(count)])  48.7 us
    pallas_call x9, Pallas kernels, merge(): pl.pallas_call(merge_kernel, grid=(half,), in_specs=specs, out_specs=out_...  41.3 us
    pallas_call x2, Pallas kernels, hidden(): pl.pallas_call(hidden_kernel, grid_spec=pltpu.PrefetchScalarGridSpec(num_...  27.3 us
    pallas_call x1, Pallas kernels, middle_back(): pl.pallas_call(middle_kernel, grid_spec=pltpu.PrefetchScalarGridSpec(num_...  27 us
    pallas_call x1, Pallas kernels, attend_back(): pl.pallas_call(functools.partial(attend_back_kernel, width), grid=(seqs,...  22.8 us
    pallas_call x1, Pallas kernels, hidden_back(): pl.pallas_call(hidden_back_kernel, grid_spec=pltpu.PrefetchScalarGridSpec...  21.9 us
  transfers between devices with their start and end apart: 54, of which 16 were waited for; matrix products, arithmetic and copies ran while one was open for 0% of the time, Pallas kernels for 49%

commit v1 on v0

--- a/solution.py
+++ b/solution.py
@@ -202,7 +202,7 @@
 
 def prep(side, tok_t, cot_t, cols):
     width, rows = tok_t.shape
-    block = min(256, rows)
+    block = min(128, rows)
     half = round_up(width // 2, 128)
     nat = pl.BlockSpec((block, width), lambda i, *_: (i, 0))
     turned = pl.BlockSpec((width, block), lambda i, *_: (0, i))
@@ -407,7 +407,7 @@
     store_pair(side, att_ref[...], ao_ref, aa_ref)
     mid = joined_dot(ao_ref[...], aa_ref[...], wo_ref[...], wa_ref[...])
     mid += x_ref[...].T.astype(F32) + rows_ref[4:5, :]
-    mid_ref[...] = mid.T
+    mid_ref[...] = mid.astype(BF16).T
     centred = mid - jnp.mean(mid, axis=1, keepdims=True)
     inverse = lax.rsqrt(jnp.mean(centred * centred, axis=1, keepdims=True) + EPS)
     normed = centred * inverse
@@ -440,7 +440,7 @@
         out_shape=[
             shape_of((rows, wide), BF16),
             shape_of((rows, wide), BF16),
-            shape_of((width, rows), F32),
+            shape_of((width, rows), BF16),
             shape_of((rows, wide), BF16),
             shape_of((rows, wide), BF16),
             shape_of((width, rows), BF16),
@@ -489,15 +489,17 @@
     )(start, own, away, w_own, w_away, bias)
 
 
-def hidden_back_kernel(meta_ref, cot_ref, w1_ref, w2_ref, s1_ref, s2_ref, ge_ref, sum_ref):
-    def part(w_ref, slope_ref):
-        ge = jnp.dot(cot_ref[...], w_ref[...], preferred_element_type=F32) * slope_ref[...].astype(F32)
-        ge_ref[...] = ge.astype(BF16).T
-        sum_ref[...] = jnp.broadcast_to(jnp.sum(ge, axis=0, keepdims=True), sum_ref.shape)
-
-    first = pl.program_id(0) < pl.num_programs(0) // 2
-    pl.when(first)(lambda: part(w1_ref, s1_ref))
-    pl.when(jnp.logical_not(first))(lambda: part(w2_ref, s2_ref))
+def hidden_back_kernel(meta_ref, cot_ref, w1_hbm, w2_hbm, s1_hbm, s2_hbm, ge_ref, sum_ref, w_buf, s_buf, sem):
+    steps, _, tile = w_buf.shape
+
+    def block_of(first, second):
+        return lambda i: (first if i < steps // 2 else second).at[:, pl.ds(i % (steps // 2) * tile, tile)]
+
+    step = pl.program_id(0)
+    stream(step, steps, (block_of(w1_hbm, w2_hbm), block_of(s1_hbm, s2_hbm)), (w_buf, s_buf), sem)
+    ge = jnp.dot(cot_ref[...], w_buf[step], preferred_element_type=F32) * s_buf[step].astype(F32)
+    ge_ref[...] = ge.astype(BF16).T
+    sum_ref[...] = jnp.broadcast_to(jnp.sum(ge, axis=0, keepdims=True), sum_ref.shape)
 
 
 def hidden_back(meta, cot, w_first_t, w_second_t, slope_first, slope_second):
@@ -505,24 +507,21 @@
     rows = cot.shape[0]
     tile = 640
     steps = units // tile
-    first = lambda i: jnp.minimum(i, steps - 1)
-    second = lambda i: jnp.maximum(i - steps, 0)
     place = lambda i, m: jnp.where(i < steps, (1 - m[0]) * steps + i, m[0] * steps + i - steps)
     return pl.pallas_call(
         hidden_back_kernel,
         grid_spec=pltpu.PrefetchScalarGridSpec(
             num_scalar_prefetch=1,
             grid=(2 * steps,),
-            in_specs=[
-                pl.BlockSpec((rows, width), lambda i, m: (0, 0)),
-                pl.BlockSpec((width, tile), lambda i, m: (0, first(i))),
-                pl.BlockSpec((width, tile), lambda i, m: (0, second(i))),
-                pl.BlockSpec((rows, tile), lambda i, m: (0, first(i))),
-                pl.BlockSpec((rows, tile), lambda i, m: (0, second(i))),
-            ],
+            in_specs=[pl.BlockSpec((rows, width), lambda i, m: (0, 0))] + [ANYWHERE] * 4,
             out_specs=[
                 pl.BlockSpec((tile, rows), lambda i, m: (place(i, m), 0)),
                 pl.BlockSpec((8, tile), lambda i, m: (0, place(i, m))),
+            ],
+            scratch_shapes=[
+                pltpu.VMEM((2 * steps, width, tile), BF16),
+                pltpu.VMEM((2 * steps, rows, tile), BF16),
+                pltpu.SemaphoreType.DMA((2, 2 * steps)),
             ],
         ),
         out_shape=[shape_of((2 * units, rows), BF16), shape_of((8, 2 * units), F32)],
@@ -538,7 +537,7 @@
 def middle_kernel(
     meta_ref, g_ref, wo_hbm, wa_hbm, n_hbm, inv_ref, gain_ref, cot_hbm, po_hbm, pa_hbm,
     gm_ref, gmb_ref, ga_ref, s_gain_ref, s_shift_ref, s_bias_ref,
-    acc_ref, prod_ref, wo_buf, wa_buf, n_ref, cot_ref, po_ref, pa_ref, sem, sem_late,
+    acc_ref, prod_ref, wo_buf, wa_buf, n_ref, cot_ref, p_ref, sem, sem_late,
 ):
     side = meta_ref[0]
     width = acc_ref.shape[0]
@@ -550,7 +549,7 @@
     late = [
         pltpu.make_async_copy(src, dst, sem_late.at[j])
         for j, (src, dst) in enumerate(
-            ((n_hbm, n_ref), (cot_hbm, cot_ref), (po_hbm, po_ref), (pa_hbm, pa_ref))
+            ((n_hbm, n_ref), (cot_hbm, cot_ref), (po_hbm, p_ref.at[0]), (pa_hbm, p_ref.at[1]))
         )
     ]
 
@@ -600,10 +599,17 @@
         lax.fori_loop(0, width // ROWS, second, 0)
         g = gmb_ref[...]
         s_bias_ref[...] = row_sums(g)
-        for which, p_ref in ((side, po_ref), (1 - side, pa_ref)):
-            ga_ref[pl.ds(pl.multiple_of(which * half, 16), half), :] = jnp.dot(
-                p_ref[...], g, preferred_element_type=F32
+        part = half // 2
+
+        def attended(j, _):
+            which = jnp.bitwise_xor(j // 2, side)
+            at = pl.multiple_of(j % 2 * part, 16)
+            ga_ref[pl.ds(pl.multiple_of(which * half + at, 16), part), :] = jnp.dot(
+                p_ref[j // 2, pl.ds(at, part), :], gmb_ref[...], preferred_element_type=F32
             ).astype(BF16)
+            return 0
+
+        lax.fori_loop(0, 4, attended, 0)
 
 
 def middle_back(meta, ge, w_own, w_away, normed_t, inv_t, cols, cot_t, p_own, p_away):
@@ -633,8 +639,7 @@
                 pltpu.VMEM((steps, tile, units), BF16),
                 pltpu.VMEM((width, rows), BF16),
                 pltpu.VMEM((width, rows), BF16),
-                pltpu.VMEM((half, width), BF16),
-                pltpu.VMEM((half, width), BF16),
+                pltpu.VMEM((2, half, width), BF16),
                 pltpu.SemaphoreType.DMA((2, steps)),
                 pltpu.SemaphoreType.DMA((4,)),
             ],
@@ -780,7 +785,7 @@
     weights = jnp.concatenate([w1_buf[i], w2_buf[i]], axis=1)
     acts = jnp.concatenate([a1_ref[...], a2_ref[...]], axis=1)
     total = lax.dot_general(weights, acts, NT, preferred_element_type=F32)
-    out_ref[...] = (total + mid_ref[...] + cols_ref[:, 7:8]).astype(BF16)
+    out_ref[...] = (total + mid_ref[...].astype(F32) + cols_ref[:, 7:8]).astype(BF16)
 
 
 def block_output(act_first, act_second, w_away_t, w_own_t, middle_t, cols):
@@ -838,104 +843,128 @@
 SLOTS = 4
 
 
-def spread_kernel(spec, meta_ref, lo_ref, la_ref, ro_ref, ra_ref, *refs):
-    group, which, batch, n_into = spec
-    refs = refs[n_into:]
-    keeps, sends, stages, sem = refs[:3], refs[3:6], refs[6:9], refs[9]
-    count, chunk = group.count, group.chunks[which]
-    step, steps = pl.program_id(0), pl.num_programs(0)
-    rank, first = meta_ref[0], meta_ref[1]
-    padded = group.padded(which)
-    half = count // 2
-
-    def rows_of(k):
-        return pl.ds(group.base(k, which), group.rows(k, which))
-
-    def wait_slot(slot):
-        for k in range(3):
-            pltpu.make_async_copy(
-                stages[k].at[slot], keeps[k].at[0, rows_of(k), :], sem.at[k, slot]
-            ).wait()
-
+def spread_kernel(spec, meta_ref, *refs):
+    group, batches, starts = spec
+    members = len(batches)
+    inputs, refs = refs[: 4 * members], refs[4 * members :]
+    keeps, sends, refs = refs[:3], refs[3:6], refs[6:]
+    step = pl.program_id(0)
+    rank = meta_ref[0]
+    half = group.count // 2
     lanes = group.lanes
-    total = joined_dot(lo_ref[...], la_ref[...], ro_ref[:, :lanes], ra_ref[:, :lanes])
-    for s in range(batch):
-        index = step * batch + s
-        slot = s % SLOTS if batch % SLOTS == 0 else lax.rem(index, SLOTS)
-        if s >= SLOTS:
-            wait_slot(slot)
+
+    def member(which):
+        lo_ref, la_ref, ro_ref, ra_ref = inputs[4 * which : 4 * which + 4]
+        stages, sem = refs[4 * which : 4 * which + 3], refs[4 * which + 3]
+        chunk, batch = group.chunks[which], batches[which]
+        padded = group.padded(which)
+
+        def rows_of(k):
+            return pl.ds(group.base(k, which), group.rows(k, which))
+
+        def wait_slot(slot):
+            for k in range(3):
+                pltpu.make_async_copy(
+                    stages[k].at[slot], keeps[k].at[0, rows_of(k), :], sem.at[k, slot]
+                ).wait()
+
+        def work():
+            local = step - starts[which]
+            total = joined_dot(lo_ref[...], la_ref[...], ro_ref[:, :lanes], ra_ref[:, :lanes])
+            for s in range(batch):
+                index = local * batch + s
+                slot = s % SLOTS if batch % SLOTS == 0 else lax.rem(index, SLOTS)
+                if s >= SLOTS:
+                    wait_slot(slot)
+                else:
+                    pl.when(index >= SLOTS)(lambda slot=slot: wait_slot(slot))
+                mixed = jnp.bitwise_xor(index, rank)
+                part = total[s * chunk : (s + 1) * chunk]
+                for k in range(3):
+                    low, width = group.cuts[k], group.widths[k]
+                    stages[k][slot, :chunk, :] = part[:, low : low + width].astype(BF16)
+                    if k == 2 and group.left_over:
+                        each, pieces = group.each(which), group.pieces
+                        extra = part[:, low + width :]
+                        if pieces * each > chunk:
+                            extra = jnp.concatenate(
+                                [extra, jnp.zeros((pieces * each - chunk, group.left_over), F32)], axis=0
+                            )
+                        extra = jnp.concatenate(
+                            [extra[j * each : (j + 1) * each] for j in range(pieces)], axis=1
+                        )
+                        stages[k][slot, padded : padded + each, :] = extra.astype(BF16)
+                    place = jnp.int32(0)
+                    order = group.orders[k]
+                    for depth, bit in enumerate(order):
+                        place += ((mixed >> bit) & 1) << (len(order) - 1 - depth)
+
+                    @pl.when(place < half)
+                    def _(k=k, slot=slot, place=place):
+                        pltpu.make_async_copy(
+                            stages[k].at[slot], keeps[k].at[place, rows_of(k), :], sem.at[k, slot]
+                        ).start()
+
+                    @pl.when(place >= half)
+                    def _(k=k, slot=slot, place=place):
+                        pltpu.make_async_copy(
+                            stages[k].at[slot], sends[k].at[place - half, rows_of(k), :], sem.at[k, slot]
+                        ).start()
+
+        return work, wait_slot
+
+    parts = [member(which) for which in range(members)]
+    for which, (work, _) in enumerate(parts):
+        if members == 1:
+            work()
         else:
-            pl.when(index >= SLOTS)(lambda slot=slot: wait_slot(slot))
-        mixed = jnp.bitwise_xor(first + index, rank)
-        part = total[s * chunk : (s + 1) * chunk]
-        for k in range(3):
-            low, width = group.cuts[k], group.widths[k]
-            stages[k][slot, :chunk, :] = part[:, low : low + width].astype(BF16)
-            if k == 2 and group.left_over:
-                each, pieces = group.each(which), group.pieces
-                extra = part[:, low + width :]
-                if pieces * each > chunk:
-                    extra = jnp.concatenate(
-                        [extra, jnp.zeros((pieces * each - chunk, group.left_over), F32)], axis=0
-                    )
-                extra = jnp.concatenate([extra[j * each : (j + 1) * each] for j in range(pieces)], axis=1)
-                stages[k][slot, padded : padded + each, :] = extra.astype(BF16)
-            place = jnp.int32(0)
-            order = group.orders[k]
-            for depth, bit in enumerate(order):
-                place += ((mixed >> bit) & 1) << (len(order) - 1 - depth)
-
-            @pl.when(place < half)
-            def _(k=k, slot=slot, place=place):
-                pltpu.make_async_copy(
-                    stages[k].at[slot], keeps[k].at[place, rows_of(k), :], sem.at[k, slot]
-                ).start()
-
-            @pl.when(place >= half)
-            def _(k=k, slot=slot, place=place):
-                pltpu.make_async_copy(
-                    stages[k].at[slot], sends[k].at[place - half, rows_of(k), :], sem.at[k, slot]
-                ).start()
-
-    @pl.when(step == steps - 1)
+            pl.when((step >= starts[which]) & (step < starts[which + 1]))(work)
+
+    @pl.when(step == starts[members] - 1)
     def _():
-        for slot in range(SLOTS):
-            wait_slot(slot)
-
-
-def spread(group, which, meta, lefts, rights, into=None):
-    left_own, left_away = lefts
-    columns, tokens = left_own.shape
-    count, chunk = group.count, group.chunks[which]
-    batch = 1
-    while batch * chunk % 16:
-        batch *= 2
+        for _, wait_slot in parts:
+            for slot in range(SLOTS):
+                wait_slot(slot)
+
+
+def spread(group, meta, lefts, rights):
+    count = group.count
+    batches, starts, specs, scratch, ins = [], [0], [], [], []
+    flops = 0
+    for which, ((left_own, left_away), right) in enumerate(zip(lefts, rights)):
+        columns, tokens = left_own.shape
+        chunk = group.chunks[which]
+        batch = 1
+        while batch * chunk % 16:
+            batch *= 2
+        steps, start = columns // (batch * chunk), starts[-1]
+        left = pl.BlockSpec(
+            (batch * chunk, tokens),
+            lambda i, *_, start=start, steps=steps: (jnp.clip(i - start, 0, steps - 1), 0),
+        )
+        whole = pl.BlockSpec(right[0].shape, lambda i, *_: (0, 0))
+        specs += [left, left, whole, whole]
+        ins += [left_own, left_away, *right]
+        scratch += [pltpu.VMEM((SLOTS, group.rows(k, which), group.widths[k]), BF16) for k in range(3)]
+        scratch.append(pltpu.SemaphoreType.DMA((3, SLOTS)))
+        batches.append(batch)
+        starts.append(start + steps)
+        flops += 4 * columns * tokens * group.lanes
     outs = [shape_of((count // 2, group.total_rows(k), group.widths[k]), BF16) for k in range(3)] * 2
-    extra = list(into) if into is not None else []
-    spec = (group, which, batch, len(extra))
-    anywhere = pl.BlockSpec(memory_space=pl.ANY)
-    left = pl.BlockSpec((batch * chunk, tokens), lambda i, *_: (i, 0))
-    whole = pl.BlockSpec(rights[0].shape, lambda i, *_: (0, 0))
-    return pl.pallas_call(
-        functools.partial(spread_kernel, spec),
+    return pl.pallas_call(
+        functools.partial(spread_kernel, (group, batches, starts)),
         grid_spec=pltpu.PrefetchScalarGridSpec(
             num_scalar_prefetch=1,
-            grid=(columns // (batch * chunk),),
-            in_specs=[left, left, whole, whole] + [anywhere] * len(extra),
-            out_specs=[anywhere] * len(outs),
-            scratch_shapes=[
-                pltpu.VMEM((SLOTS, group.rows(k, which), group.widths[k]), BF16) for k in range(3)
-            ]
-            + [pltpu.SemaphoreType.DMA((3, SLOTS))],
+            grid=(starts[-1],),
+            in_specs=specs,
+            out_specs=[ANYWHERE] * len(outs),
+            scratch_shapes=scratch,
         ),
         out_shape=outs,
-        input_output_aliases={5 + i: i for i in range(len(extra))},
         compiler_params=params(),
-        cost_estimate=cost(
-            4 * columns * tokens * group.lanes, 4 * columns * tokens + 2 * columns * group.lanes
-        ),
+        cost_estimate=cost(flops, flops // 256),
         name="spread",
-    )(meta, left_own, left_away, *rights, *extra)
+    )(meta, *ins)
 
 
 def merge_kernel(*refs):
@@ -1002,7 +1031,7 @@
 
 
 ORDER = (
-    "sc", "hb", "mid", "mc", "e", "p", "ab", "mc", "sh", "me", "mc", "first", "s", "mh", "s", "me",
+    "sc", "hb", "mid", "mc", "e", "ab", "mc", "sh", "me", "mc", "first", "s", "mh", "s", "me",
     "mh", "s", "me", "out", "s", "mc", "s", "mh", "s", "me", "mh",
 )
 
@@ -1110,7 +1139,7 @@
             "e": Group(count, width // 2, [chunk_f, chunk_d], PLANS[1]),
             "h": Group(count, width // 2, [chunk_h], PLANS[2]),
         }
-        meta_all = jnp.stack([rank, jnp.int32(0)]).astype(jnp.int32)
+        rank_of = jnp.reshape(rank, (1,)).astype(jnp.int32)
         state, results = {}, {}
         r = types.SimpleNamespace()
 
@@ -1134,7 +1163,7 @@
 
         def do_contract():
             send("c", held(spread(
-                groups["c"], 0, hold(meta_all), (cot_t, cot_away_t), (act_second, act_away)
+                groups["c"], hold(rank_of), [(cot_t, cot_away_t)], [(act_second, act_away)]
             )))
 
         def do_hidden_back():
@@ -1153,14 +1182,9 @@
             r.gmb_away = swap_group(r.gmb_t)
 
         def do_expand():
-            r.buffers = held(spread(
-                groups["e"], 0, hold(meta_all), (r.ge, r.ge_away), (second_own, r.second_away)
-            ))
-
-        def do_project():
             send("e", held(spread(
-                groups["e"], 1, hold(meta_all), (r.gmb_t, r.gmb_away),
-                (att_own, r.att_away), r.buffers,
+                groups["e"], hold(rank_of), [(r.ge, r.ge_away), (r.gmb_t, r.gmb_away)],
+                [(second_own, r.second_away), (att_own, r.att_away)],
             )))
 
         def do_attend_back():
@@ -1169,7 +1193,7 @@
 
         def do_heads():
             send("h", held(spread(
-                groups["h"], 0, hold(meta_all), (r.gp_t, r.gp_away), (first_own, first_away)
+                groups["h"], hold(rank_of), [(r.gp_t, r.gp_away)], [(first_own, first_away)]
             )))
 
         def do_first():
@@ -1201,7 +1225,7 @@
 
         steps = {
             "sc": do_contract, "hb": do_hidden_back, "mid": do_middle,
-            "e": do_expand, "p": do_project, "ab": do_attend_back,
+            "e": do_expand, "ab": do_attend_back,
             "sh": do_heads, "first": do_first, "out": do_output, "s": do_small,
             "mc": lambda: advance("c"), "me": lambda: advance("e"),
             "mh": lambda: advance("h"),

time: 540 us -> 525 us (0.972)
  the two profiles are of different devices: /device:TPU:0 before, /device:TPU:18 now
where the time goes in v1:
time: 525 us; the launch traced here: 518 us
  Pallas kernels  311 us (59%)
  waiting for transfers between devices  141 us (27%)
  starting transfers between devices  53.3 us (10%)
  local copies, waits for them, and re-layouts  11.6 us (2%)
    ppermute x40, waiting for transfers between devices, exchange(): return lax.ppermute(x, 'rep', [(i, i ^ mask) for i in range(count)])  137 us
    pallas_call x3, Pallas kernels, spread(): pl.pallas_call(functools.partial(spread_kernel, (group, batches, starts))...  62.3 us
    ppermute x40, starting transfers between devices, exchange(): return lax.ppermute(x, 'rep', [(i, i ^ mask) for i in range(count)])  51.6 us
    pallas_call x9, Pallas kernels, merge(): pl.pallas_call(merge_kernel, grid=(half,), in_specs=specs, out_specs=out_...  41.2 us
    pallas_call x1, Pallas kernels, middle_back(): pl.pallas_call(middle_kernel, grid_spec=pltpu.PrefetchScalarGridSpec(num_...  27.7 us
    pallas_call x2, Pallas kernels, hidden(): pl.pallas_call(hidden_kernel, grid_spec=pltpu.PrefetchScalarGridSpec(num_...  27 us
    pallas_call x1, Pallas kernels, attend_back(): pl.pallas_call(functools.partial(attend_back_kernel, width), grid=(seqs,...  22.6 us
    pallas_call x1, Pallas kernels, hidden_back(): pl.pallas_call(hidden_back_kernel, grid_spec=pltpu.PrefetchScalarGridSpec...  21 us
  transfers between devices with their start and end apart: 54, of which 16 were waited for; matrix products, arithmetic and copies ran while one was open for 0% of the time, Pallas kernels for 45%

profile of v1, /device:TPU:18, one launch (start us, length us, event | category | flops | bytes accessed | tf_op | source)
XLA Modules:
  0.0 518.2 jit_solution(15180857638411895039)
XLA Ops:
  4.5 2.3 unpack.1
  6.8 7.0 %prep.1 = (bf16[512,896]{1,0:T(8,128)(2,1)}, bf16[512,896]{1,0:T(8,128)(2,1)}, bf16[512,1600]{1,0:T(8,128)(2,1)}, f32[8,1600]{1,0:T(8,128)}) custom-call(s32[1]{0:T(128)} %bitcast.1.side_ref.meta_ref, bf16[1600,512]{1,0:T(8,128)(2,1)} %bitcast.21, bf16[1600,512]{1,0:T(8,128)(2,1)} %bitcast.17, f32[1600,128]{1,0:T(8,128)} %get-tuple-element.167.cols_ref.gain_ref), custom_call_target="tpu_custom_call" | custom-call | bytes 6553600 | tf_op jit(solution)/shard_map/prep/pallas_call | solution.py:210
  14.0 2.5 collective-permute-done.1.wa_ref.wa_hbm
  16.5 14.1 %heads.1.q_ref.ka_ref.kb_ref.v_ref = bf16[512,4800]{1,0:T(8,128)(2,1)} custom-call(bf16[512,896]{1,0:T(8,128)(2,1)} %get-tuple-element.168.own_ref.refs_2_, bf16[512,896]{1,0:T(8,128)(2,1)} %get-tuple-element.219.away_ref, bf16[800,4800]{1,0:T(8,128)(2,1)} %wo_hbm.3, bf16[800,4800]{1,0:T(8,128)(2,1)} %collective-permute-done.1.wa_ref.wa_hbm, ...), custom_call_target="tpu_custom_call" | custom-call | flops 7864320000 | bytes 20275200 | tf_op jit(solution)/shard_map/heads/pallas_call | solution.py:242
  31.1 16.4 %attend.1 = (bf16[512,1600]{1,0:T(8,128)(2,1)}, f32[512,128]{1,0:T(8,128)}) custom-call(bf16[512,4800]{1,0:T(8,128)(2,1)} %heads.1.q_ref.ka_ref.kb_ref.v_ref, bf16[512,4800]{1,0:T(8,128)(2,1)} %heads.1.q_ref.ka_ref.kb_ref.v_ref, bf16[512,4800]{1,0:T(8,128)(2,1)} %heads.1.q_ref.ka_ref.kb_ref.v_ref, bf16[512,4800]{1,0:T(8,128)(2,1)} %heads.1.q_ref.ka_ref.kb_ref.v_ref), custom_call_target="tpu_custom_call" | custom-call | flops 5033164800 | bytes 6553600 | tf_op jit(solution)/shard_map/attend/pallas_call | solution.py:309
  47.5 10.7 %project.1 = (bf16[512,896]{1,0:T(8,128)(2,1)}, bf16[512,896]{1,0:T(8,128)(2,1)}, bf16[1600,512]{1,0:T(8,128)(2,1)}, bf16[512,896]{1,0:T(8,128)(2,1)}, bf16[512,...) custom-call(s32[1]{0:T(128)} %bitcast.1.side_ref.meta_ref, ...), custom_call_target="tpu_custom_call" | custom-call | flops 2621440000 | bytes 16588800 | tf_op jit(solution)/shard_map/project/pallas_call | solution.py:429
  58.2 13.6 %hidden.2 = (bf16[512,3200]{1,0:T(8,128)(2,1)}, bf16[512,3200]{1,0:T(8,128)(2,1)}) custom-call(s32[1]{0:T(128)} %bitcast.start_ref, bf16[512,896]{1,0:T(8,128)(2,1)} %get-tuple-element.177.so_ref.refs_2_, bf16[512,896]{1,0:T(8,128)(2,1)} %get-tuple-element.178.sa_ref, bf16[800,6400]{1,0:T(8,128)(2,1)} %wo_hbm.2, ...), custom_call_target="tpu_custom_call" | custom-call | flops 5242880000 | bytes 16793600 | tf_op jit(solution)/shard_map/hidden/pallas_call | solution.py:477
  72.3 13.4 %hidden.3 = (bf16[512,3200]{1,0:T(8,128)(2,1)}, bf16[512,3200]{1,0:T(8,128)(2,1)}) custom-call(s32[1]{0:T(128)} %bitcast.5.start_ref, bf16[512,896]{1,0:T(8,128)(2,1)} %get-tuple-element.177.so_ref.refs_2_, bf16[512,896]{1,0:T(8,128)(2,1)} %get-tuple-element.178.sa_ref, bf16[800,6400]{1,0:T(8,128)(2,1)} %wo_hbm.2, ...), custom_call_target="tpu_custom_call" | custom-call | flops 5242880000 | bytes 16793600 | tf_op jit(solution)/shard_map/hidden/pallas_call | solution.py:477
  86.9 17.8 %spread.3 = (bf16[8,112,1152]{2,1,0:T(8,128)(2,1)}, bf16[8,112,1152]{2,1,0:T(8,128)(2,1)}, bf16[8,112,896]{2,1,0:T(8,128)(2,1)}, bf16[8,112,1152]{2,1,0:T(8,128)...) custom-call(s32[1]{0:T(128)} %bitcast.4.meta_ref, bf16[1600,512]{1,0:T(8,128)(2,1)} %bitcast.18, ...), custom_call_target="tpu_custom_call" | custom-call | flops 10485760000 | bytes 40960000 | tf_op jit(solution)/shard_map/spread/pallas_call | solution.py:954
  104.8 21.0 %hback.1 = (bf16[6400,512]{1,0:T(8,128)(2,1)}, f32[8,6400]{1,0:T(8,128)}) custom-call(s32[1]{0:T(128)} %bitcast.1.side_ref.meta_ref, bf16[512,1600]{1,0:T(8,128)(2,1)} %get-tuple-element.188.cot_ref, bf16[1600,3200]{1,0:T(8,128)(2,1)} %collective-permute-done.6.w1_hbm, bf16[1600,3200]{1,0:T(8,128)(2,1)} %bitcast.27, ...), custom_call_target="tpu_custom_call" | custom-call | flops 10485760000 | bytes 33587200 | tf_op jit(solution)/shard_map/hback/pallas_call | solution.py:511
  129.6 27.7 %middle.1 = (f32[1600,512]{1,0:T(8,128)}, bf16[1600,512]{1,0:T(8,128)(2,1)}, bf16[1600,512]{1,0:T(8,128)(2,1)}, f32[8,1600]{1,0:T(8,128)}, f32[8,1600]{1,0:T(8,128)}, /*index=5*/f32[8,1600]{1,0:T(8,128)}) custom-call(s32[1]{0:T(128)} %bitcast.1.side_ref.meta_ref, bf16[6400,512]{1,0:T(8,128)(2,1)} %get-tuple-element.192.g_ref.refs_0_, ...), custom_call_target="tpu_custom_call" | custom-call | flops 13107200000 | bytes 30310400 | tf_op jit(solution)/shard_map/middle/pallas_call | solution.py:625
  157.4 6.6 %collective-permute-done.9.refs_9_.refs_11_ = bf16[8,112,896]{2,1,0:T(8,128)(2,1)} collective-permute-done((bf16[8,112,896]{2,1,0:T(8,128)(2,1)}, bf16[8,112,896]{2,1,0:T(8,128)(2,1)}, u32[]{:S(2)}, u32[]{:S(2)}) %collective-permute-start.9) | collective-permute-done | bytes 1605664 | tf_op jit(solution)/shard_map/ppermute | solution.py:45
  164.0 9.4 %collective-permute-done.7.refs_1_.refs_3_ = bf16[8,112,1152]{2,1,0:T(8,128)(2,1)S(1)} collective-permute-done((bf16[8,112,1152]{2,1,0:T(8,128)(2,1)}, bf16[8,112,1152]{2,1,0:T(8,128)(2,1)S(1)}, u32[]{:S(2)}, u32[]{:S(2)}) %collective-permute-start.7) | collective-permute-done | bytes 2064416 | tf_op jit(solution)/shard_map/ppermute | solution.py:45
  176.3 7.2 %merge.9 = (bf16[4,112,1152]{2,1,0:T(8,128)(2,1)}, bf16[4,112,1152]{2,1,0:T(8,128)(2,1)}, bf16[4,112,896]{2,1,0:T(8,128)(2,1)}, bf16[4,112,1152]{2,1,0:T(8,128)(...) custom-call(bf16[8,112,1152]{2,1,0:T(8,128)(2,1)} %get-tuple-element.197.refs_0_.refs_2_, ...), custom_call_target="tpu_custom_call" | custom-call | bytes 17203200 | tf_op jit(solution)/shard_map/merge/pallas_call | solution.py:991
  183.6 28.5 %spread.4 = (bf16[8,512,256]{2,1,0:T(8,128)(2,1)}, bf16[8,512,256]{2,1,0:T(8,128)(2,1)}, bf16[8,592,256]{2,1,0:T(8,128)(2,1)}, bf16[8,512,256]{2,1,0:T(8,128)(2,...) custom-call(s32[1]{0:T(128)} %bitcast.4.meta_ref, bf16[6400,512]{1,0:T(8,128)(2,1)} %get-tuple-element.192.g_ref.refs_0_, ...), custom_call_target="tpu_custom_call" | custom-call | flops 13107200000 | bytes 51200000 | tf_op jit(solution)/shard_map/spread/pallas_call | solution.py:954
  212.1 22.6 %aback.1 = bf16[3,1600,512]{2,1,0:T(8,128)(2,1)} custom-call(bf16[512,4800]{1,0:T(8,128)(2,1)} %heads.1.q_ref.ka_ref.kb_ref.v_ref, bf16[512,4800]{1,0:T(8,128)(2,1)} %heads.1.q_ref.ka_ref.kb_ref.v_ref, bf16[512,4800]{1,0:T(8,128)(2,1)} %heads.1.q_ref.ka_ref.kb_ref.v_ref, bf16[512,4800]{1,0:T(8,128)(2,1)} %heads.1.q_ref.ka_ref.kb_ref.v_ref, ...), custom_call_target="tpu_custom_call" | custom-call | flops 5033164800 | bytes 11468800 | tf_op jit(solution)/shard_map/aback/pallas_call | solution.py:381
  239.8 16.8 %collective-permute-done.16.refs_9_.refs_11_ = bf16[4,112,896]{2,1,0:T(8,128)(2,1)S(1)} collective-permute-done((bf16[4,112,896]{2,1,0:T(8,128)(2,1)}, bf16[4,112,896]{2,1,0:T(8,128)(2,1)S(1)}, u32[]{:S(2)}, u32[]{:S(2)}) %collective-permute-start.16) | collective-permute-done | bytes 802848 | tf_op jit(solution)/shard_map/ppermute | solution.py:45
  256.7 4.0 collective-permute-done.14.refs_1_.refs_3_
  263.7 4.1 merge.10
  268.4 16.0 %spread.5 = (bf16[8,304,384]{2,1,0:T(8,128)(2,1)}, bf16[8,304,256]{2,1,0:T(8,128)(2,1)}, bf16[8,384,128]{2,1,0:T(8,128)(2,1)}, bf16[8,304,384]{2,1,0:T(8,128)(2,...) custom-call(s32[1]{0:T(128)} %bitcast.4.meta_ref, bf16[4800,512]{1,0:T(8,128)(2,1)} %bitcast.15, ...), custom_call_target="tpu_custom_call" | custom-call | flops 7864320000 | bytes 30720000 | tf_op jit(solution)/shard_map/spread/pallas_call | solution.py:954
  285.9 32.0 %collective-permute-done.24.refs_9_.refs_11_ = bf16[2,112,896]{2,1,0:T(8,128)(2,1)S(1)} collective-permute-done((bf16[2,112,896]{2,1,0:T(8,128)(2,1)}, bf16[2,112,896]{2,1,0:T(8,128)(2,1)S(1)}, u32[]{:S(2)}, u32[]{:S(2)}) %collective-permute-start.24) | collective-permute-done | bytes 401440 | tf_op jit(solution)/shard_map/ppermute | solution.py:45
  323.0 7.8 %merge.11 = (bf16[4,512,256]{2,1,0:T(8,128)(2,1)}, bf16[4,512,256]{2,1,0:T(8,128)(2,1)}, bf16[4,592,256]{2,1,0:T(8,128)(2,1)}, bf16[4,512,256]{2,1,0:T(8,128)(2,...) custom-call(bf16[8,512,256]{2,1,0:T(8,128)(2,1)} %get-tuple-element.221.refs_0_.refs_2_, ...), custom_call_target="tpu_custom_call" | custom-call | bytes 19857408 | tf_op jit(solution)/shard_map/merge/pallas_call | solution.py:991
  330.9 2.8 collective-permute-done.22.refs_1_.refs_3_
  333.6 11.7 %collective-permute-done.23.refs_5_.refs_7_ = bf16[2,112,1152]{2,1,0:T(8,128)(2,1)} collective-permute-done((bf16[2,112,1152]{2,1,0:T(8,128)(2,1)}, bf16[2,112,1152]{2,1,0:T(8,128)(2,1)}, u32[]{:S(2)}, u32[]{:S(2)}) %collective-permute-start.23) | collective-permute-done | bytes 516128 | tf_op jit(solution)/shard_map/ppermute | solution.py:45
  345.3 3.1 merge.12
  351.9 20.7 %first.1 = (bf16[1600,512]{1,0:T(8,128)(2,1)}, f32[8,1600]{1,0:T(8,128)}, f32[8,1600]{1,0:T(8,128)}, f32[8,4800]{1,0:T(8,128)}) custom-call(s32[1]{0:T(128)} %bitcast.1.side_ref.meta_ref, bf16[4800,512]{1,0:T(8,128)(2,1)} %bitcast.16, bf16[800,4800]{1,0:T(8,128)(2,1)} %wo_hbm.3, bf16[800,4800]{1,0:T(8,128)(2,1)} %collective-permute-done.1.wa_ref.wa_hbm, ...), custom_call_target="tpu_custom_call" | custom-call | flops 7864320000 | bytes 28467200 | tf_op jit(solution)/shard_map/first/pallas_call | solution.py:747
  372.7 2.0 collect.1
  375.7 5.7 %merge.13 = (bf16[4,304,384]{2,1,0:T(8,128)(2,1)}, bf16[4,304,256]{2,1,0:T(8,128)(2,1)}, bf16[4,384,128]{2,1,0:T(8,128)(2,1)}, bf16[4,304,384]{2,1,0:T(8,128)(2,...) custom-call(bf16[8,304,384]{2,1,0:T(8,128)(2,1)} %get-tuple-element.247.refs_0_.refs_2_, ...), custom_call_target="tpu_custom_call" | custom-call | bytes 11698176 | tf_op jit(solution)/shard_map/merge/pallas_call | solution.py:991
  387.0 4.4 merge.14
  393.3 20.4 %collective-permute-done.34.refs_9_.refs_11_ = bf16[4,384,128]{2,1,0:T(8,128)(2,1)S(1)} collective-permute-done((bf16[4,384,128]{2,1,0:T(8,128)(2,1)}, bf16[4,384,128]{2,1,0:T(8,128)(2,1)S(1)}, u32[]{:S(2)}, u32[]{:S(2)}) %collective-permute-start.34) | collective-permute-done | bytes 393248 | tf_op jit(solution)/shard_map/ppermute | solution.py:45
  416.5 3.3 merge.15
  419.7 2.3 collective-permute-done.35.b_ref
  423.8 3.9 collective-permute-start.39
  427.7 2.9 collective-permute-start.40
  431.6 3.1 merge.16
  436.8 18.0 %output.1 = bf16[1600,512]{1,0:T(8,128)(2,1)} custom-call(bf16[512,3200]{1,0:T(8,128)(2,1)} %get-tuple-element.278.a1_ref, bf16[512,3200]{1,0:T(8,128)(2,1)} %get-tuple-element.183.refs_2_.a2_ref, bf16[1600,3200]{1,0:T(8,128)(2,1)} %collective-permute-done.6.w1_hbm, bf16[1600,3200]{1,0:T(8,128)(2,1)} %bitcast.28, ...), custom_call_target="tpu_custom_call" | custom-call | flops 10485760000 | bytes 31948800 | tf_op jit(solution)/shard_map/output/pallas_call | solution.py:798
  454.9 1.8 add.6.a_ref
  458.7 2.6 collective-permute-start.48
  462.6 2.7 collective-permute-start.50
  465.3 2.6 finish.3
  472.3 2.6 merge.17
  474.8 2.6 collective-permute-start.51
  477.5 12.2 %collective-permute-done.48.refs_1_ = bf16[1,512,256]{2,1,0:T(8,128)(2,1)S(1)} collective-permute-done((bf16[1,512,256]{2,1,0:T(8,128)(2,1)S(1)}, bf16[1,512,256]{2,1,0:T(8,128)(2,1)S(1)}, u32[]{:S(2)}, u32[]{:S(2)}) %collective-permute-start.48) | collective-permute-done | bytes 262176 | tf_op jit(solution)/shard_map/ppermute | solution.py:45
  489.6 3.4 collective-permute-start.52
  495.4 11.8 %collective-permute-done.49.refs_3_ = bf16[1,512,256]{2,1,0:T(8,128)(2,1)S(1)} collective-permute-done((bf16[1,512,256]{2,1,0:T(8,128)(2,1)S(1)}, bf16[1,512,256]{2,1,0:T(8,128)(2,1)S(1)}, u32[]{:S(2)}, u32[]{:S(2)}) %collective-permute-start.49) | collective-permute-done | bytes 262176 | tf_op jit(solution)/shard_map/ppermute | solution.py:45
  508.0 2.8 finish.4
  510.8 4.2 collective-permute-done.53.refs_5_
  515.8 2.4 finish.5
  (172 shorter events, 59.7 us)
Async XLA Ops:
  3.9 12.6 %collective-permute-start.1 = (bf16[800,4800]{1,0:T(8,128)(2,1)}, bf16[800,4800]{1,0:T(8,128)(2,1)}, u32[]{:S(2)}, u32[]{:S(2)}) collective-permute-start(bf16[800,4800]{1,0:T(8,128)(2,1)} %wo_hbm.3), channel_id=1, source_target_pairs={{0,1},{1,0},{2,3},{3,2},{4,5},{5,4},{6,7},{7,6},{8,9},{9,8},{10,11... | collective-permute-start | bytes 23040008 | tf_op jit(solution)/shard_map/ppermute | solution.py:41
  13.8 16.8 %collective-permute-start.2 = (bf16[800,1600]{1,0:T(8,128)(2,1)S(1)}, bf16[800,1600]{1,0:T(8,128)(2,1)}, u32[]{:S(2)}, u32[]{:S(2)}) collective-permute-start(bf16[800,1600]{1,0:T(8,128)(2,1)S(1)} %copy-done.33), channel_id=1, source_target_pairs={{0,1},{1,0},{2,3},{3,2},{4,5},{5,4},{6,7},{7,6},{8,9},{9,8},{10,11... | collective-permute-start | bytes 7680008 | tf_op jit(solution)/shard_map/ppermute | solution.py:41
  30.6 27.6 %collective-permute-start.3 = (bf16[800,6400]{1,0:T(8,128)(2,1)}, bf16[800,6400]{1,0:T(8,128)(2,1)}, u32[]{:S(2)}, u32[]{:S(2)}) collective-permute-start(bf16[800,6400]{1,0:T(8,128)(2,1)} %wo_hbm.2), channel_id=1, source_target_pairs={{0,1},{1,0},{2,3},{3,2},{4,5},{5,4},{6,7},{7,6},{8,9},{9,8},{10,11... | collective-permute-start | bytes 30720008 | tf_op jit(solution)/shard_map/ppermute | solution.py:41
  30.7 74.1 %collective-permute-start.6 = (bf16[1600,3200]{1,0:T(8,128)(2,1)}, bf16[1600,3200]{1,0:T(8,128)(2,1)}, u32[]{:S(2)}, u32[]{:S(2)}) collective-permute-start(bf16[1600,3200]{1,0:T(8,128)(2,1)} %bitcast.26), channel_id=1, source_target_pairs={{0,1},{1,0},{2,3},{3,2},{4,5},{5,4},{6,7},{7,6},{8,9},{9,8},{10,11... | collective-permute-start | bytes 30720008 | tf_op jit(solution)/shard_map/ppermute | solution.py:41
  71.8 14.0 %collective-permute-start.5 = (bf16[512,3200]{1,0:T(8,128)(2,1)}, bf16[512,3200]{1,0:T(8,128)(2,1)}, u32[]{:S(2)}, u32[]{:S(2)}) collective-permute-start(bf16[512,3200]{1,0:T(8,128)(2,1)} %get-tuple-element.278.a1_ref), channel_id=1, source_target_pairs={{0,1},{1,0},{2,3},{3,2},{4,5},{5,4},{6,7},{7,6},{8,9},{9,8},{10,11... | collective-permute-start | bytes 9830408 | tf_op jit(solution)/shard_map/ppermute | solution.py:41
  72.0 13.8 %collective-permute-start.4 = (bf16[1600,512]{1,0:T(8,128)(2,1)S(1)}, bf16[1600,512]{1,0:T(8,128)(2,1)S(1)}, u32[]{:S(2)}, u32[]{:S(2)}) collective-permute-start(bf16[1600,512]{1,0:T(8,128)(2,1)S(1)} %bitcast.20), channel_id=1, source_target_pairs={{0,1},{1,0},{2,3},{3,2},{4,5},{5,4},{6,7},{7,6},{8,9},{9,8},{10,11... | collective-permute-start | bytes 4915208 | tf_op jit(solution)/shard_map/ppermute | solution.py:41
  125.8 57.7 %collective-permute-start.10 = (bf16[6400,512]{1,0:T(8,128)(2,1)}, bf16[6400,512]{1,0:T(8,128)(2,1)}, u32[]{:S(2)}, u32[]{:S(2)}) collective-permute-start(bf16[6400,512]{1,0:T(8,128)(2,1)} %get-tuple-element.192.g_ref.refs_0_), channel_id=1, source_target_pairs={{0,1},{1,0},{2,3},{3,2},{4,5},{5,4},{6,7},{7,6},{8,9},{9,8},{10,11... | collective-permute-start | bytes 19660808 | tf_op jit(solution)/shard_map/ppermute | solution.py:41
  126.0 47.4 %collective-permute-start.7 = (bf16[8,112,1152]{2,1,0:T(8,128)(2,1)}, bf16[8,112,1152]{2,1,0:T(8,128)(2,1)S(1)}, u32[]{:S(2)}, u32[]{:S(2)}) collective-permute-start(bf16[8,112,1152]{2,1,0:T(8,128)(2,1)} %get-tuple-element.198), channel_id=1, source_target_pairs={{0,2},{2,0},{4,6},{6,4},{8,10},{10,8},{12,14},{14,12},{16,18},{18,... | collective-permute-start | bytes 6193160 | tf_op jit(solution)/shard_map/ppermute | solution.py:45
  126.6 37.4 %collective-permute-start.9 = (bf16[8,112,896]{2,1,0:T(8,128)(2,1)}, bf16[8,112,896]{2,1,0:T(8,128)(2,1)}, u32[]{:S(2)}, u32[]{:S(2)}) collective-permute-start(bf16[8,112,896]{2,1,0:T(8,128)(2,1)} %get-tuple-element.202), channel_id=1, source_target_pairs={{0,8},{2,10},{4,12},{6,14},{8,0},{10,2},{12,4},{14,6},{16,24},{18,... | collective-permute-start | bytes 4816904 | tf_op jit(solution)/shard_map/ppermute | solution.py:45
  128.1 46.9 %collective-permute-start.8 = (bf16[8,112,1152]{2,1,0:T(8,128)(2,1)}, bf16[8,112,1152]{2,1,0:T(8,128)(2,1)S(1)}, u32[]{:S(2)}, u32[]{:S(2)}) collective-permute-start(bf16[8,112,1152]{2,1,0:T(8,128)(2,1)} %get-tuple-element.200), channel_id=1, source_target_pairs={{0,4},{2,6},{4,0},{6,2},{8,12},{10,14},{12,8},{14,10},{16,20},{18,... | collective-permute-start | bytes 6193160 | tf_op jit(solution)/shard_map/ppermute | solution.py:45
  157.3 26.2 %collective-permute-start.12 = (bf16[1600,512]{1,0:T(8,128)(2,1)}, bf16[1600,512]{1,0:T(8,128)(2,1)}, u32[]{:S(2)}, u32[]{:S(2)}) collective-permute-start(bf16[1600,512]{1,0:T(8,128)(2,1)} %get-tuple-element.205.refs_4_), channel_id=1, source_target_pairs={{0,1},{1,0},{2,3},{3,2},{4,5},{5,4},{6,7},{7,6},{8,9},{9,8},{10,11... | collective-permute-start | bytes 4915208 | tf_op jit(solution)/shard_map/ppermute | solution.py:41
  164.0 19.5 %collective-permute-start.13 = (bf16[512,896]{1,0:T(8,128)(2,1)}, bf16[512,896]{1,0:T(8,128)(2,1)}, u32[]{:S(2)}, u32[]{:S(2)}) collective-permute-start(bf16[512,896]{1,0:T(8,128)(2,1)} %get-tuple-element.206), channel_id=1, source_target_pairs={{0,1},{1,0},{2,3},{3,2},{4,5},{5,4},{6,7},{7,6},{8,9},{9,8},{10,11... | collective-permute-start | bytes 2752520 | tf_op jit(solution)/shard_map/ppermute | solution.py:41
  234.7 33.7 %collective-permute-start.17 = (bf16[4800,512]{1,0:T(8,128)(2,1)}, bf16[4800,512]{1,0:T(8,128)(2,1)}, u32[]{:S(2)}, u32[]{:S(2)}) collective-permute-start(bf16[4800,512]{1,0:T(8,128)(2,1)} %bitcast.14), channel_id=1, source_target_pairs={{0,1},{1,0},{2,3},{3,2},{4,5},{5,4},{6,7},{7,6},{8,9},{9,8},{10,11... | collective-permute-start | bytes 14745608 | tf_op jit(solution)/shard_map/ppermute | solution.py:41
  234.7 26.0 %collective-permute-start.14 = (bf16[4,112,1152]{2,1,0:T(8,128)(2,1)}, bf16[4,112,1152]{2,1,0:T(8,128)(2,1)S(1)}, u32[]{:S(2)}, u32[]{:S(2)}) collective-permute-start(bf16[4,112,1152]{2,1,0:T(8,128)(2,1)} %get-tuple-element.212), channel_id=1, source_target_pairs={{0,8},{2,10},{4,12},{6,14},{8,0},{10,2},{12,4},{14,6},{16,24},{18,... | collective-permute-start | bytes 3096584 | tf_op jit(solution)/shard_map/ppermute | solution.py:45
  235.5 26.7 %collective-permute-start.15 = (bf16[4,112,1152]{2,1,0:T(8,128)(2,1)}, bf16[4,112,1152]{2,1,0:T(8,128)(2,1)}, u32[]{:S(2)}, u32[]{:S(2)}) collective-permute-start(bf16[4,112,1152]{2,1,0:T(8,128)(2,1)} %get-tuple-element.214), channel_id=1, source_target_pairs={{0,2},{2,0},{4,6},{6,4},{8,10},{10,8},{12,14},{14,12},{16,18},{18,... | collective-permute-start | bytes 3096584 | tf_op jit(solution)/shard_map/ppermute | solution.py:45
  236.8 19.9 %collective-permute-start.16 = (bf16[4,112,896]{2,1,0:T(8,128)(2,1)}, bf16[4,112,896]{2,1,0:T(8,128)(2,1)S(1)}, u32[]{:S(2)}, u32[]{:S(2)}) collective-permute-start(bf16[4,112,896]{2,1,0:T(8,128)(2,1)} %get-tuple-element.216), channel_id=1, source_target_pairs={{0,4},{2,6},{4,0},{6,2},{8,12},{10,14},{12,8},{14,10},{16,20},{18,... | collective-permute-start | bytes 2408456 | tf_op jit(solution)/shard_map/ppermute | solution.py:45
  238.3 83.3 %collective-permute-start.21 = (bf16[8,592,256]{2,1,0:T(8,128)(2,1)}, bf16[8,592,256]{2,1,0:T(8,128)(2,1)S(1)}, u32[]{:S(2)}, u32[]{:S(2)}) collective-permute-start(bf16[8,592,256]{2,1,0:T(8,128)(2,1)} %get-tuple-element.226), channel_id=1, source_target_pairs={{0,8},{2,10},{4,12},{6,14},{8,0},{10,2},{12,4},{14,6},{16,24},{18,... | collective-permute-start | bytes 7274504 | tf_op jit(solution)/shard_map/ppermute | solution.py:45
  260.7 58.0 %collective-permute-start.19 = (bf16[8,512,256]{2,1,0:T(8,128)(2,1)}, bf16[8,512,256]{2,1,0:T(8,128)(2,1)}, u32[]{:S(2)}, u32[]{:S(2)}) collective-permute-start(bf16[8,512,256]{2,1,0:T(8,128)(2,1)} %get-tuple-element.222), channel_id=1, source_target_pairs={{0,2},{2,0},{4,6},{6,4},{8,10},{10,8},{12,14},{14,12},{16,18},{18,... | collective-permute-start | bytes 6291464 | tf_op jit(solution)/shard_map/ppermute | solution.py:45
  262.2 58.0 %collective-permute-start.20 = (bf16[8,512,256]{2,1,0:T(8,128)(2,1)}, bf16[8,512,256]{2,1,0:T(8,128)(2,1)}, u32[]{:S(2)}, u32[]{:S(2)}) collective-permute-start(bf16[8,512,256]{2,1,0:T(8,128)(2,1)} %get-tuple-element.224), channel_id=1, source_target_pairs={{0,4},{2,6},{4,0},{6,2},{8,12},{10,14},{12,8},{14,10},{16,20},{18,... | collective-permute-start | bytes 6291464 | tf_op jit(solution)/shard_map/ppermute | solution.py:45
  267.8 50.2 %collective-permute-start.24 = (bf16[2,112,896]{2,1,0:T(8,128)(2,1)}, bf16[2,112,896]{2,1,0:T(8,128)(2,1)S(1)}, u32[]{:S(2)}, u32[]{:S(2)}) collective-permute-start(bf16[2,112,896]{2,1,0:T(8,128)(2,1)} %get-tuple-element.233), channel_id=1, source_target_pairs={{0,2},{2,0},{4,6},{6,4},{8,10},{10,8},{12,14},{14,12},{16,18},{18,... | collective-permute-start | bytes 1204232 | tf_op jit(solution)/shard_map/ppermute | solution.py:45
  284.4 90.3 %collective-permute-start.25 = (bf16[8,304,384]{2,1,0:T(8,128)(2,1)}, bf16[8,304,384]{2,1,0:T(8,128)(2,1)}, u32[]{:S(2)}, u32[]{:S(2)}) collective-permute-start(bf16[8,304,384]{2,1,0:T(8,128)(2,1)} %get-tuple-element.248), channel_id=1, source_target_pairs={{0,2},{2,0},{4,6},{6,4},{8,10},{10,8},{12,14},{14,12},{16,18},{18,... | collective-permute-start | bytes 5603336 | tf_op jit(solution)/shard_map/ppermute | solution.py:45
  318.0 32.6 %collective-permute-start.27 = (bf16[8,384,128]{2,1,0:T(8,128)(2,1)}, bf16[8,384,128]{2,1,0:T(8,128)(2,1)}, u32[]{:S(2)}, u32[]{:S(2)}) collective-permute-start(bf16[8,384,128]{2,1,0:T(8,128)(2,1)} %get-tuple-element.252), channel_id=1, source_target_pairs={{0,8},{2,10},{4,12},{6,14},{8,0},{10,2},{12,4},{14,6},{16,24},{18,... | collective-permute-start | bytes 2359304 | tf_op jit(solution)/shard_map/ppermute | solution.py:45
  318.7 14.9 %collective-permute-start.22 = (bf16[2,112,1152]{2,1,0:T(8,128)(2,1)}, bf16[2,112,1152]{2,1,0:T(8,128)(2,1)}, u32[]{:S(2)}, u32[]{:S(2)}) collective-permute-start(bf16[2,112,1152]{2,1,0:T(8,128)(2,1)} %get-tuple-element.229), channel_id=1, source_target_pairs={{0,4},{2,6},{4,0},{6,2},{8,12},{10,14},{12,8},{14,10},{16,20},{18,... | collective-permute-start | bytes 1548296 | tf_op jit(solution)/shard_map/ppermute | solution.py:45
  320.2 25.1 %collective-permute-start.23 = (bf16[2,112,1152]{2,1,0:T(8,128)(2,1)}, bf16[2,112,1152]{2,1,0:T(8,128)(2,1)}, u32[]{:S(2)}, u32[]{:S(2)}) collective-permute-start(bf16[2,112,1152]{2,1,0:T(8,128)(2,1)} %get-tuple-element.231), channel_id=1, source_target_pairs={{0,8},{2,10},{4,12},{6,14},{8,0},{10,2},{12,4},{14,6},{16,24},{18,... | collective-permute-start | bytes 1548296 | tf_op jit(solution)/shard_map/ppermute | solution.py:45
  321.6 53.1 %collective-permute-start.26 = (bf16[8,304,256]{2,1,0:T(8,128)(2,1)}, bf16[8,304,256]{2,1,0:T(8,128)(2,1)S(1)}, u32[]{:S(2)}, u32[]{:S(2)}) collective-permute-start(bf16[8,304,256]{2,1,0:T(8,128)(2,1)} %get-tuple-element.250), channel_id=1, source_target_pairs={{0,4},{2,6},{4,0},{6,2},{8,12},{10,14},{12,8},{14,10},{16,20},{18,... | collective-permute-start | bytes 3735560 | tf_op jit(solution)/shard_map/ppermute | solution.py:45
  348.4 34.3 %collective-permute-start.29 = (bf16[4,512,256]{2,1,0:T(8,128)(2,1)}, bf16[4,512,256]{2,1,0:T(8,128)(2,1)}, u32[]{:S(2)}, u32[]{:S(2)}) collective-permute-start(bf16[4,512,256]{2,1,0:T(8,128)(2,1)} %get-tuple-element.257), channel_id=1, source_target_pairs={{0,4},{2,6},{4,0},{6,2},{8,12},{10,14},{12,8},{14,10},{16,20},{18,... | collective-permute-start | bytes 3145736 | tf_op jit(solution)/shard_map/ppermute | solution.py:45
  349.9 36.0 %collective-permute-start.30 = (bf16[4,512,256]{2,1,0:T(8,128)(2,1)}, bf16[4,512,256]{2,1,0:T(8,128)(2,1)}, u32[]{:S(2)}, u32[]{:S(2)}) collective-permute-start(bf16[4,512,256]{2,1,0:T(8,128)(2,1)} %get-tuple-element.259), channel_id=1, source_target_pairs={{0,8},{2,10},{4,12},{6,14},{8,0},{10,2},{12,4},{14,6},{16,24},{18,... | collective-permute-start | bytes 3145736 | tf_op jit(solution)/shard_map/ppermute | solution.py:45
  350.6 35.3 %collective-permute-start.31 = (bf16[4,592,256]{2,1,0:T(8,128)(2,1)}, bf16[4,592,256]{2,1,0:T(8,128)(2,1)S(1)}, u32[]{:S(2)}, u32[]{:S(2)}) collective-permute-start(bf16[4,592,256]{2,1,0:T(8,128)(2,1)} %get-tuple-element.261), channel_id=1, source_target_pairs={{0,2},{2,0},{4,6},{6,4},{8,10},{10,8},{12,14},{14,12},{16,18},{18,... | collective-permute-start | bytes 3637256 | tf_op jit(solution)/shard_map/ppermute | solution.py:45
  381.4 34.2 %collective-permute-start.32 = (bf16[4,304,384]{2,1,0:T(8,128)(2,1)}, bf16[4,304,384]{2,1,0:T(8,128)(2,1)S(1)}, u32[]{:S(2)}, u32[]{:S(2)}) collective-permute-start(bf16[4,304,384]{2,1,0:T(8,128)(2,1)} %get-tuple-element.264), channel_id=1, source_target_pairs={{0,4},{2,6},{4,0},{6,2},{8,12},{10,14},{12,8},{14,10},{16,20},{18,... | collective-permute-start | bytes 2801672 | tf_op jit(solution)/shard_map/ppermute | solution.py:45
  382.0 33.2 %collective-permute-start.33 = (bf16[4,304,256]{2,1,0:T(8,128)(2,1)}, bf16[4,304,256]{2,1,0:T(8,128)(2,1)S(1)}, u32[]{:S(2)}, u32[]{:S(2)}) collective-permute-start(bf16[4,304,256]{2,1,0:T(8,128)(2,1)} %get-tuple-element.266), channel_id=1, source_target_pairs={{0,2},{2,0},{4,6},{6,4},{8,10},{10,8},{12,14},{14,12},{16,18},{18,... | collective-permute-start | bytes 1867784 | tf_op jit(solution)/shard_map/ppermute | solution.py:45
  382.7 30.9 %collective-permute-start.34 = (bf16[4,384,128]{2,1,0:T(8,128)(2,1)}, bf16[4,384,128]{2,1,0:T(8,128)(2,1)S(1)}, u32[]{:S(2)}, u32[]{:S(2)}) collective-permute-start(bf16[4,384,128]{2,1,0:T(8,128)(2,1)} %get-tuple-element.268), channel_id=1, source_target_pairs={{0,4},{2,6},{4,0},{6,2},{8,12},{10,14},{12,8},{14,10},{16,20},{18,... | collective-permute-start | bytes 1179656 | tf_op jit(solution)/shard_map/ppermute | solution.py:45
  391.4 39.3 %collective-permute-start.38 = (bf16[2,592,256]{2,1,0:T(8,128)(2,1)}, bf16[2,592,256]{2,1,0:T(8,128)(2,1)S(1)}, u32[]{:S(2)}, u32[]{:S(2)}) collective-permute-start(bf16[2,592,256]{2,1,0:T(8,128)(2,1)} %get-tuple-element.276), channel_id=1, source_target_pairs={{0,4},{2,6},{4,0},{6,2},{8,12},{10,14},{12,8},{14,10},{16,20},{18,... | collective-permute-start | bytes 1818632 | tf_op jit(solution)/shard_map/ppermute | solution.py:45
  391.9 35.7 %collective-permute-start.36 = (bf16[2,512,256]{2,1,0:T(8,128)(2,1)}, bf16[2,512,256]{2,1,0:T(8,128)(2,1)S(1)}, u32[]{:S(2)}, u32[]{:S(2)}) collective-permute-start(bf16[2,512,256]{2,1,0:T(8,128)(2,1)} %get-tuple-element.272), channel_id=1, source_target_pairs={{0,8},{2,10},{4,12},{6,14},{8,0},{10,2},{12,4},{14,6},{16,24},{18,... | collective-permute-start | bytes 1572872 | tf_op jit(solution)/shard_map/ppermute | solution.py:45
  414.4 16.2 %collective-permute-start.37 = (bf16[2,512,256]{2,1,0:T(8,128)(2,1)}, bf16[2,512,256]{2,1,0:T(8,128)(2,1)S(1)}, u32[]{:S(2)}, u32[]{:S(2)}) collective-permute-start(bf16[2,512,256]{2,1,0:T(8,128)(2,1)} %get-tuple-element.274), channel_id=1, source_target_pairs={{0,2},{2,0},{4,6},{6,4},{8,10},{10,8},{12,14},{14,12},{16,18},{18,... | collective-permute-start | bytes 1572872 | tf_op jit(solution)/shard_map/ppermute | solution.py:45
  423.8 11.8 %collective-permute-start.39 = (f32[16,3200]{1,0:T(8,128)}, f32[16,3200]{1,0:T(8,128)S(1)}, u32[]{:S(2)}, u32[]{:S(2)}) collective-permute-start(f32[16,3200]{1,0:T(8,128)} %add.5.a_ref), channel_id=1, source_target_pairs={{0,8},{2,10},{4,12},{6,14},{8,0},{10,2},{12,4},{14,6},{16,24},{18,... | collective-permute-start | bytes 614408 | tf_op jit(solution)/shard_map/ppermute | solution.py:45
  427.6 29.0 %collective-permute-start.42 = (bf16[1,112,896]{2,1,0:T(8,128)(2,1)}, bf16[1,112,896]{2,1,0:T(8,128)(2,1)S(1)}, u32[]{:S(2)}, u32[]{:S(2)}) collective-permute-start(bf16[1,112,896]{2,1,0:T(8,128)(2,1)} %get-tuple-element.286), channel_id=1, source_target_pairs={{0,16},{2,18},{4,20},{6,22},{8,24},{10,26},{12,28},{14,30},{16,0},... | collective-permute-start | bytes 602120 | tf_op jit(solution)/shard_map/ppermute | solution.py:45
  427.7 29.5 %collective-permute-start.40 = (bf16[1,112,1152]{2,1,0:T(8,128)(2,1)}, bf16[1,112,1152]{2,1,0:T(8,128)(2,1)S(1)}, u32[]{:S(2)}, u32[]{:S(2)}) collective-permute-start(bf16[1,112,1152]{2,1,0:T(8,128)(2,1)} %get-tuple-element.282), channel_id=1, source_target_pairs={{0,16},{2,18},{4,20},{6,22},{8,24},{10,26},{12,28},{14,30},{16,0},... | collective-permute-start | bytes 774152 | tf_op jit(solution)/shard_map/ppermute | solution.py:45
  430.6 28.1 %collective-permute-start.41 = (bf16[1,112,1152]{2,1,0:T(8,128)(2,1)}, bf16[1,112,1152]{2,1,0:T(8,128)(2,1)S(1)}, u32[]{:S(2)}, u32[]{:S(2)}) collective-permute-start(bf16[1,112,1152]{2,1,0:T(8,128)(2,1)} %get-tuple-element.284), channel_id=1, source_target_pairs={{0,16},{2,18},{4,20},{6,22},{8,24},{10,26},{12,28},{14,30},{16,0},... | collective-permute-start | bytes 774152 | tf_op jit(solution)/shard_map/ppermute | solution.py:45
  434.7 36.4 %collective-permute-start.45 = (bf16[2,304,256]{2,1,0:T(8,128)(2,1)}, bf16[2,304,256]{2,1,0:T(8,128)(2,1)S(1)}, u32[]{:S(2)}, u32[]{:S(2)}) collective-permute-start(bf16[2,304,256]{2,1,0:T(8,128)(2,1)} %get-tuple-element.291), channel_id=1, source_target_pairs={{0,8},{2,10},{4,12},{6,14},{8,0},{10,2},{12,4},{14,6},{16,24},{18,... | collective-permute-start | bytes 933896 | tf_op jit(solution)/shard_map/ppermute | solution.py:45
  435.5 35.9 %collective-permute-start.44 = (bf16[2,304,384]{2,1,0:T(8,128)(2,1)}, bf16[2,304,384]{2,1,0:T(8,128)(2,1)S(1)}, u32[]{:S(2)}, u32[]{:S(2)}) collective-permute-start(bf16[2,304,384]{2,1,0:T(8,128)(2,1)} %get-tuple-element.289), channel_id=1, source_target_pairs={{0,8},{2,10},{4,12},{6,14},{8,0},{10,2},{12,4},{14,6},{16,24},{18,... | collective-permute-start | bytes 1400840 | tf_op jit(solution)/shard_map/ppermute | solution.py:45
  457.1 12.6 %collective-permute-start.46 = (bf16[2,384,128]{2,1,0:T(8,128)(2,1)S(1)}, bf16[2,384,128]{2,1,0:T(8,128)(2,1)S(1)}, u32[]{:S(2)}, u32[]{:S(2)}) collective-permute-start(bf16[2,384,128]{2,1,0:T(8,128)(2,1)S(1)} %copy-done.38), channel_id=1, source_target_pairs={{0,2},{2,0},{4,6},{6,4},{8,10},{10,8},{12,14},{14,12},{16,18},{18,... | collective-permute-start | bytes 589832 | tf_op jit(solution)/shard_map/ppermute | solution.py:45
  458.7 30.9 %collective-permute-start.48 = (bf16[1,512,256]{2,1,0:T(8,128)(2,1)S(1)}, bf16[1,512,256]{2,1,0:T(8,128)(2,1)S(1)}, u32[]{:S(2)}, u32[]{:S(2)}) collective-permute-start(bf16[1,512,256]{2,1,0:T(8,128)(2,1)S(1)} %copy-done.37), channel_id=1, source_target_pairs={{0,16},{2,18},{4,20},{6,22},{8,24},{10,26},{12,28},{14,30},{16,0},... | collective-permute-start | bytes 786440 | tf_op jit(solution)/shard_map/ppermute | solution.py:45
  462.6 44.6 %collective-permute-start.50 = (bf16[1,592,256]{2,1,0:T(8,128)(2,1)S(1)}, bf16[1,592,256]{2,1,0:T(8,128)(2,1)S(1)}, u32[]{:S(2)}, u32[]{:S(2)}) collective-permute-start(bf16[1,592,256]{2,1,0:T(8,128)(2,1)S(1)} %copy-done.35), channel_id=1, source_target_pairs={{0,16},{2,18},{4,20},{6,22},{8,24},{10,26},{12,28},{14,30},{16,0},... | collective-permute-start | bytes 909320 | tf_op jit(solution)/shard_map/ppermute | solution.py:45
  469.7 23.3 %collective-permute-start.47 = (f32[16,3200]{1,0:T(8,128)}, f32[16,3200]{1,0:T(8,128)S(1)}, u32[]{:S(2)}, u32[]{:S(2)}) collective-permute-start(f32[16,3200]{1,0:T(8,128)} %add.7.a_ref), channel_id=1, source_target_pairs={{0,2},{2,0},{4,6},{6,4},{8,10},{10,8},{12,14},{14,12},{16,18},{18,... | collective-permute-start | bytes 614408 | tf_op jit(solution)/shard_map/ppermute | solution.py:45
  471.1 36.1 %collective-permute-start.49 = (bf16[1,512,256]{2,1,0:T(8,128)(2,1)S(1)}, bf16[1,512,256]{2,1,0:T(8,128)(2,1)S(1)}, u32[]{:S(2)}, u32[]{:S(2)}) collective-permute-start(bf16[1,512,256]{2,1,0:T(8,128)(2,1)S(1)} %copy-done.36), channel_id=1, source_target_pairs={{0,16},{2,18},{4,20},{6,22},{8,24},{10,26},{12,28},{14,30},{16,0},... | collective-permute-start | bytes 786440 | tf_op jit(solution)/shard_map/ppermute | solution.py:45
  474.8 40.2 %collective-permute-start.51 = (bf16[1,304,384]{2,1,0:T(8,128)(2,1)}, bf16[1,304,384]{2,1,0:T(8,128)(2,1)S(1)}, u32[]{:S(2)}, u32[]{:S(2)}) collective-permute-start(bf16[1,304,384]{2,1,0:T(8,128)(2,1)} %get-tuple-element.306), channel_id=1, source_target_pairs={{0,16},{2,18},{4,20},{6,22},{8,24},{10,26},{12,28},{14,30},{16,0},... | collective-permute-start | bytes 700424 | tf_op jit(solution)/shard_map/ppermute | solution.py:45
  489.6 25.4 %collective-permute-start.52 = (bf16[1,304,256]{2,1,0:T(8,128)(2,1)}, bf16[1,304,256]{2,1,0:T(8,128)(2,1)S(1)}, u32[]{:S(2)}, u32[]{:S(2)}) collective-permute-start(bf16[1,304,256]{2,1,0:T(8,128)(2,1)} %get-tuple-element.308), channel_id=1, source_target_pairs={{0,16},{2,18},{4,20},{6,22},{8,24},{10,26},{12,28},{14,30},{16,0},... | collective-permute-start | bytes 466952 | tf_op jit(solution)/shard_map/ppermute | solution.py:45
  493.0 22.0 %collective-permute-start.53 = (bf16[1,384,128]{2,1,0:T(8,128)(2,1)}, bf16[1,384,128]{2,1,0:T(8,128)(2,1)S(1)}, u32[]{:S(2)}, u32[]{:S(2)}) collective-permute-start(bf16[1,384,128]{2,1,0:T(8,128)(2,1)} %get-tuple-element.310), channel_id=1, source_target_pairs={{0,16},{2,18},{4,20},{6,22},{8,24},{10,26},{12,28},{14,30},{16,0},... | collective-permute-start | bytes 294920 | tf_op jit(solution)/shard_map/ppermute | solution.py:45
  (45 other events, 287.2 us)

commit v2 on v1

--- a/solution.py
+++ b/solution.py
@@ -18,7 +18,7 @@
 F32 = jnp.float32
 BF16 = jnp.bfloat16
 NT = (((1,), (1,)), ((), ()))
-VMEM_LIMIT = 60 * 1024 * 1024
+VMEM_LIMIT = 67_043_328
 
 
 def shape_of(shape, dtype):
@@ -100,7 +100,7 @@
 
 def gather_smalls(smalls):
     widest = max(x.shape[0] for x in smalls)
-    return pl.pallas_call(gather_kernel, out_shape=shape_of((16, widest), F32), name="gather")(*smalls)
+    return pl.pallas_call(gather_kernel, out_shape=shape_of((16, widest), F32), compiler_params=params(), name="gather")(*smalls)
 
 
 def unpack_kernel(side_ref, own_ref, away_ref, rows_ref, cols_ref, packed_ref):
@@ -121,7 +121,7 @@
         unpack_kernel,
         in_specs=[pl.BlockSpec(memory_space=pltpu.SMEM), vmem, vmem],
         out_shape=[shape_of((8, width), F32), shape_of((width, 128), F32), shape_of((1, 3 * width), F32)],
-        name="unpack",
+        compiler_params=params(), name="unpack",
     )(side, own, away)
 
 
@@ -152,7 +152,7 @@
         collect_kernel,
         in_specs=[pl.BlockSpec(memory_space=pltpu.SMEM)] + [vmem] * (2 + len(rows)),
         out_shape=[out, out],
-        name="collect",
+        compiler_params=params(), name="collect",
     )(side, pack, eb, *rows)
 
 
@@ -161,7 +161,7 @@
 
 
 def add(a, b):
-    return pl.pallas_call(add_kernel, out_shape=shape_of(a.shape, a.dtype), name="add")(a, b)
+    return pl.pallas_call(add_kernel, out_shape=shape_of(a.shape, a.dtype), compiler_params=params(), name="add")(a, b)
 
 
 def divide_kernel(a_ref, b_ref, *outs):
@@ -172,7 +172,7 @@
 
 def divide(a, b, sizes):
     return pl.pallas_call(
-        divide_kernel, out_shape=[shape_of((n,), F32) for n in sizes], name="divide"
+        divide_kernel, out_shape=[shape_of((n,), F32) for n in sizes], compiler_params=params(), name="divide"
     )(a, b)
 
 
@@ -318,7 +318,7 @@
         out_specs=[blk(lambda s, p: (s, p)), blk(lambda s, p: (s, 0))],
         out_shape=[shape_of((rows, width), BF16), shape_of((rows, 2 * HD), F32)],
         cost_estimate=cost(rows * LEN * width * 12, 8 * rows * width),
-        name="attend",
+        compiler_params=params(), name="attend",
     )(packed, packed, packed, packed)
 
 
@@ -394,7 +394,7 @@
         out_shape=shape_of((3, width, rows), BF16),
         scratch_shapes=[pltpu.VMEM((LEN, 2 * HD), BF16)],
         cost_estimate=cost(rows * LEN * width * 12, 14 * rows * width),
-        name="aback",
+        compiler_params=params(), name="aback",
     )(packed, packed, packed, packed, grad_t, attended, lse)
     return out.reshape(3 * width, rows)
 
@@ -1092,7 +1092,7 @@
         tok_t, cot_t, contract_own = tokens.T, cotangent.T, w_contract.T
         own_small = gather_smalls(smalls)
         away_small = swap_group(own_small)
-        heads_in, _ = lax.optimization_barrier((w_heads, away_small))
+        heads_in, _ = lax.optimization_barrier((w_heads, own_small))
         heads_away = swap_group(heads_in)
         small_rows, cols, packed_row = unpack_smalls(sides, own_small, away_small, width)
         first_own, first_out, cot, cot_sum = prep(sides, tok_t, cot_t, cols)
@@ -1121,7 +1121,7 @@
         start_second = jnp.reshape(side * tiles, (1,)).astype(jnp.int32)
 
         def do_hidden(start, bias):
-            return held(hidden(hold(start), second_own, second_out, w_expand, expand_away, bias, units))
+            return held(hidden(start, second_own, second_out, w_expand, expand_away, hold(bias), units))
 
         attended, lse = held(attend(packed))
         att_own, att_out, middle_t, second_own, second_out, normed_t, inv_t = held(project(

time: 525 us -> 534 us (1.017)
  waiting for transfers between devices: 141 us -> 163 us
  local copies, waits for them, and re-layouts: 11.6 us -> 0 us
    ppermute x40, waiting for transfers between devices: 137 us -> 150 us  [exchange(): return lax.ppermute(x, 'rep', [(i, i ^ mask) for i in range(count)])]
    unnamed x78 -> x0, local copies, waits for them, and re-layouts: 11.6 us -> none
    ppermute x14, waiting for transfers between devices: 4.2 us -> 12.4 us  [swap_group(): return lax.ppermute(x, 'grp', [(0, 1), (1, 0)])]
where the time goes in v2:
time: 534 us; the launch traced here: 527 us
  Pallas kernels  311 us (58%)
  waiting for transfers between devices  163 us (31%)
  starting transfers between devices  52.1 us (10%)
    ppermute x40, waiting for transfers between devices, exchange(): return lax.ppermute(x, 'rep', [(i, i ^ mask) for i in range(count)])  150 us
    pallas_call x3, Pallas kernels, spread(): pl.pallas_call(functools.partial(spread_kernel, (group, batches, starts))...  62.6 us
    ppermute x40, starting transfers between devices, exchange(): return lax.ppermute(x, 'rep', [(i, i ^ mask) for i in range(count)])  49.8 us
    pallas_call x9, Pallas kernels, merge(): pl.pallas_call(merge_kernel, grid=(half,), in_specs=specs, out_specs=out_...  41.1 us
    pallas_call x1, Pallas kernels, middle_back(): pl.pallas_call(middle_kernel, grid_spec=pltpu.PrefetchScalarGridSpec(num_...  27.7 us
    pallas_call x2, Pallas kernels, hidden(): pl.pallas_call(hidden_kernel, grid_spec=pltpu.PrefetchScalarGridSpec(num_...  27.1 us
    pallas_call x1, Pallas kernels, attend_back(): pl.pallas_call(functools.partial(attend_back_kernel, width), grid=(seqs,...  22.6 us
    pallas_call x1, Pallas kernels, hidden_back(): pl.pallas_call(hidden_back_kernel, grid_spec=pltpu.PrefetchScalarGridSpec...  21 us
  transfers between devices with their start and end apart: 54, of which 16 were waited for; matrix products, arithmetic and copies ran while one was open for 0% of the time, Pallas kernels for 45%

profile of v2, /device:TPU:18, one launch (start us, length us, event | category | flops | bytes accessed | tf_op | source)
XLA Modules:
  0.0 526.6 jit_solution(9549273359991059827)
XLA Ops:
  2.7 12.4 %collective-permute-done.away_ref.bias_ref = f32[16,3200]{1,0:T(8,128)} collective-permute-done((f32[16,3200]{1,0:T(8,128)}, f32[16,3200]{1,0:T(8,128)}, u32[]{:S(2)}, u32[]{:S(2)}) %collective-permute-start) | collective-permute-done | bytes 204832 | tf_op jit(solution)/shard_map/ppermute | solution.py:41
  15.1 2.2 unpack.1
  17.4 6.8 %prep.1 = (bf16[512,896]{1,0:T(8,128)(2,1)}, bf16[512,896]{1,0:T(8,128)(2,1)}, bf16[512,1600]{1,0:T(8,128)(2,1)}, f32[8,1600]{1,0:T(8,128)}) custom-call(s32[1]{0:T(128)} %bitcast.1.side_ref.meta_ref, bf16[1600,512]{1,0:T(8,128)(2,1)} %bitcast.21, bf16[1600,512]{1,0:T(8,128)(2,1)} %bitcast.17, f32[1600,128]{1,0:T(8,128)} %get-tuple-element.167.cols_ref.gain_ref), custom_call_target="tpu_custom_call" | custom-call | bytes 6553600 | tf_op jit(solution)/shard_map/prep/pallas_call | solution.py:210
  24.4 14.1 %heads.1.q_ref.ka_ref.kb_ref.v_ref = bf16[512,4800]{1,0:T(8,128)(2,1)} custom-call(bf16[512,896]{1,0:T(8,128)(2,1)} %get-tuple-element.168.own_ref.refs_2_, bf16[512,896]{1,0:T(8,128)(2,1)} %get-tuple-element.219.away_ref, bf16[800,4800]{1,0:T(8,128)(2,1)} %wo_hbm.3, bf16[800,4800]{1,0:T(8,128)(2,1)} %collective-permute-done.1.wa_ref.wa_hbm, ...), custom_call_target="tpu_custom_call" | custom-call | flops 7864320000 | bytes 20275200 | tf_op jit(solution)/shard_map/heads/pallas_call | solution.py:242
  39.0 16.4 %attend.1 = (bf16[512,1600]{1,0:T(8,128)(2,1)}, f32[512,128]{1,0:T(8,128)}) custom-call(bf16[512,4800]{1,0:T(8,128)(2,1)} %heads.1.q_ref.ka_ref.kb_ref.v_ref, bf16[512,4800]{1,0:T(8,128)(2,1)} %heads.1.q_ref.ka_ref.kb_ref.v_ref, bf16[512,4800]{1,0:T(8,128)(2,1)} %heads.1.q_ref.ka_ref.kb_ref.v_ref, bf16[512,4800]{1,0:T(8,128)(2,1)} %heads.1.q_ref.ka_ref.kb_ref.v_ref), custom_call_target="tpu_custom_call" | custom-call | flops 5033164800 | bytes 6553600 | tf_op jit(solution)/shard_map/attend/pallas_call | solution.py:309
  55.4 10.7 %project.1 = (bf16[512,896]{1,0:T(8,128)(2,1)}, bf16[512,896]{1,0:T(8,128)(2,1)}, bf16[1600,512]{1,0:T(8,128)(2,1)}, bf16[512,896]{1,0:T(8,128)(2,1)}, bf16[512,...) custom-call(s32[1]{0:T(128)} %bitcast.1.side_ref.meta_ref, ...), custom_call_target="tpu_custom_call" | custom-call | flops 2621440000 | bytes 16588800 | tf_op jit(solution)/shard_map/project/pallas_call | solution.py:429
  66.1 13.5 %hidden.2 = (bf16[512,3200]{1,0:T(8,128)(2,1)}, bf16[512,3200]{1,0:T(8,128)(2,1)}) custom-call(s32[1]{0:T(128)} %bitcast.start_ref, bf16[512,896]{1,0:T(8,128)(2,1)} %get-tuple-element.175.so_ref.refs_2_, bf16[512,896]{1,0:T(8,128)(2,1)} %get-tuple-element.176.sa_ref, bf16[800,6400]{1,0:T(8,128)(2,1)} %wo_hbm.2, ...), custom_call_target="tpu_custom_call" | custom-call | flops 5242880000 | bytes 16793600 | tf_op jit(solution)/shard_map/hidden/pallas_call | solution.py:477
  80.2 13.5 %hidden.3 = (bf16[512,3200]{1,0:T(8,128)(2,1)}, bf16[512,3200]{1,0:T(8,128)(2,1)}) custom-call(s32[1]{0:T(128)} %bitcast.5.start_ref, bf16[512,896]{1,0:T(8,128)(2,1)} %get-tuple-element.175.so_ref.refs_2_, bf16[512,896]{1,0:T(8,128)(2,1)} %get-tuple-element.176.sa_ref, bf16[800,6400]{1,0:T(8,128)(2,1)} %wo_hbm.2, ...), custom_call_target="tpu_custom_call" | custom-call | flops 5242880000 | bytes 16793600 | tf_op jit(solution)/shard_map/hidden/pallas_call | solution.py:477
  93.7 18.1 %spread.3 = (bf16[8,112,1152]{2,1,0:T(8,128)(2,1)}, bf16[8,112,1152]{2,1,0:T(8,128)(2,1)}, bf16[8,112,896]{2,1,0:T(8,128)(2,1)}, bf16[8,112,1152]{2,1,0:T(8,128)...) custom-call(s32[1]{0:T(128)} %bitcast.4.meta_ref, bf16[1600,512]{1,0:T(8,128)(2,1)} %bitcast.19, ...), custom_call_target="tpu_custom_call" | custom-call | flops 10485760000 | bytes 40960000 | tf_op jit(solution)/shard_map/spread/pallas_call | solution.py:954
  111.8 21.0 %hback.1 = (bf16[6400,512]{1,0:T(8,128)(2,1)}, f32[8,6400]{1,0:T(8,128)}) custom-call(s32[1]{0:T(128)} %bitcast.1.side_ref.meta_ref, bf16[512,1600]{1,0:T(8,128)(2,1)} %get-tuple-element.188.cot_ref, bf16[1600,3200]{1,0:T(8,128)(2,1)} %collective-permute-done.6.w1_hbm, bf16[1600,3200]{1,0:T(8,128)(2,1)} %bitcast.27, ...), custom_call_target="tpu_custom_call" | custom-call | flops 10485760000 | bytes 33587200 | tf_op jit(solution)/shard_map/hback/pallas_call | solution.py:511
  136.8 27.7 %middle.1 = (f32[1600,512]{1,0:T(8,128)}, bf16[1600,512]{1,0:T(8,128)(2,1)}, bf16[1600,512]{1,0:T(8,128)(2,1)}, f32[8,1600]{1,0:T(8,128)}, f32[8,1600]{1,0:T(8,128)}, /*index=5*/f32[8,1600]{1,0:T(8,128)}) custom-call(s32[1]{0:T(128)} %bitcast.1.side_ref.meta_ref, bf16[6400,512]{1,0:T(8,128)(2,1)} %get-tuple-element.192.g_ref.refs_0_, ...), custom_call_target="tpu_custom_call" | custom-call | flops 13107200000 | bytes 30310400 | tf_op jit(solution)/shard_map/middle/pallas_call | solution.py:625
  164.6 6.4 %collective-permute-done.9.refs_9_.refs_11_ = bf16[8,112,896]{2,1,0:T(8,128)(2,1)} collective-permute-done((bf16[8,112,896]{2,1,0:T(8,128)(2,1)}, bf16[8,112,896]{2,1,0:T(8,128)(2,1)}, u32[]{:S(2)}, u32[]{:S(2)}) %collective-permute-start.9) | collective-permute-done | bytes 1605664 | tf_op jit(solution)/shard_map/ppermute | solution.py:45
  170.9 9.6 %collective-permute-done.7.refs_1_.refs_3_ = bf16[8,112,1152]{2,1,0:T(8,128)(2,1)} collective-permute-done((bf16[8,112,1152]{2,1,0:T(8,128)(2,1)}, bf16[8,112,1152]{2,1,0:T(8,128)(2,1)}, u32[]{:S(2)}, u32[]{:S(2)}) %collective-permute-start.7) | collective-permute-done | bytes 2064416 | tf_op jit(solution)/shard_map/ppermute | solution.py:45
  182.0 7.2 %merge.9 = (bf16[4,112,1152]{2,1,0:T(8,128)(2,1)}, bf16[4,112,1152]{2,1,0:T(8,128)(2,1)}, bf16[4,112,896]{2,1,0:T(8,128)(2,1)}, bf16[4,112,1152]{2,1,0:T(8,128)(...) custom-call(bf16[8,112,1152]{2,1,0:T(8,128)(2,1)} %get-tuple-element.197.refs_0_.refs_2_, ...), custom_call_target="tpu_custom_call" | custom-call | bytes 17203200 | tf_op jit(solution)/shard_map/merge/pallas_call | solution.py:991
  189.2 28.6 %spread.4 = (bf16[8,512,256]{2,1,0:T(8,128)(2,1)}, bf16[8,512,256]{2,1,0:T(8,128)(2,1)}, bf16[8,592,256]{2,1,0:T(8,128)(2,1)}, bf16[8,512,256]{2,1,0:T(8,128)(2,...) custom-call(s32[1]{0:T(128)} %bitcast.4.meta_ref, bf16[6400,512]{1,0:T(8,128)(2,1)} %get-tuple-element.192.g_ref.refs_0_, ...), custom_call_target="tpu_custom_call" | custom-call | flops 13107200000 | bytes 51200000 | tf_op jit(solution)/shard_map/spread/pallas_call | solution.py:954
  217.8 22.6 %aback.1 = bf16[3,1600,512]{2,1,0:T(8,128)(2,1)} custom-call(bf16[512,4800]{1,0:T(8,128)(2,1)} %heads.1.q_ref.ka_ref.kb_ref.v_ref, bf16[512,4800]{1,0:T(8,128)(2,1)} %heads.1.q_ref.ka_ref.kb_ref.v_ref, bf16[512,4800]{1,0:T(8,128)(2,1)} %heads.1.q_ref.ka_ref.kb_ref.v_ref, bf16[512,4800]{1,0:T(8,128)(2,1)} %heads.1.q_ref.ka_ref.kb_ref.v_ref, ...), custom_call_target="tpu_custom_call" | custom-call | flops 5033164800 | bytes 11468800 | tf_op jit(solution)/shard_map/aback/pallas_call | solution.py:381
  245.5 17.0 %collective-permute-done.16.refs_9_.refs_11_ = bf16[4,112,896]{2,1,0:T(8,128)(2,1)} collective-permute-done((bf16[4,112,896]{2,1,0:T(8,128)(2,1)}, bf16[4,112,896]{2,1,0:T(8,128)(2,1)}, u32[]{:S(2)}, u32[]{:S(2)}) %collective-permute-start.16) | collective-permute-done | bytes 802848 | tf_op jit(solution)/shard_map/ppermute | solution.py:45
  262.5 4.0 collective-permute-done.14.refs_1_.refs_3_
  269.5 4.1 merge.10
  274.2 16.0 %spread.5 = (bf16[8,304,384]{2,1,0:T(8,128)(2,1)}, bf16[8,304,256]{2,1,0:T(8,128)(2,1)}, bf16[8,384,128]{2,1,0:T(8,128)(2,1)}, bf16[8,304,384]{2,1,0:T(8,128)(2,...) custom-call(s32[1]{0:T(128)} %bitcast.4.meta_ref, bf16[4800,512]{1,0:T(8,128)(2,1)} %bitcast.15, ...), custom_call_target="tpu_custom_call" | custom-call | flops 7864320000 | bytes 30720000 | tf_op jit(solution)/shard_map/spread/pallas_call | solution.py:954
  291.7 32.2 %collective-permute-done.24.refs_9_.refs_11_ = bf16[2,112,896]{2,1,0:T(8,128)(2,1)} collective-permute-done((bf16[2,112,896]{2,1,0:T(8,128)(2,1)}, bf16[2,112,896]{2,1,0:T(8,128)(2,1)}, u32[]{:S(2)}, u32[]{:S(2)}) %collective-permute-start.24) | collective-permute-done | bytes 401440 | tf_op jit(solution)/shard_map/ppermute | solution.py:45
  328.0 7.8 %merge.11 = (bf16[4,512,256]{2,1,0:T(8,128)(2,1)}, bf16[4,512,256]{2,1,0:T(8,128)(2,1)}, bf16[4,592,256]{2,1,0:T(8,128)(2,1)}, bf16[4,512,256]{2,1,0:T(8,128)(2,...) custom-call(bf16[8,512,256]{2,1,0:T(8,128)(2,1)} %get-tuple-element.221.refs_0_.refs_2_, ...), custom_call_target="tpu_custom_call" | custom-call | bytes 19857408 | tf_op jit(solution)/shard_map/merge/pallas_call | solution.py:991
  335.8 3.5 collective-permute-done.22.refs_1_.refs_3_
  339.3 11.7 %collective-permute-done.23.refs_5_.refs_7_ = bf16[2,112,1152]{2,1,0:T(8,128)(2,1)} collective-permute-done((bf16[2,112,1152]{2,1,0:T(8,128)(2,1)}, bf16[2,112,1152]{2,1,0:T(8,128)(2,1)}, u32[]{:S(2)}, u32[]{:S(2)}) %collective-permute-start.23) | collective-permute-done | bytes 516128 | tf_op jit(solution)/shard_map/ppermute | solution.py:45
  351.0 3.1 merge.12
  357.6 20.8 %first.1 = (bf16[1600,512]{1,0:T(8,128)(2,1)}, f32[8,1600]{1,0:T(8,128)}, f32[8,1600]{1,0:T(8,128)}, f32[8,4800]{1,0:T(8,128)}) custom-call(s32[1]{0:T(128)} %bitcast.1.side_ref.meta_ref, bf16[4800,512]{1,0:T(8,128)(2,1)} %bitcast.16, bf16[800,4800]{1,0:T(8,128)(2,1)} %wo_hbm.3, bf16[800,4800]{1,0:T(8,128)(2,1)} %collective-permute-done.1.wa_ref.wa_hbm, ...), custom_call_target="tpu_custom_call" | custom-call | flops 7864320000 | bytes 28467200 | tf_op jit(solution)/shard_map/first/pallas_call | solution.py:747
  378.4 2.0 collect.1
  380.4 5.6 %merge.13 = (bf16[4,304,384]{2,1,0:T(8,128)(2,1)}, bf16[4,304,256]{2,1,0:T(8,128)(2,1)}, bf16[4,384,128]{2,1,0:T(8,128)(2,1)}, bf16[4,304,384]{2,1,0:T(8,128)(2,...) custom-call(bf16[8,304,384]{2,1,0:T(8,128)(2,1)} %get-tuple-element.247.refs_0_.refs_2_, ...), custom_call_target="tpu_custom_call" | custom-call | bytes 11698176 | tf_op jit(solution)/shard_map/merge/pallas_call | solution.py:991
  390.3 4.4 merge.14
  396.9 21.5 %collective-permute-done.34.refs_9_.refs_11_ = bf16[4,384,128]{2,1,0:T(8,128)(2,1)} collective-permute-done((bf16[4,384,128]{2,1,0:T(8,128)(2,1)}, bf16[4,384,128]{2,1,0:T(8,128)(2,1)}, u32[]{:S(2)}, u32[]{:S(2)}) %collective-permute-start.34) | collective-permute-done | bytes 393248 | tf_op jit(solution)/shard_map/ppermute | solution.py:45
  419.1 3.3 merge.15
  422.4 4.8 collective-permute-done.35.b_ref
  429.0 4.6 collective-permute-start.39
  433.5 2.9 collective-permute-start.40
  436.5 3.1 merge.16
  441.8 2.5 collective-permute-start.44
  444.3 18.0 %output.1 = bf16[1600,512]{1,0:T(8,128)(2,1)} custom-call(bf16[512,3200]{1,0:T(8,128)(2,1)} %get-tuple-element.278.a1_ref, bf16[512,3200]{1,0:T(8,128)(2,1)} %get-tuple-element.183.refs_2_.a2_ref, bf16[1600,3200]{1,0:T(8,128)(2,1)} %collective-permute-done.6.w1_hbm, bf16[1600,3200]{1,0:T(8,128)(2,1)} %bitcast.28, ...), custom_call_target="tpu_custom_call" | custom-call | flops 10485760000 | bytes 31948800 | tf_op jit(solution)/shard_map/output/pallas_call | solution.py:798
  466.0 2.2 collective-permute-start.48
  468.2 1.9 collective-permute-done.43.b_ref
  470.3 2.6 finish.3
  476.2 2.7 collective-permute-start.49
  478.9 2.6 merge.17
  481.7 16.2 %collective-permute-done.48.refs_1_ = bf16[1,512,256]{2,1,0:T(8,128)(2,1)} collective-permute-done((bf16[1,512,256]{2,1,0:T(8,128)(2,1)}, bf16[1,512,256]{2,1,0:T(8,128)(2,1)}, u32[]{:S(2)}, u32[]{:S(2)}) %collective-permute-start.48) | collective-permute-done | bytes 262176 | tf_op jit(solution)/shard_map/ppermute | solution.py:45
  497.9 3.4 collective-permute-start.52
  503.0 12.5 %collective-permute-done.49.refs_3_ = bf16[1,512,256]{2,1,0:T(8,128)(2,1)} collective-permute-done((bf16[1,512,256]{2,1,0:T(8,128)(2,1)}, bf16[1,512,256]{2,1,0:T(8,128)(2,1)}, u32[]{:S(2)}, u32[]{:S(2)}) %collective-permute-start.49) | collective-permute-done | bytes 262176 | tf_op jit(solution)/shard_map/ppermute | solution.py:45
  515.5 2.8 finish.4
  518.3 5.9 %collective-permute-done.53.refs_5_ = bf16[1,384,128]{2,1,0:T(8,128)(2,1)} collective-permute-done((bf16[1,384,128]{2,1,0:T(8,128)(2,1)}, bf16[1,384,128]{2,1,0:T(8,128)(2,1)}, u32[]{:S(2)}, u32[]{:S(2)}) %collective-permute-start.53) | collective-permute-done | bytes 98336 | tf_op jit(solution)/shard_map/ppermute | solution.py:45
  524.2 2.4 finish.5
  (94 shorter events, 47.1 us)
Async XLA Ops:
  2.2 22.2 %collective-permute-start.1 = (bf16[800,4800]{1,0:T(8,128)(2,1)}, bf16[800,4800]{1,0:T(8,128)(2,1)}, u32[]{:S(2)}, u32[]{:S(2)}) collective-permute-start(bf16[800,4800]{1,0:T(8,128)(2,1)} %wo_hbm.3), channel_id=1, source_target_pairs={{0,1},{1,0},{2,3},{3,2},{4,5},{5,4},{6,7},{7,6},{8,9},{9,8},{10,11... | collective-permute-start | bytes 23040008 | tf_op jit(solution)/shard_map/ppermute | solution.py:41
  2.2 12.9 %collective-permute-start = (f32[16,3200]{1,0:T(8,128)}, f32[16,3200]{1,0:T(8,128)}, u32[]{:S(2)}, u32[]{:S(2)}) collective-permute-start(f32[16,3200]{1,0:T(8,128)} %gather.1.own_ref.bias_ref), channel_id=1, source_target_pairs={{0,1},{1,0},{2,3},{3,2},{4,5},{5,4},{6,7},{7,6},{8,9},{9,8},{10,11... | collective-permute-start | bytes 614408 | tf_op jit(solution)/shard_map/ppermute | solution.py:41
  24.2 14.3 %collective-permute-start.2 = (bf16[800,1600]{1,0:T(8,128)(2,1)}, bf16[800,1600]{1,0:T(8,128)(2,1)}, u32[]{:S(2)}, u32[]{:S(2)}) collective-permute-start(bf16[800,1600]{1,0:T(8,128)(2,1)} %po_hbm.1), channel_id=1, source_target_pairs={{0,1},{1,0},{2,3},{3,2},{4,5},{5,4},{6,7},{7,6},{8,9},{9,8},{10,11... | collective-permute-start | bytes 7680008 | tf_op jit(solution)/shard_map/ppermute | solution.py:41
  38.5 27.6 %collective-permute-start.3 = (bf16[800,6400]{1,0:T(8,128)(2,1)}, bf16[800,6400]{1,0:T(8,128)(2,1)}, u32[]{:S(2)}, u32[]{:S(2)}) collective-permute-start(bf16[800,6400]{1,0:T(8,128)(2,1)} %wo_hbm.2), channel_id=1, source_target_pairs={{0,1},{1,0},{2,3},{3,2},{4,5},{5,4},{6,7},{7,6},{8,9},{9,8},{10,11... | collective-permute-start | bytes 30720008 | tf_op jit(solution)/shard_map/ppermute | solution.py:41
  38.8 72.9 %collective-permute-start.6 = (bf16[1600,3200]{1,0:T(8,128)(2,1)}, bf16[1600,3200]{1,0:T(8,128)(2,1)}, u32[]{:S(2)}, u32[]{:S(2)}) collective-permute-start(bf16[1600,3200]{1,0:T(8,128)(2,1)} %bitcast.26), channel_id=1, source_target_pairs={{0,1},{1,0},{2,3},{3,2},{4,5},{5,4},{6,7},{7,6},{8,9},{9,8},{10,11... | collective-permute-start | bytes 30720008 | tf_op jit(solution)/shard_map/ppermute | solution.py:41
  79.6 14.0 %collective-permute-start.5 = (bf16[512,3200]{1,0:T(8,128)(2,1)}, bf16[512,3200]{1,0:T(8,128)(2,1)}, u32[]{:S(2)}, u32[]{:S(2)}) collective-permute-start(bf16[512,3200]{1,0:T(8,128)(2,1)} %get-tuple-element.278.a1_ref), channel_id=1, source_target_pairs={{0,1},{1,0},{2,3},{3,2},{4,5},{5,4},{6,7},{7,6},{8,9},{9,8},{10,11... | collective-permute-start | bytes 9830408 | tf_op jit(solution)/shard_map/ppermute | solution.py:41
  80.0 13.6 %collective-permute-start.4 = (bf16[1600,512]{1,0:T(8,128)(2,1)}, bf16[1600,512]{1,0:T(8,128)(2,1)}, u32[]{:S(2)}, u32[]{:S(2)}) collective-permute-start(bf16[1600,512]{1,0:T(8,128)(2,1)} %bitcast.18), channel_id=1, source_target_pairs={{0,1},{1,0},{2,3},{3,2},{4,5},{5,4},{6,7},{7,6},{8,9},{9,8},{10,11... | collective-permute-start | bytes 4915208 | tf_op jit(solution)/shard_map/ppermute | solution.py:41
  132.8 56.4 %collective-permute-start.10 = (bf16[6400,512]{1,0:T(8,128)(2,1)}, bf16[6400,512]{1,0:T(8,128)(2,1)}, u32[]{:S(2)}, u32[]{:S(2)}) collective-permute-start(bf16[6400,512]{1,0:T(8,128)(2,1)} %get-tuple-element.192.g_ref.refs_0_), channel_id=1, source_target_pairs={{0,1},{1,0},{2,3},{3,2},{4,5},{5,4},{6,7},{7,6},{8,9},{9,8},{10,11... | collective-permute-start | bytes 19660808 | tf_op jit(solution)/shard_map/ppermute | solution.py:41
  133.3 47.3 %collective-permute-start.7 = (bf16[8,112,1152]{2,1,0:T(8,128)(2,1)}, bf16[8,112,1152]{2,1,0:T(8,128)(2,1)}, u32[]{:S(2)}, u32[]{:S(2)}) collective-permute-start(bf16[8,112,1152]{2,1,0:T(8,128)(2,1)} %get-tuple-element.198), channel_id=1, source_target_pairs={{0,2},{2,0},{4,6},{6,4},{8,10},{10,8},{12,14},{14,12},{16,18},{18,... | collective-permute-start | bytes 6193160 | tf_op jit(solution)/shard_map/ppermute | solution.py:45
  133.8 37.1 %collective-permute-start.9 = (bf16[8,112,896]{2,1,0:T(8,128)(2,1)}, bf16[8,112,896]{2,1,0:T(8,128)(2,1)}, u32[]{:S(2)}, u32[]{:S(2)}) collective-permute-start(bf16[8,112,896]{2,1,0:T(8,128)(2,1)} %get-tuple-element.202), channel_id=1, source_target_pairs={{0,8},{2,10},{4,12},{6,14},{8,0},{10,2},{12,4},{14,6},{16,24},{18,... | collective-permute-start | bytes 4816904 | tf_op jit(solution)/shard_map/ppermute | solution.py:45
  135.3 46.7 %collective-permute-start.8 = (bf16[8,112,1152]{2,1,0:T(8,128)(2,1)}, bf16[8,112,1152]{2,1,0:T(8,128)(2,1)}, u32[]{:S(2)}, u32[]{:S(2)}) collective-permute-start(bf16[8,112,1152]{2,1,0:T(8,128)(2,1)} %get-tuple-element.200), channel_id=1, source_target_pairs={{0,4},{2,6},{4,0},{6,2},{8,12},{10,14},{12,8},{14,10},{16,20},{18,... | collective-permute-start | bytes 6193160 | tf_op jit(solution)/shard_map/ppermute | solution.py:45
  164.5 24.8 %collective-permute-start.12 = (bf16[1600,512]{1,0:T(8,128)(2,1)}, bf16[1600,512]{1,0:T(8,128)(2,1)}, u32[]{:S(2)}, u32[]{:S(2)}) collective-permute-start(bf16[1600,512]{1,0:T(8,128)(2,1)} %get-tuple-element.205.refs_4_), channel_id=1, source_target_pairs={{0,1},{1,0},{2,3},{3,2},{4,5},{5,4},{6,7},{7,6},{8,9},{9,8},{10,11... | collective-permute-start | bytes 4915208 | tf_op jit(solution)/shard_map/ppermute | solution.py:41
  170.9 18.3 %collective-permute-start.13 = (bf16[512,896]{1,0:T(8,128)(2,1)}, bf16[512,896]{1,0:T(8,128)(2,1)}, u32[]{:S(2)}, u32[]{:S(2)}) collective-permute-start(bf16[512,896]{1,0:T(8,128)(2,1)} %get-tuple-element.206), channel_id=1, source_target_pairs={{0,1},{1,0},{2,3},{3,2},{4,5},{5,4},{6,7},{7,6},{8,9},{9,8},{10,11... | collective-permute-start | bytes 2752520 | tf_op jit(solution)/shard_map/ppermute | solution.py:41
  240.4 33.7 %collective-permute-start.17 = (bf16[4800,512]{1,0:T(8,128)(2,1)}, bf16[4800,512]{1,0:T(8,128)(2,1)}, u32[]{:S(2)}, u32[]{:S(2)}) collective-permute-start(bf16[4800,512]{1,0:T(8,128)(2,1)} %bitcast.14), channel_id=1, source_target_pairs={{0,1},{1,0},{2,3},{3,2},{4,5},{5,4},{6,7},{7,6},{8,9},{9,8},{10,11... | collective-permute-start | bytes 14745608 | tf_op jit(solution)/shard_map/ppermute | solution.py:41
  240.5 26.1 %collective-permute-start.14 = (bf16[4,112,1152]{2,1,0:T(8,128)(2,1)}, bf16[4,112,1152]{2,1,0:T(8,128)(2,1)}, u32[]{:S(2)}, u32[]{:S(2)}) collective-permute-start(bf16[4,112,1152]{2,1,0:T(8,128)(2,1)} %get-tuple-element.212), channel_id=1, source_target_pairs={{0,8},{2,10},{4,12},{6,14},{8,0},{10,2},{12,4},{14,6},{16,24},{18,... | collective-permute-start | bytes 3096584 | tf_op jit(solution)/shard_map/ppermute | solution.py:45
  241.0 27.0 %collective-permute-start.15 = (bf16[4,112,1152]{2,1,0:T(8,128)(2,1)}, bf16[4,112,1152]{2,1,0:T(8,128)(2,1)}, u32[]{:S(2)}, u32[]{:S(2)}) collective-permute-start(bf16[4,112,1152]{2,1,0:T(8,128)(2,1)} %get-tuple-element.214), channel_id=1, source_target_pairs={{0,2},{2,0},{4,6},{6,4},{8,10},{10,8},{12,14},{14,12},{16,18},{18,... | collective-permute-start | bytes 3096584 | tf_op jit(solution)/shard_map/ppermute | solution.py:45
  242.5 20.0 %collective-permute-start.16 = (bf16[4,112,896]{2,1,0:T(8,128)(2,1)}, bf16[4,112,896]{2,1,0:T(8,128)(2,1)}, u32[]{:S(2)}, u32[]{:S(2)}) collective-permute-start(bf16[4,112,896]{2,1,0:T(8,128)(2,1)} %get-tuple-element.216), channel_id=1, source_target_pairs={{0,4},{2,6},{4,0},{6,2},{8,12},{10,14},{12,8},{14,10},{16,20},{18,... | collective-permute-start | bytes 2408456 | tf_op jit(solution)/shard_map/ppermute | solution.py:45
  244.0 83.4 %collective-permute-start.21 = (bf16[8,592,256]{2,1,0:T(8,128)(2,1)}, bf16[8,592,256]{2,1,0:T(8,128)(2,1)}, u32[]{:S(2)}, u32[]{:S(2)}) collective-permute-start(bf16[8,592,256]{2,1,0:T(8,128)(2,1)} %get-tuple-element.226), channel_id=1, source_target_pairs={{0,8},{2,10},{4,12},{6,14},{8,0},{10,2},{12,4},{14,6},{16,24},{18,... | collective-permute-start | bytes 7274504 | tf_op jit(solution)/shard_map/ppermute | solution.py:45
  266.5 57.9 %collective-permute-start.19 = (bf16[8,512,256]{2,1,0:T(8,128)(2,1)}, bf16[8,512,256]{2,1,0:T(8,128)(2,1)}, u32[]{:S(2)}, u32[]{:S(2)}) collective-permute-start(bf16[8,512,256]{2,1,0:T(8,128)(2,1)} %get-tuple-element.222), channel_id=1, source_target_pairs={{0,2},{2,0},{4,6},{6,4},{8,10},{10,8},{12,14},{14,12},{16,18},{18,... | collective-permute-start | bytes 6291464 | tf_op jit(solution)/shard_map/ppermute | solution.py:45
  268.0 57.9 %collective-permute-start.20 = (bf16[8,512,256]{2,1,0:T(8,128)(2,1)}, bf16[8,512,256]{2,1,0:T(8,128)(2,1)}, u32[]{:S(2)}, u32[]{:S(2)}) collective-permute-start(bf16[8,512,256]{2,1,0:T(8,128)(2,1)} %get-tuple-element.224), channel_id=1, source_target_pairs={{0,4},{2,6},{4,0},{6,2},{8,12},{10,14},{12,8},{14,10},{16,20},{18,... | collective-permute-start | bytes 6291464 | tf_op jit(solution)/shard_map/ppermute | solution.py:45
  273.6 50.3 %collective-permute-start.24 = (bf16[2,112,896]{2,1,0:T(8,128)(2,1)}, bf16[2,112,896]{2,1,0:T(8,128)(2,1)}, u32[]{:S(2)}, u32[]{:S(2)}) collective-permute-start(bf16[2,112,896]{2,1,0:T(8,128)(2,1)} %get-tuple-element.233), channel_id=1, source_target_pairs={{0,2},{2,0},{4,6},{6,4},{8,10},{10,8},{12,14},{14,12},{16,18},{18,... | collective-permute-start | bytes 1204232 | tf_op jit(solution)/shard_map/ppermute | solution.py:45
  290.1 90.2 %collective-permute-start.25 = (bf16[8,304,384]{2,1,0:T(8,128)(2,1)}, bf16[8,304,384]{2,1,0:T(8,128)(2,1)}, u32[]{:S(2)}, u32[]{:S(2)}) collective-permute-start(bf16[8,304,384]{2,1,0:T(8,128)(2,1)} %get-tuple-element.248), channel_id=1, source_target_pairs={{0,2},{2,0},{4,6},{6,4},{8,10},{10,8},{12,14},{14,12},{16,18},{18,... | collective-permute-start | bytes 5603336 | tf_op jit(solution)/shard_map/ppermute | solution.py:45
  323.9 32.1 %collective-permute-start.27 = (bf16[8,384,128]{2,1,0:T(8,128)(2,1)}, bf16[8,384,128]{2,1,0:T(8,128)(2,1)}, u32[]{:S(2)}, u32[]{:S(2)}) collective-permute-start(bf16[8,384,128]{2,1,0:T(8,128)(2,1)} %get-tuple-element.252), channel_id=1, source_target_pairs={{0,8},{2,10},{4,12},{6,14},{8,0},{10,2},{12,4},{14,6},{16,24},{18,... | collective-permute-start | bytes 2359304 | tf_op jit(solution)/shard_map/ppermute | solution.py:45
  324.4 14.9 %collective-permute-start.22 = (bf16[2,112,1152]{2,1,0:T(8,128)(2,1)}, bf16[2,112,1152]{2,1,0:T(8,128)(2,1)}, u32[]{:S(2)}, u32[]{:S(2)}) collective-permute-start(bf16[2,112,1152]{2,1,0:T(8,128)(2,1)} %get-tuple-element.229), channel_id=1, source_target_pairs={{0,4},{2,6},{4,0},{6,2},{8,12},{10,14},{12,8},{14,10},{16,20},{18,... | collective-permute-start | bytes 1548296 | tf_op jit(solution)/shard_map/ppermute | solution.py:45
  325.9 25.1 %collective-permute-start.23 = (bf16[2,112,1152]{2,1,0:T(8,128)(2,1)}, bf16[2,112,1152]{2,1,0:T(8,128)(2,1)}, u32[]{:S(2)}, u32[]{:S(2)}) collective-permute-start(bf16[2,112,1152]{2,1,0:T(8,128)(2,1)} %get-tuple-element.231), channel_id=1, source_target_pairs={{0,8},{2,10},{4,12},{6,14},{8,0},{10,2},{12,4},{14,6},{16,24},{18,... | collective-permute-start | bytes 1548296 | tf_op jit(solution)/shard_map/ppermute | solution.py:45
  327.4 52.9 %collective-permute-start.26 = (bf16[8,304,256]{2,1,0:T(8,128)(2,1)}, bf16[8,304,256]{2,1,0:T(8,128)(2,1)}, u32[]{:S(2)}, u32[]{:S(2)}) collective-permute-start(bf16[8,304,256]{2,1,0:T(8,128)(2,1)} %get-tuple-element.250), channel_id=1, source_target_pairs={{0,4},{2,6},{4,0},{6,2},{8,12},{10,14},{12,8},{14,10},{16,20},{18,... | collective-permute-start | bytes 3735560 | tf_op jit(solution)/shard_map/ppermute | solution.py:45
  354.1 33.0 %collective-permute-start.29 = (bf16[4,512,256]{2,1,0:T(8,128)(2,1)}, bf16[4,512,256]{2,1,0:T(8,128)(2,1)}, u32[]{:S(2)}, u32[]{:S(2)}) collective-permute-start(bf16[4,512,256]{2,1,0:T(8,128)(2,1)} %get-tuple-element.257), channel_id=1, source_target_pairs={{0,4},{2,6},{4,0},{6,2},{8,12},{10,14},{12,8},{14,10},{16,20},{18,... | collective-permute-start | bytes 3145736 | tf_op jit(solution)/shard_map/ppermute | solution.py:45
  355.5 34.8 %collective-permute-start.30 = (bf16[4,512,256]{2,1,0:T(8,128)(2,1)}, bf16[4,512,256]{2,1,0:T(8,128)(2,1)}, u32[]{:S(2)}, u32[]{:S(2)}) collective-permute-start(bf16[4,512,256]{2,1,0:T(8,128)(2,1)} %get-tuple-element.259), channel_id=1, source_target_pairs={{0,8},{2,10},{4,12},{6,14},{8,0},{10,2},{12,4},{14,6},{16,24},{18,... | collective-permute-start | bytes 3145736 | tf_op jit(solution)/shard_map/ppermute | solution.py:45
  356.1 34.3 %collective-permute-start.31 = (bf16[4,592,256]{2,1,0:T(8,128)(2,1)}, bf16[4,592,256]{2,1,0:T(8,128)(2,1)}, u32[]{:S(2)}, u32[]{:S(2)}) collective-permute-start(bf16[4,592,256]{2,1,0:T(8,128)(2,1)} %get-tuple-element.261), channel_id=1, source_target_pairs={{0,2},{2,0},{4,6},{6,4},{8,10},{10,8},{12,14},{14,12},{16,18},{18,... | collective-permute-start | bytes 3637256 | tf_op jit(solution)/shard_map/ppermute | solution.py:45
  386.0 33.2 %collective-permute-start.32 = (bf16[4,304,384]{2,1,0:T(8,128)(2,1)}, bf16[4,304,384]{2,1,0:T(8,128)(2,1)}, u32[]{:S(2)}, u32[]{:S(2)}) collective-permute-start(bf16[4,304,384]{2,1,0:T(8,128)(2,1)} %get-tuple-element.264), channel_id=1, source_target_pairs={{0,4},{2,6},{4,0},{6,2},{8,12},{10,14},{12,8},{14,10},{16,20},{18,... | collective-permute-start | bytes 2801672 | tf_op jit(solution)/shard_map/ppermute | solution.py:45
  386.6 32.3 %collective-permute-start.33 = (bf16[4,304,256]{2,1,0:T(8,128)(2,1)}, bf16[4,304,256]{2,1,0:T(8,128)(2,1)}, u32[]{:S(2)}, u32[]{:S(2)}) collective-permute-start(bf16[4,304,256]{2,1,0:T(8,128)(2,1)} %get-tuple-element.266), channel_id=1, source_target_pairs={{0,2},{2,0},{4,6},{6,4},{8,10},{10,8},{12,14},{14,12},{16,18},{18,... | collective-permute-start | bytes 1867784 | tf_op jit(solution)/shard_map/ppermute | solution.py:45
  387.1 31.3 %collective-permute-start.34 = (bf16[4,384,128]{2,1,0:T(8,128)(2,1)}, bf16[4,384,128]{2,1,0:T(8,128)(2,1)}, u32[]{:S(2)}, u32[]{:S(2)}) collective-permute-start(bf16[4,384,128]{2,1,0:T(8,128)(2,1)} %get-tuple-element.268), channel_id=1, source_target_pairs={{0,4},{2,6},{4,0},{6,2},{8,12},{10,14},{12,8},{14,10},{16,20},{18,... | collective-permute-start | bytes 1179656 | tf_op jit(solution)/shard_map/ppermute | solution.py:45
  394.7 41.8 %collective-permute-start.38 = (bf16[2,592,256]{2,1,0:T(8,128)(2,1)}, bf16[2,592,256]{2,1,0:T(8,128)(2,1)}, u32[]{:S(2)}, u32[]{:S(2)}) collective-permute-start(bf16[2,592,256]{2,1,0:T(8,128)(2,1)} %get-tuple-element.276), channel_id=1, source_target_pairs={{0,4},{2,6},{4,0},{6,2},{8,12},{10,14},{12,8},{14,10},{16,20},{18,... | collective-permute-start | bytes 1818632 | tf_op jit(solution)/shard_map/ppermute | solution.py:45
  395.3 38.2 %collective-permute-start.36 = (bf16[2,512,256]{2,1,0:T(8,128)(2,1)}, bf16[2,512,256]{2,1,0:T(8,128)(2,1)}, u32[]{:S(2)}, u32[]{:S(2)}) collective-permute-start(bf16[2,512,256]{2,1,0:T(8,128)(2,1)} %get-tuple-element.272), channel_id=1, source_target_pairs={{0,8},{2,10},{4,12},{6,14},{8,0},{10,2},{12,4},{14,6},{16,24},{18,... | collective-permute-start | bytes 1572872 | tf_op jit(solution)/shard_map/ppermute | solution.py:45
  418.4 18.1 %collective-permute-start.37 = (bf16[2,512,256]{2,1,0:T(8,128)(2,1)}, bf16[2,512,256]{2,1,0:T(8,128)(2,1)}, u32[]{:S(2)}, u32[]{:S(2)}) collective-permute-start(bf16[2,512,256]{2,1,0:T(8,128)(2,1)} %get-tuple-element.274), channel_id=1, source_target_pairs={{0,2},{2,0},{4,6},{6,4},{8,10},{10,8},{12,14},{14,12},{16,18},{18,... | collective-permute-start | bytes 1572872 | tf_op jit(solution)/shard_map/ppermute | solution.py:45
  429.0 12.9 %collective-permute-start.39 = (f32[16,3200]{1,0:T(8,128)}, f32[16,3200]{1,0:T(8,128)}, u32[]{:S(2)}, u32[]{:S(2)}) collective-permute-start(f32[16,3200]{1,0:T(8,128)} %add.5.a_ref), channel_id=1, source_target_pairs={{0,8},{2,10},{4,12},{6,14},{8,0},{10,2},{12,4},{14,6},{16,24},{18,... | collective-permute-start | bytes 614408 | tf_op jit(solution)/shard_map/ppermute | solution.py:45
  433.5 30.5 %collective-permute-start.42 = (bf16[1,112,896]{2,1,0:T(8,128)(2,1)}, bf16[1,112,896]{2,1,0:T(8,128)(2,1)}, u32[]{:S(2)}, u32[]{:S(2)}) collective-permute-start(bf16[1,112,896]{2,1,0:T(8,128)(2,1)} %get-tuple-element.286), channel_id=1, source_target_pairs={{0,16},{2,18},{4,20},{6,22},{8,24},{10,26},{12,28},{14,30},{16,0},... | collective-permute-start | bytes 602120 | tf_op jit(solution)/shard_map/ppermute | solution.py:45
  433.5 31.0 %collective-permute-start.40 = (bf16[1,112,1152]{2,1,0:T(8,128)(2,1)}, bf16[1,112,1152]{2,1,0:T(8,128)(2,1)}, u32[]{:S(2)}, u32[]{:S(2)}) collective-permute-start(bf16[1,112,1152]{2,1,0:T(8,128)(2,1)} %get-tuple-element.282), channel_id=1, source_target_pairs={{0,16},{2,18},{4,20},{6,22},{8,24},{10,26},{12,28},{14,30},{16,0},... | collective-permute-start | bytes 774152 | tf_op jit(solution)/shard_map/ppermute | solution.py:45
  436.4 29.6 %collective-permute-start.41 = (bf16[1,112,1152]{2,1,0:T(8,128)(2,1)}, bf16[1,112,1152]{2,1,0:T(8,128)(2,1)}, u32[]{:S(2)}, u32[]{:S(2)}) collective-permute-start(bf16[1,112,1152]{2,1,0:T(8,128)(2,1)} %get-tuple-element.284), channel_id=1, source_target_pairs={{0,16},{2,18},{4,20},{6,22},{8,24},{10,26},{12,28},{14,30},{16,0},... | collective-permute-start | bytes 774152 | tf_op jit(solution)/shard_map/ppermute | solution.py:45
  439.6 36.6 %collective-permute-start.45 = (bf16[2,304,256]{2,1,0:T(8,128)(2,1)}, bf16[2,304,256]{2,1,0:T(8,128)(2,1)}, u32[]{:S(2)}, u32[]{:S(2)}) collective-permute-start(bf16[2,304,256]{2,1,0:T(8,128)(2,1)} %get-tuple-element.291), channel_id=1, source_target_pairs={{0,8},{2,10},{4,12},{6,14},{8,0},{10,2},{12,4},{14,6},{16,24},{18,... | collective-permute-start | bytes 933896 | tf_op jit(solution)/shard_map/ppermute | solution.py:45
  441.8 37.1 %collective-permute-start.44 = (bf16[2,304,384]{2,1,0:T(8,128)(2,1)}, bf16[2,304,384]{2,1,0:T(8,128)(2,1)}, u32[]{:S(2)}, u32[]{:S(2)}) collective-permute-start(bf16[2,304,384]{2,1,0:T(8,128)(2,1)} %get-tuple-element.289), channel_id=1, source_target_pairs={{0,8},{2,10},{4,12},{6,14},{8,0},{10,2},{12,4},{14,6},{16,24},{18,... | collective-permute-start | bytes 1400840 | tf_op jit(solution)/shard_map/ppermute | solution.py:45
  466.0 31.8 %collective-permute-start.48 = (bf16[1,512,256]{2,1,0:T(8,128)(2,1)}, bf16[1,512,256]{2,1,0:T(8,128)(2,1)}, u32[]{:S(2)}, u32[]{:S(2)}) collective-permute-start(bf16[1,512,256]{2,1,0:T(8,128)(2,1)} %get-tuple-element.299), channel_id=1, source_target_pairs={{0,16},{2,18},{4,20},{6,22},{8,24},{10,26},{12,28},{14,30},{16,0},... | collective-permute-start | bytes 786440 | tf_op jit(solution)/shard_map/ppermute | solution.py:45
  470.1 45.4 %collective-permute-start.50 = (bf16[1,592,256]{2,1,0:T(8,128)(2,1)}, bf16[1,592,256]{2,1,0:T(8,128)(2,1)}, u32[]{:S(2)}, u32[]{:S(2)}) collective-permute-start(bf16[1,592,256]{2,1,0:T(8,128)(2,1)} %get-tuple-element.303), channel_id=1, source_target_pairs={{0,16},{2,18},{4,20},{6,22},{8,24},{10,26},{12,28},{14,30},{16,0},... | collective-permute-start | bytes 909320 | tf_op jit(solution)/shard_map/ppermute | solution.py:45
  474.7 26.6 %collective-permute-start.47 = (f32[16,3200]{1,0:T(8,128)}, f32[16,3200]{1,0:T(8,128)}, u32[]{:S(2)}, u32[]{:S(2)}) collective-permute-start(f32[16,3200]{1,0:T(8,128)} %add.7.a_ref), channel_id=1, source_target_pairs={{0,2},{2,0},{4,6},{6,4},{8,10},{10,8},{12,14},{14,12},{16,18},{18,... | collective-permute-start | bytes 614408 | tf_op jit(solution)/shard_map/ppermute | solution.py:45
  476.2 39.3 %collective-permute-start.49 = (bf16[1,512,256]{2,1,0:T(8,128)(2,1)}, bf16[1,512,256]{2,1,0:T(8,128)(2,1)}, u32[]{:S(2)}, u32[]{:S(2)}) collective-permute-start(bf16[1,512,256]{2,1,0:T(8,128)(2,1)} %get-tuple-element.301), channel_id=1, source_target_pairs={{0,16},{2,18},{4,20},{6,22},{8,24},{10,26},{12,28},{14,30},{16,0},... | collective-permute-start | bytes 786440 | tf_op jit(solution)/shard_map/ppermute | solution.py:45
  481.5 42.6 %collective-permute-start.51 = (bf16[1,304,384]{2,1,0:T(8,128)(2,1)}, bf16[1,304,384]{2,1,0:T(8,128)(2,1)}, u32[]{:S(2)}, u32[]{:S(2)}) collective-permute-start(bf16[1,304,384]{2,1,0:T(8,128)(2,1)} %get-tuple-element.306), channel_id=1, source_target_pairs={{0,16},{2,18},{4,20},{6,22},{8,24},{10,26},{12,28},{14,30},{16,0},... | collective-permute-start | bytes 700424 | tf_op jit(solution)/shard_map/ppermute | solution.py:45
  497.9 26.3 %collective-permute-start.52 = (bf16[1,304,256]{2,1,0:T(8,128)(2,1)}, bf16[1,304,256]{2,1,0:T(8,128)(2,1)}, u32[]{:S(2)}, u32[]{:S(2)}) collective-permute-start(bf16[1,304,256]{2,1,0:T(8,128)(2,1)} %get-tuple-element.308), channel_id=1, source_target_pairs={{0,16},{2,18},{4,20},{6,22},{8,24},{10,26},{12,28},{14,30},{16,0},... | collective-permute-start | bytes 466952 | tf_op jit(solution)/shard_map/ppermute | solution.py:45
  501.3 22.9 %collective-permute-start.53 = (bf16[1,384,128]{2,1,0:T(8,128)(2,1)}, bf16[1,384,128]{2,1,0:T(8,128)(2,1)}, u32[]{:S(2)}, u32[]{:S(2)}) collective-permute-start(bf16[1,384,128]{2,1,0:T(8,128)(2,1)} %get-tuple-element.310), channel_id=1, source_target_pairs={{0,16},{2,18},{4,20},{6,22},{8,24},{10,26},{12,28},{14,30},{16,0},... | collective-permute-start | bytes 294920 | tf_op jit(solution)/shard_map/ppermute | solution.py:45
  (6 other events, 50.6 us)
